TPU v7x, 32 devices: a whole 2x2x4 slice. The times are simulated.
32 devices in a mesh: grp: 2 (over x), dom: 16 (over z, y, core).
Axes of the slice: x: 2, y: 2, z: 4, core: 2. Of those that a mesh axis runs over, the one named last changes fastest.
Arguments:
- positions: float32 [512, 3, 128], P(('grp', 'dom')), may hold values from 0 to 1
- smoothing: float32 [512, 128], P(('grp', 'dom')), may hold values from 0.35 to 0.55
- energy: float32 [512, 128], P(('grp', 'dom')), may hold values from 0.5 to 2
- mass: float32 [512, 128], P(('grp', 'dom')), may hold values from 0.00390625 to 0.015625
- old_density: float32 [512, 128], P(('grp', 'dom')), may hold values from 1 to 6
- active: int32 [512, 128], P(('grp', 'dom')), may hold values 0 or 1
- pair_list: int32 [512, 2], P(('grp', 'dom')), may hold values from 0 to 15
- export_leaves: int32 [768, 2], P(('grp', 'dom')), may hold values from 0 to 15
- export_route: int32 [768, 1], P(('grp', 'dom')), may hold values from 0 to 14; in each aligned block of 24 rows (0 to 23, 24 to 47, ...) at most 2 rows name the same one
Outputs:
- density: float32 [512, 128], P(('grp', 'dom'))
- acceleration: float32 [512, 3, 128], P(('grp', 'dom'))
- timestep: float32 [], replicated
Inputs may be any that keep to these rules, and one draw needn't show every extreme that they name: `pair_list`: indices of leaf blocks of the domain that holds the row. `export_leaves`: column 0 is a leaf block of the domain that holds the row, column 1 a leaf block of the destination domain. `export_route`: among the rows of one domain no value occurs more than 2 times; in some domains one value occurs exactly 2 times. `active`: every domain holds some particles with value 1.
All inputs are finite; a program needn't handle non-finite values. No bound on the sum of `active` on one device may be relied on, other than what follows from the above.
Results may differ from a plain program's by a relative error of at most 0.0003.
Values sent between devices are 32-bit elements; how exact they have to be, the bound alone decides.
No kernel may reach another device: no remote copies, remote signals or barrier semaphores. Data moves between devices by JAX's collectives and lax.ppermute only.
A program may use at most 64 MiB of HBM per device.

v0:
```python
import math

import jax
import jax.numpy as jnp
from jax import lax
from jax.sharding import PartitionSpec as P

MOST = 2


ADIABATIC = 5.0 / 3.0
COURANT = 0.3
batch_tiles = 8


def kernel_value(dist, smooth):
    ratio = dist / smooth
    inner = 1.0 - 6.0 * ratio * ratio + 6.0 * ratio * ratio * ratio
    remain = jnp.maximum(1.0 - ratio, 0.0)
    outer = 2.0 * remain * remain * remain
    return jnp.where(ratio < 0.5, inner, outer) * (8.0 / math.pi) / (smooth * smooth * smooth)


def kernel_slope(dist, smooth):
    ratio = dist / smooth
    inner = -12.0 + 18.0 * ratio
    remain = jnp.maximum(1.0 - ratio, 0.0)
    outer = -6.0 * remain * remain / jnp.maximum(ratio, 0.5)
    square = smooth * smooth
    return jnp.where(ratio < 0.5, inner, outer) * (8.0 / math.pi) / (square * square * smooth)


def density_tile(own_pos, own_h, far_pos, far_mass):
    offset = own_pos[:, :, None] - far_pos[:, None, :]
    dist = jnp.sqrt(jnp.sum(offset * offset, axis=0))
    return jnp.sum(kernel_value(dist, own_h[:, None]) * far_mass[None, :], axis=1)


def force_tile(own_pos, own_h, own_term, far_pos, far_h, far_mass, far_term):
    offset = own_pos[:, :, None] - far_pos[:, None, :]
    dist = jnp.sqrt(jnp.sum(offset * offset, axis=0))
    slope = 0.5 * (kernel_slope(dist, own_h[:, None]) + kernel_slope(dist, far_h[None, :]))
    weight = far_mass[None, :] * (own_term[:, None] + far_term[None, :]) * slope
    return -jnp.sum(weight[None, :, :] * offset, axis=2)


def blockwise(kernel, operands):
    count = operands[0].shape[0]
    width = min(batch_tiles, count)
    shaped = tuple((item.reshape((count // width, width) + item.shape[1:]) for item in operands))
    result = lax.map(lambda group: jax.vmap(kernel)(*group), shaped)
    return result.reshape((count,) + result.shape[2:])


def collect(owner, values):
    flat = values.reshape(values.shape[0], -1)
    total = jnp.dot(
        owner, flat, precision=lax.Precision.HIGHEST, preferred_element_type=jnp.float32
    )
    return total.reshape((owner.shape[0],) + values.shape[1:])


def body(
    positions, smoothing, energy, mass, old_density, active, pair_list, export_leaves, export_route
):
    leaves = positions.shape[0]
    width = positions.shape[2]
    exported = export_leaves.shape[0]
    domains = lax.axis_size("dom")
    myself = lax.axis_index("dom")
    slots = domains * MOST
    target_dom = (myself + 1 + export_route[:, 0]) % domains
    columns = jnp.arange(domains, dtype=jnp.int32)
    onehot = (target_dom[:, None] == columns[None, :]).astype(jnp.int32)
    earlier = jnp.cumsum(onehot, axis=0) - onehot
    rank_in = jnp.sum(earlier * onehot, axis=1)
    slot_of = target_dom * MOST + rank_in
    match = (slot_of[None, :] == jnp.arange(slots, dtype=jnp.int32)[:, None]).astype(jnp.int32)
    filled = jnp.sum(match, axis=1) > 0
    chosen = jnp.sum(match * jnp.arange(exported, dtype=jnp.int32)[None, :], axis=1)
    send_leaf = export_leaves[chosen, 0]
    send_target = jnp.where(filled, export_leaves[chosen, 1], 0)
    leaf_ids = jnp.arange(leaves, dtype=jnp.int32)
    slot_owner = ((send_leaf[None, :] == leaf_ids[:, None]) & filled[None, :]).astype(jnp.float32)
    pair_owner = (pair_list[None, :, 0] == leaf_ids[:, None]).astype(jnp.float32)
    own_idx = pair_list[:, 0]
    far_idx = pair_list[:, 1]
    send_pos = positions[send_leaf]
    send_h = smoothing[send_leaf]
    wanted = lax.all_to_all(
        send_target.reshape(domains, MOST), "dom", split_axis=0, concat_axis=0, tiled=True
    )
    wanted = wanted.reshape(slots)
    served = jnp.concatenate(
        [positions[wanted], smoothing[wanted][:, None, :], mass[wanted][:, None, :]], axis=1
    )
    fetched = lax.all_to_all(
        served.reshape(domains, MOST, 5, width), "dom", split_axis=0, concat_axis=0, tiled=True
    )
    fetched = fetched.reshape(slots, 5, width)
    remote_density = collect(
        slot_owner, blockwise(density_tile, (send_pos, send_h, fetched[:, 0:3], fetched[:, 4]))
    )
    local_part = blockwise(
        density_tile, (positions[own_idx], smoothing[own_idx], positions[far_idx], mass[far_idx])
    )
    self_term = mass * kernel_value(jnp.zeros_like(smoothing), smoothing)
    summed = collect(pair_owner, local_part) + remote_density
    density = jnp.where(active == 1, self_term + summed, old_density)
    term = (ADIABATIC - 1.0) * energy / density
    far_term = lax.all_to_all(
        term[wanted].reshape(domains, MOST, width), "dom", split_axis=0, concat_axis=0, tiled=True
    )
    far_term = far_term.reshape(slots, width)
    remote_force = blockwise(
        force_tile,
        (
            send_pos,
            send_h,
            term[send_leaf],
            fetched[:, 0:3],
            fetched[:, 3],
            fetched[:, 4],
            far_term,
        ),
    )
    remote_accel = collect(slot_owner, remote_force)
    local_force = blockwise(
        force_tile,
        (
            positions[own_idx],
            smoothing[own_idx],
            term[own_idx],
            positions[far_idx],
            smoothing[far_idx],
            mass[far_idx],
            term[far_idx],
        ),
    )
    accel = collect(pair_owner, local_force) + remote_accel
    acceleration = jnp.where((active == 1)[:, None, :], accel, 0.0)
    speed = jnp.sqrt(ADIABATIC * (ADIABATIC - 1.0) * energy)
    magnitude = jnp.sqrt(jnp.sum(acceleration * acceleration, axis=1))
    step_size = COURANT * smoothing / (speed + jnp.sqrt(smoothing * magnitude))
    local_least = jnp.min(jnp.where(active == 1, step_size, jnp.inf))
    timestep = lax.pmin(local_least, ("grp", "dom"))
    return (density, acceleration, timestep)


def solution(mesh):
    return jax.shard_map(
        body,
        mesh=mesh,
        in_specs=(
            P(("grp", "dom"), None, None),
            P(("grp", "dom"), None),
            P(("grp", "dom"), None),
            P(("grp", "dom"), None),
            P(("grp", "dom"), None),
            P(("grp", "dom"), None),
            P(("grp", "dom"), None),
            P(("grp", "dom"), None),
            P(("grp", "dom"), None),
        ),
        out_specs=(P(("grp", "dom"), None), P(("grp", "dom"), None, None), P()),
        check_vma=False,
    )
```

profile of v0, /device:TPU:0, one launch (start us, length us, event | category | flops | bytes accessed | tf_op | source)
XLA Modules:
  0.0 107.7 jit_solution(8637589466511635926)
XLA Ops:
  0.7 0.7 fusion.71
  1.7 0.7 fusion.70
  2.4 1.4 %gather_fusion.6 = s32[32]{0:T(128)S(1)} fusion(s32[24,2]{0,1:T(2,128)} %param.24, s32[32]{0:T(128)S(1)} %get-tuple-element.380), kind=kCustom, calls=%fused_computation.6 | custom fusion | bytes 512 | tf_op jit(solution)/shard_map/gather | solution.py:82
  3.9 0.7 select_n.140
  4.6 7.4 %all-to-all-start = ((s32[16,1,2]{2,1,0:T(1,128)}), s32[16,1,2]{2,1,0:T(1,128)S(1)}, u32[]{:S(2)}, u32[]{:S(2)}) async-start(s32[16,1,2]{2,1,0:T(1,128)} %bitcast.42), calls=%async_computation | async-start | bytes 16384 | tf_op jit(solution)/shard_map/all_to_all | solution.py:90
  13.2 0.8 gather_fusion.4
  17.0 2.3 %while.40 = (s32[]{:T(128)}, f32[2,8,128]{2,1,0:T(8,128)S(1)}, f32[2,8,3,128]{3,2,1,0:T(4,128)S(1)}, f32[2,8,3,128]{3,2,1,0:T(4,128)S(1)}, f32[2,8,128]{2,1,0:T(8,128)S(1)}, /*index=5*/f32[2,8,128]{2,1,0:T(8,128)S(1)}, s32[]{:T(128)}) while((s32[]{:T(128)}, f32[2,8,128]{2,1,0:T(8,128)S(1)}, f32[2,8,3,128]{3,2,1,0:T(4,128)S(1)}, ...), condition=%wide.region_3.4_spmd, body=%wide.region_0.0_spmd.sunk | while | flops 3277826 | bytes 1167461 | solution.py:51
  20.0 0.7 reduce.3
  22.6 0.7 pad_maximum_fusion
  23.2 6.0 %all-to-all-start.1 = ((f32[16,2,5,128]{3,1,2,0:T(2,128)}), f32[16,2,5,128]{3,1,2,0:T(2,128)S(1)}, u32[]{:S(2)}, u32[]{:S(2)}) async-start(f32[16,2,5,128]{3,1,2,0:T(2,128)} %pad_maximum_fusion), calls=%async_computation.1 | async-start | bytes 163840 | tf_op jit(solution)/shard_map/all_to_all | solution.py:97
  29.3 7.1 %all-to-all-done.1 = f32[16,2,5,128]{3,1,2,0:T(2,128)S(1)} async-done(((f32[16,2,5,128]{3,1,2,0:T(2,128)}), f32[16,2,5,128]{3,1,2,0:T(2,128)S(1)}, u32[]{:S(2)}, u32[]{:S(2)}) %all-to-all-start.1) | async-done | bytes 81952 | tf_op jit(solution)/shard_map/all_to_all | solution.py:97
  36.5 4.6 %while.41 = (s32[]{:T(128)}, f32[4,8,128]{2,1,0:T(8,128)S(1)}, f32[4,8,3,128]{3,2,1,0:T(4,128)S(1)}, f32[4,8,3,128]{3,2,1,0:T(4,128)S(1)}, f32[4,8,128]{2,1,0:T(8,128)S(1)}, /*index=5*/f32[4,8,128]{2,1,0:T(8,128)S(1)}, s32[]{:T(128)}) while((s32[]{:T(128)}, f32[4,8,128]{2,1,0:T(8,128)S(1)}, f32[4,8,3,128]{3,2,1,0:T(4,128)S(1)}, ...), condition=%wide.region_11.12_spmd, body=%wide.region_8.11_spmd.sunk | while | flops 3277826 | bytes 1167461 | solution.py:51
  41.1 0.7 multiply_divide_fusion
  42.9 1.2 %gather_fusion.15 = f32[32,128]{1,0:T(8,128)} fusion(f32[16,128]{1,0:T(8,128)S(1)} %get-tuple-element.382, s32[1024]{0:T(1024)S(1)} %pad_clamp_fusion), kind=kCustom, calls=%fused_computation.15 | custom fusion | bytes 32896 | tf_op jit(solution)/shard_map/gather | solution.py:112
  44.1 4.6 %while.42 = (s32[]{:T(128)}, f32[2,8,3,128]{3,2,1,0:T(4,128)S(1)}, f32[2,8,128]{2,1,0:T(8,128)S(1)}, f32[2,8,128]{2,1,0:T(8,128)S(1)}, f32[2,8,128]{2,1,0:T(8,12...) while((s32[]{:T(128)}, f32[2,8,3,128]{3,2,1,0:T(4,128)S(1)}, ...), condition=%wide.region_15.16_spmd, body=%wide.region_12.15_spmd.sunk | while | flops 6297602 | bytes 2318465 | solution.py:51
  44.7 0.8 multiply_multiply_fusion.28
  45.4 1.0 fusion.91
  47.0 0.8 multiply_multiply_fusion.28
  47.8 1.0 fusion.91
  48.7 3.5 %all-to-all-start.2 = ((f32[16,2,128]{2,1,0:T(2,128)}), f32[16,2,128]{2,1,0:T(2,128)S(1)}, u32[]{:S(2)}, u32[]{:S(2)}) async-start(f32[16,2,128]{2,1,0:T(2,128)} %bitcast.61), calls=%async_computation.2 | async-start | bytes 32768 | tf_op jit(solution)/shard_map/all_to_all | solution.py:111
  53.0 5.8 %all-to-all-done.2 = f32[16,2,128]{2,1,0:T(2,128)S(1)} async-done(((f32[16,2,128]{2,1,0:T(2,128)}), f32[16,2,128]{2,1,0:T(2,128)S(1)}, u32[]{:S(2)}, u32[]{:S(2)}) %all-to-all-start.2) | async-done | bytes 16416 | tf_op jit(solution)/shard_map/all_to_all | solution.py:111
  58.7 9.3 %while.43 = (s32[]{:T(128)}, f32[4,8,3,128]{3,2,1,0:T(4,128)S(1)}, f32[4,8,128]{2,1,0:T(8,128)S(1)}, f32[4,8,128]{2,1,0:T(8,128)S(1)}, f32[4,8,128]{2,1,0:T(8,12...) while((s32[]{:T(128)}, f32[4,8,3,128]{3,2,1,0:T(4,128)S(1)}, ...), condition=%wide.region_19.20_spmd, body=%wide.region_16.19_spmd.sunk | while | flops 6297602 | bytes 2318465 | solution.py:51
  59.3 0.8 multiply_multiply_fusion.30
  60.1 1.0 fusion.93
  61.6 0.8 multiply_multiply_fusion.30
  62.4 1.0 fusion.93
  63.9 0.8 multiply_multiply_fusion.30
  64.7 1.0 fusion.93
  66.3 0.8 multiply_multiply_fusion.30
  67.0 1.0 fusion.93
  68.0 0.8 multiply_reduce_fusion.2
  69.4 38.3 %pmin.7 = f32[]{:T(128)} all-reduce(f32[]{:T(128)} %select_reduce_fusion.2), channel_id=1, replica_groups=mesh['grp'=2,'dom'=16] {'grp','dom'}, use_global_device_ids=true, to_apply=%region_22.23 | all-reduce | flops 1 | bytes 8 | tf_op jit(solution)/shard_map/pmin | solution.py:146
  (132 shorter events, 19.4 us)
Async XLA Ops:
  0.6 11.4 %copy-start = (f32[16,3,128]{2,0,1:T(8,128)S(1)}, f32[16,3,128]{2,0,1:T(8,128)}, u32[]{:S(2)}) copy-start(f32[16,3,128]{2,0,1:T(8,128)} %param.17) | copy-start | bytes 73732
  0.6 12.6 %copy-start.1 = (s32[24,2]{0,1:T(2,128)S(1)}, s32[24,2]{0,1:T(2,128)}, u32[]{:S(2)}) copy-start(s32[24,2]{0,1:T(2,128)} %param.24) | copy-start | bytes 580
  0.7 11.4 %copy-start.6 = (s32[16,2]{0,1:T(2,128)S(1)}, s32[16,2]{0,1:T(2,128)}, u32[]{:S(2)}) copy-start(s32[16,2]{0,1:T(2,128)} %param.23) | copy-start | bytes 388
  0.7 12.0 %copy-start.2 = (f32[16,128]{1,0:T(8,128)S(1)}, f32[16,128]{1,0:T(8,128)}, u32[]{:S(2)}) copy-start(f32[16,128]{1,0:T(8,128)} %param.18) | copy-start | bytes 24580
  4.6 14.9 %all-to-all-start = ((s32[16,1,2]{2,1,0:T(1,128)}), s32[16,1,2]{2,1,0:T(1,128)S(1)}, u32[]{:S(2)}, u32[]{:S(2)}) async-start(s32[16,1,2]{2,1,0:T(1,128)} %bitcast.42), calls=%async_computation | async-start | bytes 16384 | tf_op jit(solution)/shard_map/all_to_all | solution.py:90
  14.0 2.4 %copy-start.4 = (s32[16,128]{1,0:T(8,128)S(1)}, s32[16,128]{1,0:T(8,128)}, u32[]{:S(2)}) copy-start(s32[16,128]{1,0:T(8,128)} %param.22) | copy-start | bytes 24580
  14.0 2.4 %copy-start.3 = (f32[16,128]{1,0:T(8,128)S(1)}, f32[16,128]{1,0:T(8,128)}, u32[]{:S(2)}) copy-start(f32[16,128]{1,0:T(8,128)} %param.20) | copy-start | bytes 24580
  23.2 13.1 %all-to-all-start.1 = ((f32[16,2,5,128]{3,1,2,0:T(2,128)}), f32[16,2,5,128]{3,1,2,0:T(2,128)S(1)}, u32[]{:S(2)}, u32[]{:S(2)}) async-start(f32[16,2,5,128]{3,1,2,0:T(2,128)} %pad_maximum_fusion), calls=%async_computation.1 | async-start | bytes 163840 | tf_op jit(solution)/shard_map/all_to_all | solution.py:97
  36.5 4.6 %copy-start.5 = (f32[16,128]{1,0:T(8,128)S(1)}, f32[16,128]{1,0:T(8,128)}, u32[]{:S(2)}) copy-start(f32[16,128]{1,0:T(8,128)} %param.19) | copy-start | bytes 24580
  36.5 4.6 %copy-start.7 = (f32[16,128]{1,0:T(8,128)S(1)}, f32[16,128]{1,0:T(8,128)}, u32[]{:S(2)}) copy-start(f32[16,128]{1,0:T(8,128)} %param.21) | copy-start | bytes 24580
  48.7 10.0 %all-to-all-start.2 = ((f32[16,2,128]{2,1,0:T(2,128)}), f32[16,2,128]{2,1,0:T(2,128)S(1)}, u32[]{:S(2)}, u32[]{:S(2)}) async-start(f32[16,2,128]{2,1,0:T(2,128)} %bitcast.61), calls=%async_computation.2 | async-start | bytes 32768 | tf_op jit(solution)/shard_map/all_to_all | solution.py:111
where the time goes:
time: 108 us
  blocking collectives  38.3 us (35%)
  other arithmetic  23.5 us (22%)
  starting transfers between devices  16.9 us (16%)
  waiting for transfers between devices  12.9 us (12%)
  local copies, waits for them, and re-layouts  12.7 us (12%)
  matrix products  1.74 us (2%)
    pmin x1, blocking collectives, body(): timestep = lax.pmin(local_least, ('grp', 'dom'))  38.3 us
    all_to_all x1, starting transfers between devices, body(): lax.all_to_all(send_target.reshape(domains, MOST), 'dom', split_axis=0, c...  7.41 us
    all_to_all x1, waiting for transfers between devices, body(): lax.all_to_all(served.reshape(domains, MOST, 5, width), 'dom', split_axis...  7.1 us
    all_to_all x1, starting transfers between devices, body(): lax.all_to_all(served.reshape(domains, MOST, 5, width), 'dom', split_axis...  6 us
    all_to_all x1, waiting for transfers between devices, body(): lax.all_to_all(term[wanted].reshape(domains, MOST, width), 'dom', split_a...  5.75 us
    reduce_sum x6, other arithmetic, force_tile(): return -jnp.sum(weight[None, :, :] * offset, axis=2)  5.74 us
    mul x6, other arithmetic, force_tile(): weight = far_mass[None, :] * (own_term[:, None] + far_term[None, :]) * slope  4.61 us
    all_to_all x1, starting transfers between devices, body(): lax.all_to_all(term[wanted].reshape(domains, MOST, width), 'dom', split_a...  3.51 us
  transfers between devices with their start and end apart: 3, of which 2 were waited for; matrix products, arithmetic and copies ran while one was open for 7% of the time, Pallas kernels for 0%

commit v1 on v0

v1 whole, which is shorter than its diff:
```python
import math

import jax
import jax.numpy as jnp
from jax import lax
from jax.experimental import pallas as pl
from jax.experimental.pallas import tpu as pltpu
from jax.sharding import Mesh, PartitionSpec as P

ADIABATIC = 5.0 / 3.0
COURANT = 0.3
GROUP = 4
ROWS = 5
TINY = 1e-30
NORM = 8.0 / math.pi


def wide(ref, at, count):
    return ref[pl.ds(at, count), :]


def spread(out_ref, item, rows, leaves):
    width = rows.shape[1]
    turned = rows.T
    for leaf in range(leaves):
        out_ref[item, leaf] = jnp.broadcast_to(turned[:, leaf : leaf + 1], (width, width))


def separation(own_ref, own, far):
    dx = own_ref[0, own] - far[0]
    dy = own_ref[1, own] - far[1]
    dz = own_ref[2, own] - far[2]
    square = jnp.maximum(dx * dx + dy * dy + dz * dz, TINY)
    inverse = lax.rsqrt(square)
    return dx, dy, dz, square * inverse, inverse


def density_tile(own_ref, own, far):
    _, _, _, dist, _ = separation(own_ref, own, far)
    ratio = dist * own_ref[3, own]
    left = 1.0 - ratio
    inner = 1.0 - 6.0 * (ratio * ratio * left)
    remain = jnp.maximum(left, 0.0)
    outer = 2.0 * (remain * remain * remain)
    value = jnp.where(ratio < 0.5, inner, outer)
    return (jnp.sum(value * far[4], axis=1, keepdims=True),)


def slope(dist, inverse, smooth_inverse, smooth):
    ratio = dist * smooth_inverse
    remain = jnp.maximum(1.0 - ratio, 0.0)
    return jnp.where(ratio < 0.5, 3.0 * ratio - 2.0, -(remain * remain) * (smooth * inverse))


def force_tile(own_ref, own, far):
    dx, dy, dz, dist, inverse = separation(own_ref, own, far)
    mine = slope(dist, inverse, own_ref[3, own], own_ref[4, own]) * own_ref[5, own]
    theirs = slope(dist, inverse, far[5], far[3]) * far[6]
    weight = (mine + theirs) * (far[4] * (own_ref[6, own] + far[7]))
    return tuple(jnp.sum(weight * item, axis=1, keepdims=True) for item in (dx, dy, dz))


def tiles(count, entry, tile, acc_refs, own_ref, leaves):
    span = acc_refs[0].shape[1]
    for ref in acc_refs:
        ref[...] = jnp.zeros_like(ref)
    width = acc_refs[0].shape[0]
    lane = lax.broadcasted_iota(jnp.int32, (width, span), 1)
    short = lax.broadcasted_iota(jnp.int32, (1, span), 1)
    step = math.gcd(GROUP, count)

    def body(group, owners):
        for k in range(step):
            e = group * step + k
            own, far = entry(e)
            for ref, column in zip(acc_refs, tile(own_ref, own, far)):
                ref[...] = jnp.where(lane == e, column, ref[...])
            owners = jnp.where(short == e, own, owners)
        return owners

    owners = lax.fori_loop(0, count // step, body, jnp.full((1, span), -1, jnp.int32))
    leaf = lax.broadcasted_iota(jnp.int32, (leaves, span), 0)
    onehot = (leaf == owners).astype(jnp.float32)
    return [
        lax.dot_general(
            onehot,
            ref[...],
            (((1,), (1,)), ((), ())),
            precision=lax.Precision.HIGHEST,
            preferred_element_type=jnp.float32,
        )
        for ref in acc_refs
    ]


def local_entry(pair_ref, own_rows, leaves):
    def entry(e):
        own = pair_ref[e, 0]
        far = pair_ref[e, 1]
        return own, [wide(own_rows, c * leaves + far, 1) for c in range(own_rows.shape[0] // leaves)]

    return entry


def remote_entry(me_ref, leaf_ref, route_ref, near_ref, peer_ref, leaves, domains):
    me = me_ref[0]

    def entry(e):
        own = leaf_ref[e, 0]
        far = leaf_ref[e, 1]
        target = me + 1 + route_ref[e, 0]
        target = jnp.where(target >= domains, target - domains, target)
        chip = target // 2
        same = (target % 2) == (me % 2)
        rows = [
            jnp.where(
                same,
                near_ref[chip, pl.ds(c * leaves + far, 1), :],
                peer_ref[chip, pl.ds(c * leaves + far, 1), :],
            )
            for c in range(ROWS)
        ]
        return own, target, far, rows

    return entry


def slope_scale(h):
    square = h * h
    return (0.5 * NORM * 6.0) / (square * square * h)


def own_columns(out_ref, rows_ref, leaves, term=None):
    for c in range(3):
        spread(out_ref, c, rows_ref[pl.ds(c * leaves, leaves), :], leaves)
    h = rows_ref[pl.ds(3 * leaves, leaves), :]
    spread(out_ref, 3, 1.0 / h, leaves)
    if term is not None:
        spread(out_ref, 4, h, leaves)
        spread(out_ref, 5, slope_scale(h), leaves)
        spread(out_ref, 6, term, leaves)


def solution(mesh):
    groups, domains = mesh.shape["grp"], mesh.shape["dom"]
    chips = domains // 2
    fine = Mesh(mesh.devices.reshape(groups, chips, 2), ("grp", "chip", "core"))
    everyone = ("grp", "chip", "core")
    vmem = pl.BlockSpec(memory_space=pltpu.VMEM)
    smem = pl.BlockSpec(memory_space=pltpu.SMEM)

    def body(
        positions, smoothing, energy, mass, old_density, active, pair_list, export_leaves, export_route
    ):
        leaves, _, width = positions.shape
        pairs, exports = pair_list.shape[0], export_leaves.shape[0]
        local_span = -(-pairs // 128) * 128
        remote_span = -(-exports // 128) * 128
        f32 = jnp.float32
        sheet = jax.ShapeDtypeStruct((leaves, width), f32)
        me = (lax.axis_index("chip") * 2 + lax.axis_index("core")).astype(jnp.int32).reshape(1)
        own = jnp.concatenate(
            [positions.transpose(1, 0, 2).reshape(3 * leaves, width), smoothing, mass], axis=0
        )
        outgoing = jnp.broadcast_to(own[None], (chips,) + own.shape)
        near = lax.all_to_all(outgoing, "chip", split_axis=0, concat_axis=0, tiled=True)
        peer = lax.ppermute(near, "core", [(0, 1), (1, 0)])

        def local_density(pair_ref, own_ref, out_ref, cols, acc):
            own_columns(cols, own_ref, leaves)
            (total,) = tiles(
                pairs, local_entry(pair_ref, own_ref, leaves), density_tile, [acc], cols, leaves
            )
            out_ref[...] = total

        local_sum = pl.pallas_call(
            local_density,
            out_shape=sheet,
            in_specs=[smem, vmem],
            out_specs=vmem,
            scratch_shapes=[
                pltpu.VMEM((4, leaves, width, width), f32),
                pltpu.VMEM((width, local_span), f32),
            ],
            cost_estimate=pl.CostEstimate(
                flops=pairs * width * width * 30, bytes_accessed=65536, transcendentals=0
            ),
            name="local_density",
        )(pair_list, own)

        def remote_density(
            me_ref, leaf_ref, route_ref, own_ref, near_ref, peer_ref, local_ref, energy_ref,
            old_ref, active_ref, density_ref, term_ref, cols, acc
        ):
            own_columns(cols, own_ref, leaves)
            entry = remote_entry(me_ref, leaf_ref, route_ref, near_ref, peer_ref, leaves, domains)

            def pick(e):
                mine, _, _, rows = entry(e)
                return mine, rows

            (total,) = tiles(exports, pick, density_tile, [acc], cols, leaves)
            h = own_ref[pl.ds(3 * leaves, leaves), :]
            scale = NORM / (h * h * h)
            summed = (local_ref[...] + total + own_ref[pl.ds(4 * leaves, leaves), :]) * scale
            density = jnp.where(active_ref[...] == 1, summed, old_ref[...])
            density_ref[...] = density
            term_ref[...] = (ADIABATIC - 1.0) * energy_ref[...] / density

        density, term = pl.pallas_call(
            remote_density,
            out_shape=(sheet, sheet),
            in_specs=[smem, smem, smem] + [vmem] * 7,
            out_specs=(vmem, vmem),
            scratch_shapes=[
                pltpu.VMEM((4, leaves, width, width), f32),
                pltpu.VMEM((width, remote_span), f32),
            ],
            cost_estimate=pl.CostEstimate(
                flops=exports * width * width * 30, bytes_accessed=65536, transcendentals=0
            ),
            name="remote_density",
        )(me, export_leaves, export_route, own, near, peer, local_sum, energy, old_density, active)

        terms = lax.all_to_all(
            jnp.broadcast_to(term[None], (domains,) + term.shape),
            ("chip", "core"),
            split_axis=0,
            concat_axis=0,
            tiled=True,
        )

        def local_force(pair_ref, own_ref, term_ref, out_ref, cols, ax, ay, az):
            own_columns(cols, own_ref, leaves, term_ref[...])
            h = own_ref[pl.ds(3 * leaves, leaves), :]
            out_ref[0] = 1.0 / h
            out_ref[1] = slope_scale(h)

            def entry(e):
                mine = pair_ref[e, 0]
                far = pair_ref[e, 1]
                rows = [wide(own_ref, c * leaves + far, 1) for c in range(ROWS)]
                rows += [out_ref[c, pl.ds(far, 1), :] for c in range(2)]
                rows.append(wide(term_ref, far, 1))
                return mine, rows

            totals = tiles(pairs, entry, force_tile, [ax, ay, az], cols, leaves)
            for c in range(3):
                out_ref[c] = totals[c]

        local_accel = pl.pallas_call(
            local_force,
            out_shape=jax.ShapeDtypeStruct((3, leaves, width), f32),
            in_specs=[smem, vmem, vmem],
            out_specs=vmem,
            scratch_shapes=[pltpu.VMEM((7, leaves, width, width), f32)]
            + [pltpu.VMEM((width, local_span), f32)] * 3,
            cost_estimate=pl.CostEstimate(
                flops=pairs * width * width * 60, bytes_accessed=65536, transcendentals=0
            ),
            name="local_force",
        )(pair_list, own, term)

        members = groups * domains

        def remote_force(
            me_ref, leaf_ref, route_ref, own_ref, near_ref, peer_ref, term_ref, terms_ref,
            local_ref, energy_ref, active_ref, accel_ref, least_ref, cols, ax, ay, az
        ):
            own_columns(cols, own_ref, leaves, term_ref[...])
            entry = remote_entry(me_ref, leaf_ref, route_ref, near_ref, peer_ref, leaves, domains)

            def pick(e):
                mine, target, far, rows = entry(e)
                h = rows[3]
                rows = rows + [1.0 / h, slope_scale(h), terms_ref[target, pl.ds(far, 1), :]]
                return mine, rows

            totals = tiles(exports, pick, force_tile, [ax, ay, az], cols, leaves)
            awake = active_ref[...] == 1
            square = jnp.zeros((leaves, width), f32)
            for c in range(3):
                part = jnp.where(awake, -(local_ref[c] + totals[c]), 0.0)
                accel_ref[c] = part
                square = square + part * part
            h = own_ref[pl.ds(3 * leaves, leaves), :]
            speed = jnp.sqrt(ADIABATIC * (ADIABATIC - 1.0) * energy_ref[...])
            step = COURANT * h / (speed + jnp.sqrt(h * jnp.sqrt(square)))
            least_ref[...] = jnp.full(
                (members, width), jnp.min(jnp.where(awake, step, jnp.inf)), f32
            )

        accel, least = pl.pallas_call(
            remote_force,
            out_shape=(
                jax.ShapeDtypeStruct((3, leaves, width), f32),
                jax.ShapeDtypeStruct((members, width), f32),
            ),
            in_specs=[smem, smem, smem] + [vmem] * 8,
            out_specs=(vmem, vmem),
            scratch_shapes=[pltpu.VMEM((7, leaves, width, width), f32)]
            + [pltpu.VMEM((width, remote_span), f32)] * 3,
            cost_estimate=pl.CostEstimate(
                flops=exports * width * width * 60, bytes_accessed=65536, transcendentals=0
            ),
            name="remote_force",
        )(me, export_leaves, export_route, own, near, peer, term, terms, local_accel, energy, active)

        everywhere = lax.all_to_all(least, everyone, split_axis=0, concat_axis=0, tiled=True)
        return density, accel.transpose(1, 0, 2), jnp.min(everywhere)

    flat = P(everyone, None)
    deep = P(everyone, None, None)
    return jax.shard_map(
        body,
        mesh=fine,
        in_specs=(deep,) + (flat,) * 8,
        out_specs=(flat, deep, P()),
        check_vma=False,
    )
```

time: 108 us -> 66.4 us (0.61)
  Pallas kernels: 0 us -> 23.1 us
  other arithmetic: 23.5 us -> 1.41 us
  starting transfers between devices: 16.9 us -> 3.51 us
  waiting for transfers between devices: 12.9 us -> 1.79 us
  blocking collectives: 38.3 us -> 29.3 us
  local copies, waits for them, and re-layouts: 12.7 us -> 6.05 us
  matrix products: 1.74 us -> 0 us
    pmin x1 -> x0, blocking collectives: 38.3 us -> none  [body(): timestep = lax.pmin(local_least, ('grp', 'dom'))]
    all_to_all x0 -> x2, blocking collectives: none -> 29.3 us  [the longest x1 18 us: body(): lax.all_to_all(outgoing, 'chip', split_axis=0, concat_axis=0, tiled=True)]
    pallas_call x0 -> x4, Pallas kernels: none -> 23.1 us  [the longest x1 7.74 us: body(): pl.pallas_call(remote_force, out_shape=(jax.ShapeDtypeStruct((3, leaves,...]
    reduce_sum x26 -> x0, other arithmetic: 15.1 us -> none  [the longest x6 5.74 us: force_tile(): return -jnp.sum(weight[None, :, :] * offset, axis=2)]
    all_to_all x3 -> x1, starting transfers between devices: 16.9 us -> 3.51 us  [body(): lax.all_to_all(jnp.broadcast_to(term[None], (domains,) + term.shape), ('c...]
    all_to_all x3 -> x1, waiting for transfers between devices: 12.9 us -> 1.78 us  [body(): lax.all_to_all(jnp.broadcast_to(term[None], (domains,) + term.shape), ('c...]
    gather x16 -> x0, local copies, waits for them, and re-layouts: 10.9 us -> none  [the longest x1 1.43 us: body(): send_target = jnp.where(filled, export_leaves[chosen, 1], 0)]
    mul x18 -> x0, other arithmetic: 4.78 us -> none  [the longest x6 4.61 us: force_tile(): weight = far_mass[None, :] * (own_term[:, None] + far_term[None, :]) * slope]
  transfers between devices with their start and end apart: 3 -> 2, of which waited for: 2 -> 1; matrix products, arithmetic and copies ran while one was open for 7% -> 3% of each run, Pallas kernels for 0% -> 15%
where the time goes in v1:
time: 66.4 us; the launch traced here: 65.8 us
  blocking collectives  29.3 us (44%)
  Pallas kernels  23.1 us (35%)
  local copies, waits for them, and re-layouts  6.05 us (9%)
  starting transfers between devices  3.51 us (5%)
  waiting for transfers between devices  1.79 us (3%)
  other arithmetic  1.41 us (2%)
    all_to_all x1, blocking collectives, body(): lax.all_to_all(outgoing, 'chip', split_axis=0, concat_axis=0, tiled=True)  18 us
    all_to_all x1, blocking collectives, body(): lax.all_to_all(least, everyone, split_axis=0, concat_axis=0, tiled=True)  11.3 us
    pallas_call x1, Pallas kernels, body(): pl.pallas_call(remote_force, out_shape=(jax.ShapeDtypeStruct((3, leaves,...  7.74 us
    pallas_call x1, Pallas kernels, body(): pl.pallas_call(local_force, out_shape=jax.ShapeDtypeStruct((3, leaves, wi...  6.09 us
    pallas_call x1, Pallas kernels, body(): pl.pallas_call(remote_density, out_shape=(sheet, sheet), in_specs=[smem,...  5.15 us
    unnamed x17, local copies, waits for them, and re-layouts  4.68 us
    pallas_call x1, Pallas kernels, body(): pl.pallas_call(local_density, out_shape=sheet, in_specs=[smem, vmem], out...  4.1 us
    all_to_all x1, starting transfers between devices, body(): lax.all_to_all(jnp.broadcast_to(term[None], (domains,) + term.shape), ('c...  3.51 us
  transfers between devices with their start and end apart: 2, of which 1 were waited for; matrix products, arithmetic and copies ran while one was open for 3% of the time, Pallas kernels for 15%

profile of v1, /device:TPU:0, one launch (start us, length us, event | category | flops | bytes accessed | tf_op | source)
XLA Modules:
  0.0 65.8 jit_solution(15729857238831523271)
XLA Ops:
  0.6 0.8 %pad_maximum_fusion.own_ref = f32[80,128]{1,0:T(8,128)S(1)} fusion(f32[16,128]{1,0:T(8,128)} %param.12, f32[16,128]{1,0:T(8,128)} %param.10, f32[48,128]{1,0:T(8,128)} %bitcast.8), kind=kLoop, calls=%fused_computation | loop fusion | flops 20480 | bytes 81920 | tf_op jit(solution)/shard_map/concatenate | solution.py:162
  1.4 0.0 copy-start.1
  1.4 0.6 copy-done.1
  2.0 18.0 %all_to_all.19.near_ref = f32[8,80,128]{2,1,0:T(8,128)S(1)} all-to-all(f32[8,80,128]{2,1,0:T(8,128)S(1)} %broadcast_in_dim.4), channel_id=1, replica_groups=mesh['grp'=2,'chip'=8,'core'=2] {'chip'}, dimensions={0} | all-to-all | bytes 655360 | tf_op jit(solution)/shard_map/all_to_all | solution.py:166
  20.0 0.0 copy-start
  20.0 0.0 collective-permute-start
  20.0 0.0 copy-start.5
  20.0 0.7 %copy-done.5 = s32[24,2]{0,1:T(2,128)S(1)} copy-done((s32[24,2]{0,1:T(2,128)S(1)}, s32[24,2]{0,1:T(2,128)}, u32[]{:S(2)}) %copy-start.5) | copy-done | bytes 216
  20.7 0.0 copy-start.6
  20.7 0.7 %copy.19.leaf_ref = s32[24,2]{1,0:T(8,128)} copy(s32[24,2]{0,1:T(2,128)S(1)} %copy-done.5) | data formatting | bytes 384 | tf_op args[7]
  21.4 0.0 copy-done.6
  21.4 0.0 copy-start.4
  21.4 0.7 %copy.20.route_ref = s32[24,1]{1,0:T(8,128)} copy(s32[24,1]{0,1:T(1,128)S(1)} %copy-done.6) | data formatting | bytes 192 | tf_op args[8]
  22.1 0.0 copy-done.4
  22.1 0.7 %copy.18.pair_ref = s32[16,2]{1,0:T(8,128)} copy(s32[16,2]{0,1:T(2,128)S(1)} %copy-done.4) | data formatting | bytes 256 | tf_op args[6]
  22.8 4.1 %local_density.1.local_ref = f32[16,128]{1,0:T(8,128)} custom-call(s32[16,2]{1,0:T(8,128)} %copy.18.pair_ref, f32[80,128]{1,0:T(8,128)} %copy-done.1), custom_call_target="tpu_custom_call" | custom-call | flops 7864320 | bytes 65536 | tf_op jit(solution)/shard_map/local_density/pallas_call | solution.py:176
  26.9 0.0 collective-permute-done.peer_ref
  26.9 0.0 copy-start.2
  26.9 0.0 copy-done
  26.9 0.7 %copy-done.2 = f32[8,80,128]{2,1,0:T(8,128)} copy-done((f32[8,80,128]{2,1,0:T(8,128)}, f32[8,80,128]{2,1,0:T(8,128)S(1)}, u32[]{:S(2)}) %copy-start.2) | copy-done | bytes 327704
  27.6 5.2 %remote_density.1 = (f32[16,128]{1,0:T(8,128)}, f32[16,128]{1,0:T(8,128)}) custom-call(s32[1]{0:T(128)} %bitcast.me_ref, s32[24,2]{1,0:T(8,128)} %copy.19.leaf_ref, s32[24,1]{1,0:T(8,128)} %copy.20.route_ref, f32[80,128]{1,0:T(8,128)} %copy-done.1, f32[8,80,128]{2,1,0:T(8,128)} %copy-done, f32[8,80,128]{2,1,0:T(8,128)} %copy-done.2, ...), custom_call_target="tpu_custom_call" | custom-call | flops 11796480 | bytes 65536 | tf_op jit(solution)/shard_map/remote_density/pallas_call | solution.py:210
  32.7 1.4 %broadcast_in_dim.5 = f32[16,16,128]{2,1,0:T(8,128)} broadcast(f32[16,128]{1,0:T(8,128)} %get-tuple-element.8.term_ref), dimensions={1,2} | broadcast | bytes 139264 | tf_op jit(solution)/shard_map/broadcast_in_dim | solution.py:226
  34.1 3.5 %all-to-all-start.1 = ((f32[16,16,128]{2,1,0:T(8,128)}), f32[16,16,128]{2,1,0:T(8,128)S(1)}, u32[]{:S(2)}, u32[]{:S(2)}) async-start(f32[16,16,128]{2,1,0:T(8,128)} %broadcast_in_dim.5), calls=%async_computation.1 | async-start | bytes 262144 | tf_op jit(solution)/shard_map/all_to_all | solution.py:225
  37.6 6.1 %local_force.1.local_ref = f32[3,16,128]{2,1,0:T(8,128)} custom-call(s32[16,2]{1,0:T(8,128)} %copy.18.pair_ref, f32[80,128]{1,0:T(8,128)} %copy-done.1, f32[16,128]{1,0:T(8,128)} %get-tuple-element.8.term_ref), custom_call_target="tpu_custom_call" | custom-call | flops 15728640 | bytes 65536 | tf_op jit(solution)/shard_map/local_force/pallas_call | solution.py:251
  43.7 1.8 %all-to-all-done.1.terms_ref = f32[16,16,128]{2,1,0:T(8,128)S(1)} async-done(((f32[16,16,128]{2,1,0:T(8,128)}), f32[16,16,128]{2,1,0:T(8,128)S(1)}, u32[]{:S(2)}, u32[]{:S(2)}) %all-to-all-start.1) | async-done | bytes 131104 | tf_op jit(solution)/shard_map/all_to_all | solution.py:225
  45.5 0.0 copy-start.3
  45.5 0.6 copy-done.3
  46.1 7.7 %remote_force.1 = (f32[3,16,128]{2,1,0:T(8,128)}, f32[32,128]{1,0:T(8,128)}) custom-call(s32[1]{0:T(128)} %bitcast.me_ref, s32[24,2]{1,0:T(8,128)} %copy.19.leaf_ref, s32[24,1]{1,0:T(8,128)} %copy.20.route_ref, f32[80,128]{1,0:T(8,128)} %copy-done.1, f32[8,80,128]{2,1,0:T(8,128)} %copy-done, f32[8,80,128]{2,1,0:T(8,128)} %copy-done.2, ...), custom_call_target="tpu_custom_call" | custom-call | flops 23592960 | bytes 65536 | tf_op jit(solution)/shard_map/remote_force/pallas_call | solution.py:293
  53.9 11.3 %all_to_all.20 = f32[32,1,128]{2,1,0:T(1,128)S(1)} all-to-all(f32[32,1,128]{2,1,0:T(1,128)} %bitcast.9), channel_id=1, replica_groups=mesh['grp'=2,'chip'=8,'core'=2] {'grp','chip','core'}, dimensions={0} | all-to-all | bytes 32768 | tf_op jit(solution)/shard_map/all_to_all | solution.py:309
  65.2 0.6 reduce_min.9
  (1 shorter events, 0.0 us)
Async XLA Ops:
  1.4 0.6 copy-start.1
  20.0 6.8 %copy-start = (f32[8,80,128]{2,1,0:T(8,128)}, f32[8,80,128]{2,1,0:T(8,128)S(1)}, u32[]{:S(2)}) copy-start(f32[8,80,128]{2,1,0:T(8,128)S(1)} %all_to_all.19.near_ref) | copy-start | bytes 983044
  20.0 6.8 %collective-permute-start = (f32[8,80,128]{2,1,0:T(8,128)S(1)}, f32[8,80,128]{2,1,0:T(8,128)S(1)}, u32[]{:S(2)}, u32[]{:S(2)}) collective-permute-start(f32[8,80,128]{2,1,0:T(8,128)S(1)} %all_to_all.19.near_ref), channel_id=1, source_target_pairs={{0,1},{1,0},{2,3},{3,2},{4,5},{5,4},{6,7},{7,6},{8,9},{9,8},{10,11... | collective-permute-start | bytes 983048 | tf_op jit(solution)/shard_map/ppermute | solution.py:167
  20.0 0.7 %copy-start.5 = (s32[24,2]{0,1:T(2,128)S(1)}, s32[24,2]{0,1:T(2,128)}, u32[]{:S(2)}) copy-start(s32[24,2]{0,1:T(2,128)} %param.16) | copy-start | bytes 580
  20.7 0.7 %copy-start.6 = (s32[24,1]{0,1:T(1,128)S(1)}, s32[24,1]{0,1:T(1,128)}, u32[]{:S(2)}) copy-start(s32[24,1]{0,1:T(1,128)} %param.17) | copy-start | bytes 292
  21.4 0.7 %copy-start.4 = (s32[16,2]{0,1:T(2,128)S(1)}, s32[16,2]{0,1:T(2,128)}, u32[]{:S(2)}) copy-start(s32[16,2]{0,1:T(2,128)} %param.15) | copy-start | bytes 388
  26.9 0.7 %copy-start.2 = (f32[8,80,128]{2,1,0:T(8,128)}, f32[8,80,128]{2,1,0:T(8,128)S(1)}, u32[]{:S(2)}) copy-start(f32[8,80,128]{2,1,0:T(8,128)S(1)} %collective-permute-done.peer_ref) | copy-start | bytes 983044
  34.1 11.4 %all-to-all-start.1 = ((f32[16,16,128]{2,1,0:T(8,128)}), f32[16,16,128]{2,1,0:T(8,128)S(1)}, u32[]{:S(2)}, u32[]{:S(2)}) async-start(f32[16,16,128]{2,1,0:T(8,128)} %broadcast_in_dim.5), calls=%async_computation.1 | async-start | bytes 262144 | tf_op jit(solution)/shard_map/all_to_all | solution.py:225
  45.5 0.7 copy-start.3

commit v2 on v0

v2 whole, which is shorter than its diff:
```python
import math

import jax
import jax.numpy as jnp
from jax import lax
from jax.experimental import pallas as pl
from jax.experimental.pallas import tpu as pltpu
from jax.sharding import Mesh, PartitionSpec as P

ADIABATIC = 5.0 / 3.0
COURANT = 0.3
GROUP = 4
TINY = 1e-30
NORM = 8.0 / math.pi
MIB = 1 << 20


def turn(rows):
    width = rows[0].shape[1]
    rows = list(rows) + [jnp.zeros_like(rows[0])] * (-len(rows) % 8)
    turned = jnp.concatenate(rows, axis=0).T
    return [jnp.broadcast_to(turned[:, k : k + 1], (width, width)) for k in range(len(rows))]


def separation(own, far):
    offset = [own[c] - far[c] for c in range(3)]
    square = offset[0] * offset[0] + offset[1] * offset[1] + offset[2] * offset[2]
    square = jnp.maximum(square, TINY)
    inverse = lax.rsqrt(square)
    return offset, square * inverse, inverse


def density_tile(own, far):
    far = turn(far)
    _, dist, _ = separation(own, far)
    ratio = dist * own[3]
    left = 1.0 - ratio
    inner = 1.0 - 6.0 * (ratio * ratio * left)
    remain = jnp.maximum(left, 0.0)
    outer = 2.0 * (remain * remain * remain)
    value = jnp.where(ratio < 0.5, inner, outer)
    return jnp.sum(value * far[3], axis=0, keepdims=True)


def slope(dist, smooth_inverse, scale):
    ratio = dist * smooth_inverse
    remain = jnp.maximum(1.0 - ratio, 0.0)
    return jnp.where(ratio < 0.5, ratio * (2.0 - 3.0 * ratio), remain * remain) * scale


def force_tile(own, far):
    offset, dist, inverse = separation(own, far)
    both = slope(dist, own[3], own[4]) + slope(dist, far[3], far[4])
    return offset, (inverse * far[5]) * both


def slope_scale(h):
    square = h * h
    return (3.0 * NORM) / (square * square)


def grouped(count, body):
    step = math.gcd(GROUP, count)

    def run(group, carry):
        for k in range(step):
            body(group * step + k)
        return carry

    lax.fori_loop(0, count // step, run, 0)


def row(ref, at):
    return ref[pl.ds(at, 1), :]


def add_row(ref, at, value):
    ref[pl.ds(at, 1), :] = ref[pl.ds(at, 1), :] + value


def solution(mesh):
    groups, domains = mesh.shape["grp"], mesh.shape["dom"]
    chips = domains // 2
    fine = Mesh(mesh.devices.reshape(groups, chips, 2), ("grp", "chip", "core"))
    everyone = ("grp", "chip", "core")
    members = groups * domains
    vmem = pl.BlockSpec(memory_space=pltpu.VMEM)
    smem = pl.BlockSpec(memory_space=pltpu.SMEM)

    def call(kernel, name, outs, ins, scratch, flops, mib):
        return pl.pallas_call(
            kernel,
            out_shape=outs,
            in_specs=ins,
            out_specs=jax.tree.map(lambda _: vmem, outs),
            scratch_shapes=scratch,
            cost_estimate=pl.CostEstimate(flops=flops, bytes_accessed=1 << 16, transcendentals=0),
            compiler_params=pltpu.CompilerParams(vmem_limit_bytes=mib * MIB),
            name=name,
        )

    def body(
        positions, smoothing, energy, mass, old_density, active, pair_list, export_leaves, export_route
    ):
        leaves, _, width = positions.shape
        pairs, exports = pair_list.shape[0], export_leaves.shape[0]
        f32 = jnp.float32

        def shape(*sizes):
            return jax.ShapeDtypeStruct(sizes, f32)

        place = positions.transpose(1, 0, 2)
        pair_list, export_leaves, export_route = pair_list.T, export_leaves.T, export_route.T
        own = jnp.concatenate([place.reshape(3 * leaves, width), smoothing, mass], axis=0)
        outgoing = jnp.broadcast_to(own[None], (chips,) + own.shape)
        near = lax.all_to_all(outgoing, "chip", split_axis=0, concat_axis=0, tiled=True)

        def local_density(pair_ref, place_ref, h_ref, mass_ref, out_ref, inverse):
            inverse[...] = 1.0 / h_ref[...]
            out_ref[...] = jnp.zeros_like(out_ref)

            def tile(e):
                mine, other = pair_ref[0, e], pair_ref[1, e]
                own_rows = [row(place_ref.at[c], mine) for c in range(3)] + [row(inverse, mine)]
                far_rows = [row(place_ref.at[c], other) for c in range(3)] + [row(mass_ref, other)]
                add_row(out_ref, mine, density_tile(own_rows, far_rows))

            grouped(pairs, tile)

        local_sum = call(
            local_density, "local_density", shape(leaves, width), [smem] + [vmem] * 3,
            [pltpu.VMEM((leaves, width), f32)], pairs * width * width * 30, 4,
        )(pair_list, place, smoothing, mass)
        near, local_sum = lax.optimization_barrier((near, local_sum))
        peer = lax.ppermute(near, "core", [(0, 1), (1, 0)])

        def export(leaf_ref, route_ref, near_ref, peer_ref, e, items):
            core = lax.axis_index("core")
            me = lax.axis_index("chip") * 2 + core
            other = leaf_ref[1, e]
            target = me + 1 + route_ref[0, e]
            target = jnp.where(target >= domains, target - domains, target)
            chip = target // 2
            same = (target - chip * 2) == core
            rows = [
                jnp.where(
                    same,
                    near_ref[chip, pl.ds(c * leaves + other, 1), :],
                    peer_ref[chip, pl.ds(c * leaves + other, 1), :],
                )
                for c in items
            ]
            return leaf_ref[0, e], target, other, rows

        def remote_density(
            leaf_ref, route_ref, place_ref, h_ref, mass_ref, near_ref, peer_ref, local_ref,
            energy_ref, old_ref, active_ref, density_ref, term_ref, spread_ref, inverse, total
        ):
            inverse[...] = 1.0 / h_ref[...]
            total[...] = local_ref[...]

            def tile(e):
                mine, _, _, far = export(leaf_ref, route_ref, near_ref, peer_ref, e, (0, 1, 2, 4))
                own_rows = [row(place_ref.at[c], mine) for c in range(3)] + [row(inverse, mine)]
                add_row(total, mine, density_tile(own_rows, far))

            grouped(exports, tile)
            h = h_ref[...]
            summed = (total[...] + mass_ref[...]) * (NORM / (h * h * h))
            density = jnp.where(active_ref[...] == 1, summed, old_ref[...])
            term = (ADIABATIC - 1.0) * energy_ref[...] / density
            density_ref[...] = density
            term_ref[...] = term
            for d in range(domains):
                spread_ref[d] = term

        density, term, outgoing = call(
            remote_density,
            "remote_density",
            (shape(leaves, width), shape(leaves, width), shape(domains, leaves, width)),
            [smem, smem] + [vmem] * 9,
            [pltpu.VMEM((leaves, width), f32)] * 2,
            exports * width * width * 30,
            4 + 2 * domains * leaves * width * 32 // MIB,
        )(
            export_leaves, export_route, place, smoothing, mass, near, peer, local_sum, energy,
            old_density, active,
        )
        terms = lax.all_to_all(
            outgoing, ("chip", "core"), split_axis=0, concat_axis=0, tiled=True
        )

        def prepare(
            pair_ref, leaf_ref, route_ref, place_ref, h_ref, mass_ref, near_ref, peer_ref,
            term_ref, sum_ref, weight_ref, inverse, scale, still
        ):
            inverse[...] = 1.0 / h_ref[...]
            scale[...] = slope_scale(h_ref[...])
            sum_ref[...] = jnp.zeros_like(sum_ref)
            still[...] = jnp.zeros_like(still)

            def mine_rows(mine):
                return [row(place_ref.at[c], mine) for c in range(3)] + [
                    row(inverse, mine),
                    row(scale, mine),
                ]

            def local_tile(e):
                mine, other = pair_ref[0, e], pair_ref[1, e]
                far = mine_rows(other) + [row(mass_ref, other), row(term_ref, other)]
                far = turn(far)
                offset, weight = force_tile(mine_rows(mine), far)
                weight = weight * (row(term_ref, mine) + far[6])
                for c in range(3):
                    part = jnp.sum(weight * offset[c], axis=0, keepdims=True)
                    add_row(sum_ref.at[c], mine, part)

            def remote_tile(e):
                mine, _, _, far = export(leaf_ref, route_ref, near_ref, peer_ref, e, (0, 1, 2, 3, 4))
                h = far[3]
                far = turn(far[:3] + [1.0 / h, slope_scale(h), far[4]])
                offset, weight = force_tile(mine_rows(mine), far)
                for c in range(3):
                    part = weight * offset[c]
                    weight_ref[e, c] = part
                    add_row(still.at[c], mine, jnp.sum(part, axis=0, keepdims=True))

            grouped(pairs, local_tile)
            grouped(exports, remote_tile)
            for c in range(3):
                sum_ref[c] = sum_ref[c] + term_ref[...] * still[c]

        stash = shape(exports, 3, width, width)
        stash_mib = exports * 3 * width * width * 4 // MIB + 1
        partial, weights = call(
            prepare,
            "prepare_force",
            (shape(3, leaves, width), stash),
            [smem] * 3 + [vmem] * 6,
            [pltpu.VMEM((leaves, width), f32)] * 2 + [pltpu.VMEM((3, leaves, width), f32)],
            (pairs + exports) * width * width * 60,
            6 + stash_mib + 2 * domains * leaves * width * 32 // MIB,
        )(
            pair_list, export_leaves, export_route, place, smoothing, mass, near, peer, term
        )

        def finish(
            leaf_ref, route_ref, h_ref, terms_ref, partial_ref, weight_ref, energy_ref, active_ref,
            accel_ref, least_ref, total
        ):
            total[...] = partial_ref[...]
            me = lax.axis_index("chip") * 2 + lax.axis_index("core")
            for first in range(0, exports, 8):
                many = min(8, exports - first)
                rows = []
                for e in range(first, first + many):
                    target = me + 1 + route_ref[0, e]
                    target = jnp.where(target >= domains, target - domains, target)
                    rows.append(terms_ref[target, pl.ds(leaf_ref[1, e], 1), :])
                columns = turn(rows)
                for k in range(many):
                    mine = leaf_ref[0, first + k]
                    for c in range(3):
                        part = weight_ref[first + k, c] * columns[k]
                        add_row(total.at[c], mine, jnp.sum(part, axis=0, keepdims=True))
            awake = active_ref[...] == 1
            square = jnp.zeros((leaves, width), f32)
            for c in range(3):
                part = jnp.where(awake, total[c], 0.0)
                accel_ref[c] = part
                square = square + part * part
            h = h_ref[...]
            speed = jnp.sqrt(ADIABATIC * (ADIABATIC - 1.0) * energy_ref[...])
            step = COURANT * h / (speed + jnp.sqrt(h * jnp.sqrt(square)))
            least_ref[...] = jnp.full(
                (members, width), jnp.min(jnp.where(awake, step, jnp.inf)), f32
            )

        accel, least = call(
            finish,
            "finish_force",
            (shape(3, leaves, width), shape(members, width)),
            [smem, smem] + [vmem] * 6,
            [pltpu.VMEM((3, leaves, width), f32)],
            exports * width * width * 6,
            4 + stash_mib + 2 * domains * leaves * width * 4 // MIB,
        )(export_leaves, export_route, smoothing, terms, partial, weights, energy, active)

        everywhere = lax.all_to_all(least, everyone, split_axis=0, concat_axis=0, tiled=True)
        return density, accel.transpose(1, 0, 2), jnp.min(everywhere)

    flat = P(everyone, None)
    deep = P(everyone, None, None)
    return jax.shard_map(
        body,
        mesh=fine,
        in_specs=(deep,) + (flat,) * 8,
        out_specs=(flat, deep, P()),
        check_vma=False,
    )
```

time: 108 us -> 72.9 us (0.68)
  blocking collectives: 38.3 us -> 12.9 us
  other arithmetic: 23.5 us -> 1.41 us
  Pallas kernels: 0 us -> 18.2 us
  local copies, waits for them, and re-layouts: 12.7 us -> 21.2 us
  waiting for transfers between devices: 12.9 us -> 6.34 us
  starting transfers between devices: 16.9 us -> 11 us
  matrix products: 1.74 us -> 0 us
    pmin x1 -> x0, blocking collectives: 38.3 us -> none  [body(): timestep = lax.pmin(local_least, ('grp', 'dom'))]
    unnamed x16 -> x50, local copies, waits for them, and re-layouts: 0.05 us -> 20.4 us
    pallas_call x0 -> x4, Pallas kernels: none -> 18.2 us  [the longest x1 8.54 us: body(): call(prepare, 'prepare_force', (shape(3, leaves, width), stash), [smem] *...]
    reduce_sum x26 -> x0, other arithmetic: 15.1 us -> none  [the longest x6 5.74 us: force_tile(): return -jnp.sum(weight[None, :, :] * offset, axis=2)]
    all_to_all x0 -> x1, blocking collectives: none -> 12.9 us  [body(): lax.all_to_all(least, everyone, split_axis=0, concat_axis=0, tiled=True)]
    gather x16 -> x0, local copies, waits for them, and re-layouts: 10.9 us -> none  [the longest x1 1.43 us: body(): send_target = jnp.where(filled, export_leaves[chosen, 1], 0)]
    all_to_all x3 -> x2, waiting for transfers between devices: 12.9 us -> 4.71 us  [the longest x1 4.71 us: body(): lax.all_to_all(outgoing, 'chip', split_axis=0, concat_axis=0, tiled=True)]
    all_to_all x3 -> x2, starting transfers between devices: 16.9 us -> 11 us  [the longest x1 7.31 us: body(): lax.all_to_all(outgoing, 'chip', split_axis=0, concat_axis=0, tiled=True)]
  transfers between devices with their start and end apart: 3 -> 3, of which waited for: 2 -> 2; matrix products, arithmetic and copies ran while one was open for 7% -> 0% of each run, Pallas kernels for 0% -> 16%
where the time goes in v2:
time: 72.9 us; the launch traced here: 71.7 us
  local copies, waits for them, and re-layouts  21.2 us (29%)
  Pallas kernels  18.2 us (25%)
  blocking collectives  12.9 us (18%)
  starting transfers between devices  11 us (15%)
  waiting for transfers between devices  6.34 us (9%)
  other arithmetic  1.41 us (2%)
    unnamed x50, local copies, waits for them, and re-layouts  20.4 us
    all_to_all x1, blocking collectives, body(): lax.all_to_all(least, everyone, split_axis=0, concat_axis=0, tiled=True)  12.9 us
    pallas_call x1, Pallas kernels, body(): call(prepare, 'prepare_force', (shape(3, leaves, width), stash), [smem] *...  8.54 us
    all_to_all x1, starting transfers between devices, body(): lax.all_to_all(outgoing, 'chip', split_axis=0, concat_axis=0, tiled=True)  7.31 us
    pallas_call x1, Pallas kernels, body(): call(remote_density, 'remote_density', (shape(leaves, width), shape(leave...  4.86 us
    all_to_all x1, waiting for transfers between devices, body(): lax.all_to_all(outgoing, 'chip', split_axis=0, concat_axis=0, tiled=True)  4.71 us
    all_to_all x1, starting transfers between devices, body(): lax.all_to_all(outgoing, ('chip', 'core'), split_axis=0, concat_axis=0, t...  3.72 us
    pallas_call x1, Pallas kernels, body(): call(local_density, 'local_density', shape(leaves, width), [smem] + [vmem...  2.77 us
  transfers between devices with their start and end apart: 3, of which 2 were waited for; matrix products, arithmetic and copies ran while one was open for 0% of the time, Pallas kernels for 16%

profile of v2, /device:TPU:0, one launch (start us, length us, event | category | flops | bytes accessed | tf_op | source)
XLA Modules:
  0.0 71.7 jit_solution(12735135639953594729)
XLA Ops:
  0.6 0.8 %pad_maximum_fusion = f32[80,128]{1,0:T(8,128)S(1)} fusion(f32[16,128]{1,0:T(8,128)} %mass_ref.5, f32[16,128]{1,0:T(8,128)} %h_ref.7, f32[48,128]{1,0:T(8,128)} %bitcast.10), kind=kLoop, calls=%fused_computation | loop fusion | flops 20480 | bytes 81920 | tf_op jit(solution)/shard_map/concatenate | solution.py:114
  1.4 0.7 %broadcast_in_dim.2 = f32[8,80,128]{2,1,0:T(8,128)} broadcast(f32[80,128]{1,0:T(8,128)S(1)} %pad_maximum_fusion), dimensions={1,2} | broadcast | bytes 368640 | tf_op jit(solution)/shard_map/broadcast_in_dim | solution.py:115
  2.2 7.3 %all-to-all-start = ((f32[8,80,128]{2,1,0:T(8,128)}), f32[8,80,128]{2,1,0:T(8,128)S(1)}, u32[]{:S(2)}, u32[]{:S(2)}) async-start(f32[8,80,128]{2,1,0:T(8,128)} %broadcast_in_dim.2), calls=%async_computation | async-start | bytes 655360 | tf_op jit(solution)/shard_map/all_to_all | solution.py:116
  9.5 0.7 %copy-done.2 = f32[16,3,128]{2,0,1:T(8,128)S(1)} copy-done((f32[16,3,128]{2,0,1:T(8,128)S(1)}, f32[16,3,128]{2,0,1:T(8,128)}, u32[]{:S(2)}) %copy-start.2) | copy-done | bytes 24600
  10.2 0.7 copy-done.5
  10.9 0.7 copy-done.9
  11.6 0.7 copy-done.23
  12.3 2.8 %local_density.1.local_ref = f32[16,128]{1,0:T(8,128)S(1)} custom-call(s32[2,16]{1,0:T(2,128)S(1)} %bitcast.21, f32[3,16,128]{2,1,0:T(8,128)S(1)} %bitcast.11, f32[16,128]{1,0:T(8,128)S(1)} %copy-done.5, f32[16,128]{1,0:T(8,128)S(1)} %copy-done.9), custom_call_target="tpu_custom_call" | custom-call | flops 7864320 | bytes 65536 | tf_op jit(solution)/shard_map/local_density/pallas_call | solution.py:130
  15.1 4.7 %all-to-all-done.near_ref = f32[8,80,128]{2,1,0:T(8,128)S(1)} async-done(((f32[8,80,128]{2,1,0:T(8,128)}), f32[8,80,128]{2,1,0:T(8,128)S(1)}, u32[]{:S(2)}, u32[]{:S(2)}) %all-to-all-start) | async-done | bytes 327712 | tf_op jit(solution)/shard_map/all_to_all | solution.py:116
  19.8 1.6 %collective-permute-done.peer_ref = f32[8,80,128]{2,1,0:T(8,128)S(1)} collective-permute-done((f32[8,80,128]{2,1,0:T(8,128)S(1)}, f32[8,80,128]{2,1,0:T(8,128)S(1)}, u32[]{:S(2)}, u32[]{:S(2)}) %collective-permute-start) | collective-permute-done | bytes 327712 | tf_op jit(solution)/shard_map/ppermute | solution.py:135
  21.4 0.7 %copy-done.3 = f32[16,3,128]{2,0,1:T(8,128)S(1)} copy-done((f32[16,3,128]{2,0,1:T(8,128)S(1)}, f32[16,3,128]{2,0,1:T(8,128)}, u32[]{:S(2)}) %copy-start.3) | copy-done | bytes 24600
  22.1 0.7 copy-done.6
  22.8 0.7 copy-done.10
  23.5 0.7 copy-done.12
  24.2 0.7 copy-done.14
  24.9 0.7 copy-done.16
  25.6 0.7 copy-done.19
  27.0 4.9 %remote_density.1 = (f32[16,128]{1,0:T(8,128)}, f32[16,128]{1,0:T(8,128)S(1)}, f32[16,16,128]{2,1,0:T(8,128)}) custom-call(s32[2,24]{1,0:T(2,128)S(1)} %bitcast.15, s32[1,24]{1,0:T(1,128)S(1)} %bitcast.18, f32[3,16,128]{2,1,0:T(8,128)S(1)} %bitcast.12, f32[16,128]{1,0:T(8,128)S(1)} %copy-done.6, f32[16,128]{1,0:T(8,128)S(1)} %copy-done.10, ...), custom_call_target="tpu_custom_call" | custom-call | flops 11796480 | bytes 65536 | tf_op jit(solution)/shard_map/remote_density/pallas_call | solution.py:177
  31.8 3.7 %all-to-all-start.1 = ((f32[16,16,128]{2,1,0:T(8,128)}), f32[16,16,128]{2,1,0:T(8,128)S(1)}, u32[]{:S(2)}, u32[]{:S(2)}) async-start(f32[16,16,128]{2,1,0:T(8,128)} %get-tuple-element.15), calls=%async_computation.1 | async-start | bytes 262144 | tf_op jit(solution)/shard_map/all_to_all | solution.py:189
  35.6 0.7 %copy-done.4 = f32[16,3,128]{2,0,1:T(8,128)S(1)} copy-done((f32[16,3,128]{2,0,1:T(8,128)S(1)}, f32[16,3,128]{2,0,1:T(8,128)}, u32[]{:S(2)}) %copy-start.4) | copy-done | bytes 24600
  36.3 0.7 copy-done.7
  37.0 0.7 copy-done.11
  37.7 0.7 copy-done.17
  39.0 0.7 copy-done.24
  39.7 8.5 %prepare_force.1 = (f32[3,16,128]{2,1,0:T(8,128)S(1)}, f32[24,3,128,128]{3,2,1,0:T(8,128)S(1)}) custom-call(s32[2,16]{1,0:T(2,128)S(1)} %bitcast.22, s32[2,24]{1,0:T(2,128)S(1)} %bitcast.16, s32[1,24]{1,0:T(1,128)S(1)} %bitcast.19, f32[3,16,128]{2,1,0:T(8,128)S(1)} %bitcast.13, f32[16,128]{1,0:T(8,128)S(1)} %copy-done.7, f32[16,128]{1,0:T(8,128)S(1)} %copy-done.11, ...), custom_call_target="tpu_custom_call" | custom-call | flops 39321600 | bytes 65536 | tf_op jit(solution)/shard_map/prepare_force/pallas_call | solution.py:235
  48.2 2.2 %copy-done = f32[24,3,128,128]{3,2,1,0:T(8,128)} copy-done((f32[24,3,128,128]{3,2,1,0:T(8,128)}, f32[24,3,128,128]{3,2,1,0:T(8,128)S(1)}, u32[]{:S(2)}) %copy-start) | copy-done | bytes 4718616
  50.4 2.3 %copy-done.1 = f32[24,3,128,128]{3,2,1,0:T(8,128)S(1)} copy-done((f32[24,3,128,128]{3,2,1,0:T(8,128)S(1)}, f32[24,3,128,128]{3,2,1,0:T(8,128)}, u32[]{:S(2)}) %copy-start.1) | copy-done | bytes 4718616
  52.7 0.7 copy-done.8
  53.4 0.7 copy-done.13
  54.1 0.7 copy-done.15
  56.2 2.0 %finish_force.1 = (f32[3,16,128]{2,1,0:T(8,128)}, f32[32,128]{1,0:T(8,128)S(1)}) custom-call(s32[2,24]{1,0:T(2,128)S(1)} %bitcast.17, s32[1,24]{1,0:T(1,128)S(1)} %bitcast.20, f32[16,128]{1,0:T(8,128)S(1)} %copy-done.8, f32[16,16,128]{2,1,0:T(8,128)S(1)} %all-to-all-done.1.terms_ref, f32[3,16,128]{2,1,0:T(8,128)S(1)} %get-tuple-element.17.partial_ref, ...), custom_call_target="tpu_custom_call" | custom-call | flops 2359296 | bytes 65536 | tf_op jit(solution)/shard_map/finish_force/pallas_call | solution.py:279
  58.2 12.9 %all_to_all.19 = f32[32,1,128]{2,1,0:T(1,128)S(1)} all-to-all(f32[32,1,128]{2,1,0:T(1,128)S(1)} %bitcast.14), channel_id=1, replica_groups=mesh['grp'=2,'chip'=8,'core'=2] {'grp','chip','core'}, dimensions={0} | all-to-all | bytes 32768 | tf_op jit(solution)/shard_map/all_to_all | solution.py:289
  (32 shorter events, 3.3 us)
Async XLA Ops:
  2.2 17.6 %all-to-all-start = ((f32[8,80,128]{2,1,0:T(8,128)}), f32[8,80,128]{2,1,0:T(8,128)S(1)}, u32[]{:S(2)}, u32[]{:S(2)}) async-start(f32[8,80,128]{2,1,0:T(8,128)} %broadcast_in_dim.2), calls=%async_computation | async-start | bytes 655360 | tf_op jit(solution)/shard_map/all_to_all | solution.py:116
  9.5 0.7 %copy-start.2 = (f32[16,3,128]{2,0,1:T(8,128)S(1)}, f32[16,3,128]{2,0,1:T(8,128)}, u32[]{:S(2)}) copy-start(f32[16,3,128]{2,0,1:T(8,128)} %param.9) | copy-start | bytes 73732
  10.2 0.7 copy-start.5
  10.9 0.7 copy-start.9
  11.6 0.7 copy-start.23
  19.8 1.6 %collective-permute-start = (f32[8,80,128]{2,1,0:T(8,128)S(1)}, f32[8,80,128]{2,1,0:T(8,128)S(1)}, u32[]{:S(2)}, u32[]{:S(2)}) collective-permute-start(f32[8,80,128]{2,1,0:T(8,128)S(1)} %all-to-all-done.near_ref), channel_id=1, source_target_pairs={{0,1},{1,0},{2,3},{3,2},{4,5},{5,4},{6,7},{7,6},{8,9},{9,8},{10,11... | collective-permute-start | bytes 983048 | tf_op jit(solution)/shard_map/ppermute | solution.py:135
  21.4 0.7 %copy-start.3 = (f32[16,3,128]{2,0,1:T(8,128)S(1)}, f32[16,3,128]{2,0,1:T(8,128)}, u32[]{:S(2)}) copy-start(f32[16,3,128]{2,0,1:T(8,128)} %param.9) | copy-start | bytes 73732
  22.1 0.7 copy-start.6
  22.8 0.7 copy-start.10
  23.5 0.7 copy-start.12
  24.2 0.7 copy-start.14
  24.9 0.7 copy-start.16
  25.6 0.7 copy-start.19
  26.3 0.7 copy-start.20
  31.8 18.6 %all-to-all-start.1 = ((f32[16,16,128]{2,1,0:T(8,128)}), f32[16,16,128]{2,1,0:T(8,128)S(1)}, u32[]{:S(2)}, u32[]{:S(2)}) async-start(f32[16,16,128]{2,1,0:T(8,128)} %get-tuple-element.15), calls=%async_computation.1 | async-start | bytes 262144 | tf_op jit(solution)/shard_map/all_to_all | solution.py:189
  35.5 0.7 %copy-start.4 = (f32[16,3,128]{2,0,1:T(8,128)S(1)}, f32[16,3,128]{2,0,1:T(8,128)}, u32[]{:S(2)}) copy-start(f32[16,3,128]{2,0,1:T(8,128)} %param.9) | copy-start | bytes 73732
  36.3 0.7 copy-start.7
  37.0 0.7 copy-start.11
  37.7 0.7 copy-start.17
  38.4 0.7 copy-start.21
  39.0 0.7 copy-start.24
  48.2 2.2 %copy-start = (f32[24,3,128,128]{3,2,1,0:T(8,128)}, f32[24,3,128,128]{3,2,1,0:T(8,128)S(1)}, u32[]{:S(2)}) copy-start(f32[24,3,128,128]{3,2,1,0:T(8,128)S(1)} %get-tuple-element.18.weight_ref) | copy-start | bytes 14155780
  50.4 2.3 %copy-start.1 = (f32[24,3,128,128]{3,2,1,0:T(8,128)S(1)}, f32[24,3,128,128]{3,2,1,0:T(8,128)}, u32[]{:S(2)}) copy-start(f32[24,3,128,128]{3,2,1,0:T(8,128)} %copy-done) | copy-start | bytes 14155780
  52.7 0.7 copy-start.8
  53.4 0.7 copy-start.13
  54.1 0.7 copy-start.15
  54.8 0.7 copy-start.18
  55.5 0.7 copy-start.22

commit v3 on v2

v3 whole, which is shorter than its diff:
```python
import math

import jax
import jax.numpy as jnp
from jax import lax
from jax.experimental import pallas as pl
from jax.experimental.pallas import tpu as pltpu
from jax.sharding import Mesh, PartitionSpec as P

ADIABATIC = 5.0 / 3.0
COURANT = 0.3
GROUP = 4
TINY = 1e-30
NORM = 8.0 / math.pi
MIB = 1 << 20
X, MASS, H, INVERSE, SCALE, ORIGIN, ENERGY, OLD, ACTIVE, SUM, TABLE = 0, 3, 4, 5, 6, 7, 10, 11, 12, 13, 14


def product(a, b, dims):
    return lax.dot_general(
        a, b, (dims, ((), ())), precision=lax.Precision.HIGHEST, preferred_element_type=jnp.float32
    )


def turn(rows):
    width, count = rows[0].shape[1], len(rows)
    rows = list(rows) + [jnp.zeros_like(rows[0])] * (-count % 8)
    turned = jnp.concatenate(rows, axis=0).T
    return [jnp.broadcast_to(turned[:, k : k + 1], (width, width)) for k in range(count)]


def separation(right, place):
    norm = place[0] * place[0] + place[1] * place[1] + place[2] * place[2]
    zero = jnp.zeros_like(norm)
    left = jnp.concatenate(place + [norm, jnp.ones_like(norm), zero, zero, zero], axis=0)
    square = jnp.maximum(product(left, right, ((0,), (0,))), TINY)
    inverse = lax.rsqrt(square)
    return square * inverse, inverse


def density_tile(right, own_inverse, place, mass):
    (mass,) = turn([mass])
    dist, _ = separation(right, place)
    ratio = dist * own_inverse
    left = 1.0 - ratio
    inner = 1.0 - 6.0 * (ratio * ratio * left)
    remain = jnp.maximum(left, 0.0)
    outer = 2.0 * (remain * remain * remain)
    value = jnp.where(ratio < 0.5, inner, outer)
    return jnp.sum(value * mass, axis=0, keepdims=True)


def slope(dist, smooth_inverse, scale):
    ratio = dist * smooth_inverse
    remain = jnp.maximum(1.0 - ratio, 0.0)
    return jnp.where(ratio < 0.5, ratio * (2.0 - 3.0 * ratio), remain * remain) * scale


def weight_tile(right, own_inverse, own_scale, place, inverse, scale):
    inverse, scale = turn([inverse, scale])
    dist, over = separation(right, place)
    return over * (slope(dist, own_inverse, own_scale) + slope(dist, inverse, scale))


def moments(mass, place):
    half = [mass] + [mass * item for item in place]
    return jnp.concatenate(half + half, axis=0)


def force(weights, rows, far_term, own_term, own_place):
    item = lax.broadcasted_iota(jnp.int32, rows.shape, 0)
    rows = jnp.where(item < 4, rows, rows * far_term)
    sums = product(rows, weights, ((1,), (0,)))
    sums = own_term * sums[:4] + sums[4:]
    return own_place[:4] * sums[:1] - sums


def slope_scale(h):
    square = h * h
    return (3.0 * NORM) / (square * square)


def grouped(count, body):
    step = math.gcd(GROUP, count)

    def run(group, carry):
        for k in range(step):
            body(group * step + k)
        return carry

    lax.fori_loop(0, count // step, run, 0)


def fetch(sems, *pairs):
    copies = [pltpu.make_async_copy(a, b, sems.at[i]) for i, (a, b) in enumerate(pairs)]
    for copy in copies:
        copy.start()
    for copy in copies:
        copy.wait()


def solution(mesh):
    groups, domains = mesh.shape["grp"], mesh.shape["dom"]
    chips = domains // 2
    fine = Mesh(mesh.devices.reshape(groups, chips, 2), ("grp", "chip", "core"))
    everyone = ("grp", "chip", "core")
    members = groups * domains
    vmem = pl.BlockSpec(memory_space=pltpu.VMEM)
    hbm = pl.BlockSpec(memory_space=pltpu.HBM)

    def call(kernel, name, outs, ins, scratch, flops, mib):
        return pl.pallas_call(
            kernel,
            out_shape=outs,
            in_specs=ins,
            out_specs=jax.tree.map(lambda _: vmem, outs),
            scratch_shapes=scratch,
            cost_estimate=pl.CostEstimate(flops=flops, bytes_accessed=1 << 16, transcendentals=0),
            compiler_params=pltpu.CompilerParams(vmem_limit_bytes=mib * MIB),
            name=name,
        )

    def body(
        positions, smoothing, energy, mass, old_density, active, pair_list, export_leaves, export_route
    ):
        leaves, _, width = positions.shape
        pairs, exports = pair_list.shape[0], export_leaves.shape[0]
        f32, s32 = jnp.float32, jnp.int32
        tile_flops = width * width

        def shape(*sizes):
            return jax.ShapeDtypeStruct(sizes, f32)

        place = positions.transpose(1, 0, 2)
        pair_list, export_leaves, export_route = pair_list.T, export_leaves.T, export_route.T
        pair_table, leaf_table = pltpu.SMEM((2, pairs), s32), pltpu.SMEM((2, exports), s32)
        route_table = pltpu.SMEM((1, exports), s32)

        outgoing = jnp.concatenate(
            [
                jnp.broadcast_to(item[None], (chips,) + item.shape)
                for item in (place.reshape(3 * leaves, width), smoothing, mass)
            ],
            axis=1,
        )
        near = lax.all_to_all(outgoing, "chip", split_axis=0, concat_axis=0, tiled=True)

        def row(own_ref, item, leaf):
            return own_ref[item, pl.ds(leaf, 1), :]

        def local_place(own_ref, mine, other):
            return [row(own_ref, X + c, other) - row(own_ref, ORIGIN + c, mine) for c in range(3)]

        def local_density(
            pair_hbm, place_hbm, h_hbm, mass_hbm, energy_hbm, old_hbm, active_hbm, own_ref, right_ref,
            centred_ref, pair_ref, active_ref, sems
        ):
            fetch(
                sems,
                (pair_hbm, pair_ref),
                (place_hbm, own_ref.at[pl.ds(X, 3)]),
                (h_hbm, own_ref.at[H]),
                (mass_hbm, own_ref.at[MASS]),
                (energy_hbm, own_ref.at[ENERGY]),
                (old_hbm, own_ref.at[OLD]),
                (active_hbm, active_ref),
            )
            h = own_ref[H]
            own_ref[ACTIVE] = active_ref[...].astype(f32)
            own_ref[INVERSE] = 1.0 / h
            own_ref[SCALE] = slope_scale(h)
            own_ref[SUM] = jnp.zeros_like(h)
            norm = jnp.zeros_like(h)
            centred = []
            for c in range(3):
                mean = jnp.sum(own_ref[X + c], axis=1, keepdims=True) * (1.0 / width)
                mean = jnp.broadcast_to(mean, h.shape)
                own_ref[ORIGIN + c] = mean
                item = own_ref[X + c] - mean
                norm = norm + item * item
                centred.append(item)
            zero, one = jnp.zeros_like(h), jnp.ones_like(h)
            rights = [-2.0 * item for item in centred] + [one, norm, zero, zero, zero]
            places = [zero] + centred + [zero] * 4
            for k in range(8):
                for leaf in range(leaves):
                    right_ref[leaf, k : k + 1, :] = rights[k][leaf : leaf + 1]
                    centred_ref[leaf, k : k + 1, :] = places[k][leaf : leaf + 1]

            def tile(e):
                mine, other = pair_ref[0, e], pair_ref[1, e]
                own_ref[SUM, pl.ds(mine, 1), :] = row(own_ref, SUM, mine) + density_tile(
                    right_ref[mine],
                    row(own_ref, INVERSE, mine),
                    local_place(own_ref, mine, other),
                    row(own_ref, MASS, other),
                )

            grouped(pairs, tile)

        own, right, centred = call(
            local_density,
            "local_density",
            (shape(TABLE, leaves, width), shape(leaves, 8, width), shape(leaves, 8, width)),
            [hbm] * 7,
            [pair_table, pltpu.VMEM((leaves, width), s32), pltpu.SemaphoreType.DMA((7,))],
            pairs * tile_flops * 30,
            4,
        )(pair_list, place, smoothing, mass, energy, old_density, active)
        near, own = lax.optimization_barrier((near, own))
        peer = lax.ppermute(near, "core", [(0, 1), (1, 0)])

        def export(leaf_ref, route_ref, near_ref, peer_ref, own_ref, e, items):
            core = lax.axis_index("core")
            me = lax.axis_index("chip") * 2 + core
            mine, other = leaf_ref[0, e], leaf_ref[1, e]
            target = me + 1 + route_ref[0, e]
            target = jnp.where(target >= domains, target - domains, target)
            chip = target // 2
            same = (target - chip * 2) == core

            def get(c):
                at = pl.ds(c * leaves + other, 1)
                return jnp.where(same, near_ref[chip, at, :], peer_ref[chip, at, :])

            spot = [get(c) - row(own_ref, ORIGIN + c, mine) for c in range(3)]
            return mine, spot, [get(c) for c in items]

        def remote_density(
            leaf_hbm, route_hbm, own_ref, right_ref, near_ref, peer_ref, density_ref, term_ref,
            spread_ref, total, leaf_ref, route_ref, sems
        ):
            fetch(sems, (leaf_hbm, leaf_ref), (route_hbm, route_ref))
            total[...] = own_ref[SUM]

            def tile(e):
                mine, spot, (far_mass,) = export(
                    leaf_ref, route_ref, near_ref, peer_ref, own_ref, e, (4,)
                )
                at = pl.ds(mine, 1)
                total[at, :] = total[at, :] + density_tile(
                    right_ref[mine], row(own_ref, INVERSE, mine), spot, far_mass
                )

            grouped(exports, tile)
            inverse = own_ref[INVERSE]
            summed = (total[...] + own_ref[MASS]) * (NORM * (inverse * inverse * inverse))
            density = jnp.where(own_ref[ACTIVE] == 1.0, summed, own_ref[OLD])
            term = (ADIABATIC - 1.0) * own_ref[ENERGY] / density
            density_ref[...] = density
            term_ref[...] = term
            for d in range(domains):
                spread_ref[d] = term

        wire_mib = 2 * domains * leaves * width * 20 // MIB
        density, term, outgoing = call(
            remote_density,
            "remote_density",
            (shape(leaves, width), shape(leaves, width), shape(domains, leaves, width)),
            [hbm] * 2 + [vmem] * 4,
            [pltpu.VMEM((leaves, width), f32), leaf_table, route_table, pltpu.SemaphoreType.DMA((2,))],
            exports * tile_flops * 30,
            6 + wire_mib,
        )(export_leaves, export_route, own, right, near, peer)
        terms = lax.all_to_all(outgoing, ("chip", "core"), split_axis=0, concat_axis=0, tiled=True)

        def prepare(
            pair_hbm, leaf_hbm, route_hbm, own_ref, right_ref, centred_ref, near_ref, peer_ref,
            term_ref, sum_ref, weight_ref, moment_ref, pair_ref, leaf_ref, route_ref, sems
        ):
            fetch(sems, (pair_hbm, pair_ref), (leaf_hbm, leaf_ref), (route_hbm, route_ref))
            sum_ref[...] = jnp.zeros_like(sum_ref)

            def weigh(mine, spot, inverse, scale):
                return weight_tile(
                    right_ref[mine],
                    row(own_ref, INVERSE, mine),
                    row(own_ref, SCALE, mine),
                    spot,
                    inverse,
                    scale,
                )

            def local_tile(e):
                mine, other = pair_ref[0, e], pair_ref[1, e]
                spot = local_place(own_ref, mine, other)
                weights = weigh(mine, spot, row(own_ref, INVERSE, other), row(own_ref, SCALE, other))
                rows = moments(row(own_ref, MASS, other), spot)
                far_term, own_term = term_ref[pl.ds(other, 1), :], term_ref[pl.ds(mine, 1), :]
                sum_ref[mine] = sum_ref[mine] + force(
                    weights, rows, far_term, own_term, centred_ref[mine]
                )

            def remote_tile(e):
                mine, spot, (h, far_mass) = export(
                    leaf_ref, route_ref, near_ref, peer_ref, own_ref, e, (3, 4)
                )
                weight_ref[e] = weigh(mine, spot, 1.0 / h, slope_scale(h))
                moment_ref[e] = moments(far_mass, spot)

            grouped(pairs, local_tile)
            grouped(exports, remote_tile)

        stash_mib = 2 * exports * width * (width + 8) * 4 // MIB
        partial, weights, rows = call(
            prepare,
            "prepare_force",
            (shape(leaves, 4, width), shape(exports, width, width), shape(exports, 8, width)),
            [hbm] * 3 + [vmem] * 6,
            [pair_table, leaf_table, route_table, pltpu.SemaphoreType.DMA((3,))],
            (pairs + exports) * tile_flops * 60,
            6 + stash_mib + wire_mib,
        )(pair_list, export_leaves, export_route, own, right, centred, near, peer, term)

        def finish(
            leaf_hbm, route_hbm, own_ref, centred_ref, term_ref, terms_ref, partial_ref, weight_ref,
            moment_ref, accel_ref, least_ref, total, leaf_ref, route_ref, sems
        ):
            fetch(sems, (leaf_hbm, leaf_ref), (route_hbm, route_ref))
            total[...] = partial_ref[...]
            me = lax.axis_index("chip") * 2 + lax.axis_index("core")

            def tile(e):
                mine, other = leaf_ref[0, e], leaf_ref[1, e]
                target = me + 1 + route_ref[0, e]
                target = jnp.where(target >= domains, target - domains, target)
                far_term = terms_ref[target, pl.ds(other, 1), :]
                total[mine] = total[mine] + force(
                    weight_ref[e],
                    moment_ref[e],
                    far_term,
                    term_ref[pl.ds(mine, 1), :],
                    centred_ref[mine],
                )

            grouped(exports, tile)
            for c in range(3):
                for leaf in range(leaves):
                    accel_ref[c, leaf : leaf + 1, :] = total[leaf, c + 1 : c + 2, :]
            awake = own_ref[ACTIVE] == 1.0
            square = jnp.zeros((leaves, width), f32)
            for c in range(3):
                part = jnp.where(awake, accel_ref[c], 0.0)
                accel_ref[c] = part
                square = square + part * part
            h = own_ref[H]
            speed = jnp.sqrt(ADIABATIC * (ADIABATIC - 1.0) * own_ref[ENERGY])
            step = COURANT * h / (speed + jnp.sqrt(h * jnp.sqrt(square)))
            least_ref[...] = jnp.full(
                (members, width), jnp.min(jnp.where(awake, step, jnp.inf)), f32
            )

        accel, least = call(
            finish,
            "finish_force",
            (shape(3, leaves, width), shape(members, width)),
            [hbm] * 2 + [vmem] * 7,
            [pltpu.VMEM((leaves, 4, width), f32), leaf_table, route_table, pltpu.SemaphoreType.DMA((2,))],
            exports * tile_flops * 16,
            6 + stash_mib + wire_mib,
        )(export_leaves, export_route, own, centred, term, terms, partial, weights, rows)

        everywhere = lax.all_to_all(least, everyone, split_axis=0, concat_axis=0, tiled=True)
        return density, accel.transpose(1, 0, 2), jnp.min(everywhere)

    flat = P(everyone, None)
    deep = P(everyone, None, None)
    return jax.shard_map(
        body,
        mesh=fine,
        in_specs=(deep,) + (flat,) * 8,
        out_specs=(flat, deep, P()),
        check_vma=False,
    )
```

time: 72.9 us -> 57 us (0.78); the launches traced: 71.7 us -> 56.6 us
  local copies, waits for them, and re-layouts: 21.2 us -> 2.24 us
  Pallas kernels: 18.2 us -> 22.7 us
  waiting for transfers between devices: 6.34 us -> 5.49 us
    unnamed x50 -> x18, local copies, waits for them, and re-layouts: 20.4 us -> 0.04 us
    pallas_call x2, Pallas kernels: 11.3 us -> 14.7 us  [the longest x1 8.29 us: body(): call(prepare, 'prepare_force', (shape(leaves, 4, width), shape(exports, w...]
    broadcast_in_dim x1 -> x3, local copies, waits for them, and re-layouts: 0.75 us -> 2.2 us  [body(): jnp.broadcast_to(item[None], (chips,) + item.shape)]
    pallas_call x1, Pallas kernels: 2.01 us -> 3.19 us  [body(): call(finish, 'finish_force', (shape(3, leaves, width), shape(members, wid...]
    all_to_all x1, waiting for transfers between devices: 4.71 us -> 3.86 us  [body(): lax.all_to_all(outgoing, 'chip', split_axis=0, concat_axis=0, tiled=True)]
  transfers between devices with their start and end apart: 3 -> 3, of which waited for: 2 -> 2; matrix products, arithmetic and copies ran while one was open for 0% -> 0% of each run, Pallas kernels for 16% -> 26%
where the time goes in v3:
time: 57 us; the launch traced here: 56.6 us
  Pallas kernels  22.7 us (40%)
  blocking collectives  12.9 us (23%)
  starting transfers between devices  11 us (19%)
  waiting for transfers between devices  5.49 us (10%)
  local copies, waits for them, and re-layouts  2.24 us (4%)
  other arithmetic  1.37 us (2%)
  between operations  0.81 us (1%)
    all_to_all x1, blocking collectives, body(): lax.all_to_all(least, everyone, split_axis=0, concat_axis=0, tiled=True)  12.9 us
    pallas_call x1, Pallas kernels, body(): call(prepare, 'prepare_force', (shape(leaves, 4, width), shape(exports, w...  8.29 us
    all_to_all x1, starting transfers between devices, body(): lax.all_to_all(outgoing, 'chip', split_axis=0, concat_axis=0, tiled=True)  7.31 us
    pallas_call x1, Pallas kernels, body(): call(local_density, 'local_density', (shape(TABLE, leaves, width), shape(...  6.37 us
    pallas_call x1, Pallas kernels, body(): call(remote_density, 'remote_density', (shape(leaves, width), shape(leave...  4.84 us
    all_to_all x1, waiting for transfers between devices, body(): lax.all_to_all(outgoing, 'chip', split_axis=0, concat_axis=0, tiled=True)  3.86 us
    all_to_all x1, starting transfers between devices, body(): lax.all_to_all(outgoing, ('chip', 'core'), split_axis=0, concat_axis=0, t...  3.71 us
    pallas_call x1, Pallas kernels, body(): call(finish, 'finish_force', (shape(3, leaves, width), shape(members, wid...  3.19 us
  transfers between devices with their start and end apart: 3, of which 2 were waited for; matrix products, arithmetic and copies ran while one was open for 0% of the time, Pallas kernels for 26%

profile of v3, /device:TPU:0, one launch (start us, length us, event | category | flops | bytes accessed | tf_op | source)
XLA Modules:
  0.0 56.6 jit_solution(9531559375319237689)
XLA Ops:
  0.6 0.0 copy-start.1
  0.6 0.0 copy-start.2
  0.7 0.0 copy-start
  0.7 0.0 copy-start.8
  0.7 0.0 copy-start.6
  0.7 0.0 copy-start.5
  0.7 0.0 copy-start.4
  0.7 0.0 copy-start.7
  0.7 0.0 copy-start.3
  0.7 0.8 %broadcast_in_dim.10 = f32[8,16,128]{2,1,0:T(8,128)S(1)} broadcast(f32[16,128]{1,0:T(8,128)} %h_hbm.1), dimensions={1,2} | broadcast | bytes 73728 | tf_op jit(solution)/shard_map/broadcast_in_dim | solution.py:141
  1.5 0.7 %broadcast_in_dim.22 = f32[8,16,128]{2,1,0:T(8,128)S(1)} broadcast(f32[16,128]{1,0:T(8,128)} %mass_hbm.1), dimensions={1,2} | broadcast | bytes 73728 | tf_op jit(solution)/shard_map/broadcast_in_dim | solution.py:141
  2.2 0.8 %broadcast_in_dim.9 = f32[8,48,128]{2,1,0:T(8,128)S(1)} broadcast(f32[48,128]{1,0:T(8,128)} %bitcast.10), dimensions={1,2} | broadcast | bytes 221184 | tf_op jit(solution)/shard_map/broadcast_in_dim | solution.py:141
  2.9 0.7 %pad_maximum_fusion = f32[8,80,128]{2,1,0:T(8,128)} fusion(f32[8,16,128]{2,1,0:T(8,128)S(1)} %broadcast_in_dim.22, f32[8,16,128]{2,1,0:T(8,128)S(1)} %broadcast_in_dim.10, f32[8,48,128]{2,1,0:T(8,128)S(1)} %broadcast_in_dim.9), kind=kLoop, calls=%fused_computation | loop fusion | flops 163840 | bytes 655360 | tf_op jit(solution)/shard_map/concatenate | solution.py:139
  3.7 7.3 %all-to-all-start = ((f32[8,80,128]{2,1,0:T(8,128)}), f32[8,80,128]{2,1,0:T(8,128)S(1)}, u32[]{:S(2)}, u32[]{:S(2)}) async-start(f32[8,80,128]{2,1,0:T(8,128)} %pad_maximum_fusion), calls=%async_computation | async-start | bytes 655360 | tf_op jit(solution)/shard_map/all_to_all | solution.py:146
  11.0 0.0 copy-done.2
  11.0 0.0 copy-done
  11.0 0.0 copy-done.8
  11.0 0.0 copy-done.6
  11.0 0.0 copy-done.5
  11.0 0.0 copy-done.4
  11.0 6.4 %local_density.1 = (f32[14,16,128]{2,1,0:T(8,128)S(1)}, f32[16,8,128]{2,1,0:T(8,128)S(1)}, f32[16,8,128]{2,1,0:T(8,128)S(1)}) custom-call(s32[2,16]{1,0:T(2,128)S(1)} %bitcast.19, f32[3,16,128]{2,1,0:T(8,128)S(1)} %bitcast.11, f32[16,128]{1,0:T(8,128)S(1)} %copy-done.1, f32[16,128]{1,0:T(8,128)S(1)} %copy-done.2, f32[16,128]{1,0:T(8,128)S(1)} %copy-done.4, ...), custom_call_target="tpu_custom_call" | custom-call | flops 7864320 | bytes 65536 | tf_op jit(solution)/shard_map/local_density/pallas_call | solution.py:201
  17.4 3.9 %all-to-all-done.near_ref = f32[8,80,128]{2,1,0:T(8,128)S(1)} async-done(((f32[8,80,128]{2,1,0:T(8,128)}), f32[8,80,128]{2,1,0:T(8,128)S(1)}, u32[]{:S(2)}, u32[]{:S(2)}) %all-to-all-start) | async-done | bytes 327712 | tf_op jit(solution)/shard_map/all_to_all | solution.py:146
  21.3 0.0 collective-permute-start
  21.3 1.6 %collective-permute-done.peer_ref = f32[8,80,128]{2,1,0:T(8,128)S(1)} collective-permute-done((f32[8,80,128]{2,1,0:T(8,128)S(1)}, f32[8,80,128]{2,1,0:T(8,128)S(1)}, u32[]{:S(2)}, u32[]{:S(2)}) %collective-permute-start) | collective-permute-done | bytes 327712 | tf_op jit(solution)/shard_map/ppermute | solution.py:211
  22.9 0.0 copy-done.3
  22.9 4.8 %remote_density.1 = (f32[16,128]{1,0:T(8,128)}, f32[16,128]{1,0:T(8,128)S(1)}, f32[16,16,128]{2,1,0:T(8,128)}) custom-call(s32[2,24]{1,0:T(2,128)S(1)} %bitcast.13, s32[1,24]{1,0:T(1,128)S(1)} %bitcast.16, f32[14,16,128]{2,1,0:T(8,128)S(1)} %get-tuple-element.17.own_ref, f32[16,8,128]{2,1,0:T(8,128)S(1)} %get-tuple-element.18.right_ref, ...), custom_call_target="tpu_custom_call" | custom-call | flops 11796480 | bytes 65536 | tf_op jit(solution)/shard_map/remote_density/pallas_call | solution.py:256
  27.8 3.7 %all-to-all-start.1 = ((f32[16,16,128]{2,1,0:T(8,128)}), f32[16,16,128]{2,1,0:T(8,128)S(1)}, u32[]{:S(2)}, u32[]{:S(2)}) async-start(f32[16,16,128]{2,1,0:T(8,128)} %get-tuple-element.23), calls=%async_computation.1 | async-start | bytes 262144 | tf_op jit(solution)/shard_map/all_to_all | solution.py:265
  31.5 8.3 %prepare_force.1 = (f32[16,4,128]{2,1,0:T(4,128)S(1)}, f32[24,128,128]{2,1,0:T(8,128)S(1)}, f32[24,8,128]{2,1,0:T(8,128)S(1)}) custom-call(s32[2,16]{1,0:T(2,128)S(1)} %bitcast.20, s32[2,24]{1,0:T(2,128)S(1)} %bitcast.14, s32[1,24]{1,0:T(1,128)S(1)} %bitcast.17, f32[14,16,128]{2,1,0:T(8,128)S(1)} %get-tuple-element.17.own_ref, ...), custom_call_target="tpu_custom_call" | custom-call | flops 39321600 | bytes 65536 | tf_op jit(solution)/shard_map/prepare_force/pallas_call | solution.py:305
  39.8 0.0 all-to-all-done.1.terms_ref
  39.8 3.2 %finish_force.1 = (f32[3,16,128]{2,1,0:T(8,128)}, f32[32,128]{1,0:T(8,128)S(1)}) custom-call(s32[2,24]{1,0:T(2,128)S(1)} %bitcast.15, s32[1,24]{1,0:T(1,128)S(1)} %bitcast.18, f32[14,16,128]{2,1,0:T(8,128)S(1)} %get-tuple-element.17.own_ref, f32[16,8,128]{2,1,0:T(8,128)S(1)} %get-tuple-element.21.centred_ref, f32[16,128]{1,0:T(8,128)S(1)} %get-tuple-element.22.term_ref, ...), custom_call_target="tpu_custom_call" | custom-call | flops 6291456 | bytes 65536 | tf_op jit(solution)/shard_map/finish_force/pallas_call | solution.py:353
  43.0 12.9 %all_to_all.19 = f32[32,1,128]{2,1,0:T(1,128)S(1)} all-to-all(f32[32,1,128]{2,1,0:T(1,128)S(1)} %bitcast.12), channel_id=1, replica_groups=mesh['grp'=2,'chip'=8,'core'=2] {'grp','chip','core'}, dimensions={0} | all-to-all | bytes 32768 | tf_op jit(solution)/shard_map/all_to_all | solution.py:363
  55.9 0.6 %reduce_min.9 = f32[]{:T(128)} reduce(f32[32,1,128]{2,1,0:T(1,128)S(1)} %all_to_all.19, f32[]{:T(128)} %constant.0.clone.1), dimensions={0,1,2}, to_apply=%region_0.0 | reduce | flops 4095 | bytes 16392 | tf_op jit(solution)/shard_map/reduce_min | solution.py:364
  (2 shorter events, 0.0 us)
Async XLA Ops:
  0.6 10.4 %copy-start.1 = (f32[16,128]{1,0:T(8,128)S(1)}, f32[16,128]{1,0:T(8,128)}, u32[]{:S(2)}) copy-start(f32[16,128]{1,0:T(8,128)} %h_hbm.1) | copy-start | bytes 24580
  0.6 10.3 %copy-start.2 = (f32[16,128]{1,0:T(8,128)S(1)}, f32[16,128]{1,0:T(8,128)}, u32[]{:S(2)}) copy-start(f32[16,128]{1,0:T(8,128)} %mass_hbm.1) | copy-start | bytes 24580
  0.7 10.3 %copy-start = (f32[16,3,128]{2,0,1:T(8,128)S(1)}, f32[16,3,128]{2,0,1:T(8,128)}, u32[]{:S(2)}) copy-start(f32[16,3,128]{2,0,1:T(8,128)} %param.9) | copy-start | bytes 73732
  0.7 10.3 %copy-start.8 = (s32[16,2]{0,1:T(2,128)S(1)}, s32[16,2]{0,1:T(2,128)}, u32[]{:S(2)}) copy-start(s32[16,2]{0,1:T(2,128)} %param.15) | copy-start | bytes 388
  0.7 10.3 %copy-start.6 = (s32[16,128]{1,0:T(8,128)S(1)}, s32[16,128]{1,0:T(8,128)}, u32[]{:S(2)}) copy-start(s32[16,128]{1,0:T(8,128)} %active_hbm.1) | copy-start | bytes 24580
  0.7 10.3 %copy-start.5 = (f32[16,128]{1,0:T(8,128)S(1)}, f32[16,128]{1,0:T(8,128)}, u32[]{:S(2)}) copy-start(f32[16,128]{1,0:T(8,128)} %old_hbm.1) | copy-start | bytes 24580
  0.7 10.3 %copy-start.4 = (f32[16,128]{1,0:T(8,128)S(1)}, f32[16,128]{1,0:T(8,128)}, u32[]{:S(2)}) copy-start(f32[16,128]{1,0:T(8,128)} %energy_hbm.1) | copy-start | bytes 24580
  0.7 22.2 %copy-start.7 = (s32[24,1]{0,1:T(1,128)S(1)}, s32[24,1]{0,1:T(1,128)}, u32[]{:S(2)}) copy-start(s32[24,1]{0,1:T(1,128)} %param.17) | copy-start | bytes 292
  0.7 22.2 %copy-start.3 = (s32[24,2]{0,1:T(2,128)S(1)}, s32[24,2]{0,1:T(2,128)}, u32[]{:S(2)}) copy-start(s32[24,2]{0,1:T(2,128)} %param.16) | copy-start | bytes 580
  3.7 17.6 %all-to-all-start = ((f32[8,80,128]{2,1,0:T(8,128)}), f32[8,80,128]{2,1,0:T(8,128)S(1)}, u32[]{:S(2)}, u32[]{:S(2)}) async-start(f32[8,80,128]{2,1,0:T(8,128)} %pad_maximum_fusion), calls=%async_computation | async-start | bytes 655360 | tf_op jit(solution)/shard_map/all_to_all | solution.py:146
  21.3 1.6 %collective-permute-start = (f32[8,80,128]{2,1,0:T(8,128)S(1)}, f32[8,80,128]{2,1,0:T(8,128)S(1)}, u32[]{:S(2)}, u32[]{:S(2)}) collective-permute-start(f32[8,80,128]{2,1,0:T(8,128)S(1)} %all-to-all-done.near_ref), channel_id=1, source_target_pairs={{0,1},{1,0},{2,3},{3,2},{4,5},{5,4},{6,7},{7,6},{8,9},{9,8},{10,11... | collective-permute-start | bytes 983048 | tf_op jit(solution)/shard_map/ppermute | solution.py:211
  27.8 12.0 %all-to-all-start.1 = ((f32[16,16,128]{2,1,0:T(8,128)}), f32[16,16,128]{2,1,0:T(8,128)S(1)}, u32[]{:S(2)}, u32[]{:S(2)}) async-start(f32[16,16,128]{2,1,0:T(8,128)} %get-tuple-element.23), calls=%async_computation.1 | async-start | bytes 262144 | tf_op jit(solution)/shard_map/all_to_all | solution.py:265

commit v4 on v3

--- a/solution.py
+++ b/solution.py
@@ -16,10 +16,25 @@
 X, MASS, H, INVERSE, SCALE, ORIGIN, ENERGY, OLD, ACTIVE, SUM, TABLE = 0, 3, 4, 5, 6, 7, 10, 11, 12, 13, 14
 
 
+def split(item):
+    first = item.astype(jnp.bfloat16).astype(jnp.float32)
+    rest = item - first
+    second = rest.astype(jnp.bfloat16).astype(jnp.float32)
+    return first, second, rest - second
+
+
 def product(a, b, dims):
-    return lax.dot_general(
-        a, b, (dims, ((), ())), precision=lax.Precision.HIGHEST, preferred_element_type=jnp.float32
-    )
+    return lax.dot_general(a, b, (dims, ((), ())), preferred_element_type=jnp.float32)
+
+
+def left_terms(item):
+    first, second, third = split(item)
+    return jnp.concatenate([first, first, second, first, third, second], axis=0).astype(jnp.bfloat16)
+
+
+def right_terms(item):
+    first, second, third = split(item)
+    return jnp.concatenate([first, second, first, third, first, second], axis=0).astype(jnp.bfloat16)
 
 
 def turn(rows):
@@ -33,7 +48,7 @@
     norm = place[0] * place[0] + place[1] * place[1] + place[2] * place[2]
     zero = jnp.zeros_like(norm)
     left = jnp.concatenate(place + [norm, jnp.ones_like(norm), zero, zero, zero], axis=0)
-    square = jnp.maximum(product(left, right, ((0,), (0,))), TINY)
+    square = jnp.maximum(product(left_terms(left), right, ((0,), (0,))), TINY)
     inverse = lax.rsqrt(square)
     return square * inverse, inverse
 
@@ -70,9 +85,15 @@
 def force(weights, rows, far_term, own_term, own_place):
     item = lax.broadcasted_iota(jnp.int32, rows.shape, 0)
     rows = jnp.where(item < 4, rows, rows * far_term)
-    sums = product(rows, weights, ((1,), (0,)))
+    rows = jnp.concatenate(split(rows), axis=0).astype(jnp.bfloat16)
+    sums = product(jnp.concatenate([rows, rows, rows], axis=1), weights, ((1,), (0,)))
+    sums = sums[:8] + sums[8:16] + sums[16:]
     sums = own_term * sums[:4] + sums[4:]
     return own_place[:4] * sums[:1] - sums
+
+
+def stack(weights):
+    return jnp.concatenate([part.astype(jnp.bfloat16) for part in split(weights)], axis=0)
 
 
 def slope_scale(h):
@@ -80,8 +101,8 @@
     return (3.0 * NORM) / (square * square)
 
 
-def grouped(count, body):
-    step = math.gcd(GROUP, count)
+def grouped(count, body, group=GROUP):
+    step = math.gcd(group, count)
 
     def run(group, carry):
         for k in range(step):
@@ -136,13 +157,22 @@
         pair_table, leaf_table = pltpu.SMEM((2, pairs), s32), pltpu.SMEM((2, exports), s32)
         route_table = pltpu.SMEM((1, exports), s32)
 
-        outgoing = jnp.concatenate(
-            [
-                jnp.broadcast_to(item[None], (chips,) + item.shape)
-                for item in (place.reshape(3 * leaves, width), smoothing, mass)
-            ],
-            axis=1,
-        )
+        def copy_out(place_ref, h_ref, mass_ref, out_ref, sems):
+            copies = []
+            for k in range(chips):
+                to = out_ref.at[k]
+                copies += [(place_ref, to.at[pl.ds(0, 3)]), (h_ref, to.at[3]), (mass_ref, to.at[4])]
+            fetch(sems, *copies)
+
+        outgoing = pl.pallas_call(
+            copy_out,
+            out_shape=shape(chips, 5, leaves, width),
+            in_specs=[hbm] * 3,
+            out_specs=hbm,
+            scratch_shapes=[pltpu.SemaphoreType.DMA((3 * chips,))],
+            compiler_params=pltpu.CompilerParams(vmem_limit_bytes=MIB),
+            name="copy_out",
+        )(place, smoothing, mass).reshape(chips, 5 * leaves, width)
         near = lax.all_to_all(outgoing, "chip", split_axis=0, concat_axis=0, tiled=True)
 
         def row(own_ref, item, leaf):
@@ -182,10 +212,10 @@
             zero, one = jnp.zeros_like(h), jnp.ones_like(h)
             rights = [-2.0 * item for item in centred] + [one, norm, zero, zero, zero]
             places = [zero] + centred + [zero] * 4
-            for k in range(8):
-                for leaf in range(leaves):
-                    right_ref[leaf, k : k + 1, :] = rights[k][leaf : leaf + 1]
-                    centred_ref[leaf, k : k + 1, :] = places[k][leaf : leaf + 1]
+            for leaf in range(leaves):
+                at = slice(leaf, leaf + 1)
+                right_ref[leaf] = right_terms(jnp.concatenate([item[at] for item in rights], axis=0))
+                centred_ref[leaf] = jnp.concatenate([item[at] for item in places], axis=0)
 
             def tile(e):
                 mine, other = pair_ref[0, e], pair_ref[1, e]
@@ -201,7 +231,11 @@
         own, right, centred = call(
             local_density,
             "local_density",
-            (shape(TABLE, leaves, width), shape(leaves, 8, width), shape(leaves, 8, width)),
+            (
+                shape(TABLE, leaves, width),
+                jax.ShapeDtypeStruct((leaves, 48, width), jnp.bfloat16),
+                shape(leaves, 8, width),
+            ),
             [hbm] * 7,
             [pair_table, pltpu.VMEM((leaves, width), s32), pltpu.SemaphoreType.DMA((7,))],
             pairs * tile_flops * 30,
@@ -284,7 +318,9 @@
             def local_tile(e):
                 mine, other = pair_ref[0, e], pair_ref[1, e]
                 spot = local_place(own_ref, mine, other)
-                weights = weigh(mine, spot, row(own_ref, INVERSE, other), row(own_ref, SCALE, other))
+                weights = stack(
+                    weigh(mine, spot, row(own_ref, INVERSE, other), row(own_ref, SCALE, other))
+                )
                 rows = moments(row(own_ref, MASS, other), spot)
                 far_term, own_term = term_ref[pl.ds(other, 1), :], term_ref[pl.ds(mine, 1), :]
                 sum_ref[mine] = sum_ref[mine] + force(
@@ -295,17 +331,21 @@
                 mine, spot, (h, far_mass) = export(
                     leaf_ref, route_ref, near_ref, peer_ref, own_ref, e, (3, 4)
                 )
-                weight_ref[e] = weigh(mine, spot, 1.0 / h, slope_scale(h))
+                weight_ref[e] = stack(weigh(mine, spot, 1.0 / h, slope_scale(h)))
                 moment_ref[e] = moments(far_mass, spot)
 
             grouped(pairs, local_tile)
             grouped(exports, remote_tile)
 
-        stash_mib = 2 * exports * width * (width + 8) * 4 // MIB
+        stash_mib = 2 * exports * width * (6 * width + 32) // MIB
         partial, weights, rows = call(
             prepare,
             "prepare_force",
-            (shape(leaves, 4, width), shape(exports, width, width), shape(exports, 8, width)),
+            (
+                shape(leaves, 4, width),
+                jax.ShapeDtypeStruct((exports, 3 * width, width), jnp.bfloat16),
+                shape(exports, 8, width),
+            ),
             [hbm] * 3 + [vmem] * 6,
             [pair_table, leaf_table, route_table, pltpu.SemaphoreType.DMA((3,))],
             (pairs + exports) * tile_flops * 60,

time: 57 us -> 65.7 us (1.15)
  local copies, waits for them, and re-layouts: 2.24 us -> 15.2 us
  waiting for transfers between devices: 5.49 us -> 2.44 us
  Pallas kernels: 22.7 us -> 20.1 us
  starting transfers between devices: 11 us -> 12.7 us
  other arithmetic: 1.37 us -> 0.63 us
    unnamed x18 -> x44, local copies, waits for them, and re-layouts: 0.04 us -> 15.2 us
    all_to_all x1, waiting for transfers between devices: 3.86 us -> 0.81 us  [body(): lax.all_to_all(outgoing, 'chip', split_axis=0, concat_axis=0, tiled=True)]
    broadcast_in_dim x3 -> x0, local copies, waits for them, and re-layouts: 2.2 us -> none  [body(): jnp.broadcast_to(item[None], (chips,) + item.shape)]
    all_to_all x1, starting transfers between devices: 3.71 us -> 5.37 us  [body(): lax.all_to_all(outgoing, ('chip', 'core'), split_axis=0, concat_axis=0, t...]
    pallas_call x1, Pallas kernels: 4.84 us -> 3.95 us  [body(): call(remote_density, 'remote_density', (shape(leaves, width), shape(leave...]
    pallas_call x2 -> x3, Pallas kernels: 14.7 us -> 13.8 us  [the longest x1 8.26 us: body(): call(prepare, 'prepare_force', (shape(leaves, 4, width), jax.ShapeDtypeSt...]
    pallas_call x1, Pallas kernels: 3.19 us -> 2.41 us  [body(): call(finish, 'finish_force', (shape(3, leaves, width), shape(members, wid...]
    concatenate x1 -> x0, other arithmetic: 0.74 us -> none  [body(): jnp.concatenate([jnp.broadcast_to(item[None], (chips,) + item.shape) for...]
  transfers between devices with their start and end apart: 3 -> 3, of which waited for: 2 -> 2; matrix products, arithmetic and copies ran while one was open for 0% -> 0% of each run, Pallas kernels for 26% -> 20%
where the time goes in v4:
time: 65.7 us; the launch traced here: 64.7 us
  Pallas kernels  20.1 us (31%)
  local copies, waits for them, and re-layouts  15.2 us (23%)
  blocking collectives  12.9 us (20%)
  starting transfers between devices  12.7 us (19%)
  waiting for transfers between devices  2.44 us (4%)
  between operations  0.74 us (1%)
    unnamed x44, local copies, waits for them, and re-layouts  15.2 us
    all_to_all x1, blocking collectives, body(): lax.all_to_all(least, everyone, split_axis=0, concat_axis=0, tiled=True)  12.9 us
    pallas_call x1, Pallas kernels, body(): call(prepare, 'prepare_force', (shape(leaves, 4, width), jax.ShapeDtypeSt...  8.26 us
    all_to_all x1, starting transfers between devices, body(): lax.all_to_all(outgoing, 'chip', split_axis=0, concat_axis=0, tiled=True)  7.32 us
    all_to_all x1, starting transfers between devices, body(): lax.all_to_all(outgoing, ('chip', 'core'), split_axis=0, concat_axis=0, t...  5.37 us
    pallas_call x1, Pallas kernels, body(): call(local_density, 'local_density', (shape(TABLE, leaves, width), jax.Sh...  4.58 us
    pallas_call x1, Pallas kernels, body(): call(remote_density, 'remote_density', (shape(leaves, width), shape(leave...  3.95 us
    pallas_call x1, Pallas kernels, body(): call(finish, 'finish_force', (shape(3, leaves, width), shape(members, wid...  2.41 us
  transfers between devices with their start and end apart: 3, of which 2 were waited for; matrix products, arithmetic and copies ran while one was open for 0% of the time, Pallas kernels for 20%

profile of v4, /device:TPU:0, one launch (start us, length us, event | category | flops | bytes accessed | tf_op | source)
XLA Modules:
  0.0 64.7 jit_solution(16649270974349584505)
XLA Ops:
  0.6 0.7 %copy-done.2 = f32[16,3,128]{2,0,1:T(8,128)S(1)} copy-done((f32[16,3,128]{2,0,1:T(8,128)S(1)}, f32[16,3,128]{2,0,1:T(8,128)}, u32[]{:S(2)}) %copy-start.2) | copy-done | bytes 24600
  1.4 0.7 %copy-done.4 = f32[16,128]{1,0:T(8,128)S(1)} copy-done((f32[16,128]{1,0:T(8,128)S(1)}, f32[16,128]{1,0:T(8,128)}, u32[]{:S(2)}) %copy-start.4) | copy-done | bytes 8216
  2.1 0.7 %copy-done.6 = f32[16,128]{1,0:T(8,128)S(1)} copy-done((f32[16,128]{1,0:T(8,128)S(1)}, f32[16,128]{1,0:T(8,128)}, u32[]{:S(2)}) %copy-start.6) | copy-done | bytes 8216
  2.8 0.9 %copy_out.1 = f32[8,5,16,128]{3,2,1,0:T(8,128)} custom-call(f32[3,16,128]{2,1,0:T(8,128)S(1)} %bitcast.9, f32[16,128]{1,0:T(8,128)S(1)} %copy-done.4, f32[16,128]{1,0:T(8,128)S(1)} %copy-done.6), custom_call_target="tpu_custom_call" | custom-call | tf_op jit(solution)/shard_map/copy_out/pallas_call | solution.py:167
  3.7 7.3 %all-to-all-start = ((f32[8,80,128]{2,1,0:T(8,128)}), f32[8,80,128]{2,1,0:T(8,128)S(1)}, u32[]{:S(2)}, u32[]{:S(2)}) async-start(f32[8,80,128]{2,1,0:T(8,128)} %bitcast.3), calls=%async_computation | async-start | bytes 655360 | tf_op jit(solution)/shard_map/all_to_all | solution.py:176
  11.0 0.7 %copy-done.3 = f32[16,3,128]{2,0,1:T(8,128)S(1)} copy-done((f32[16,3,128]{2,0,1:T(8,128)S(1)}, f32[16,3,128]{2,0,1:T(8,128)}, u32[]{:S(2)}) %copy-start.3) | copy-done | bytes 24600
  11.8 0.7 %copy-done.5 = f32[16,128]{1,0:T(8,128)S(1)} copy-done((f32[16,128]{1,0:T(8,128)S(1)}, f32[16,128]{1,0:T(8,128)}, u32[]{:S(2)}) %copy-start.5) | copy-done | bytes 8216
  12.5 0.7 %copy-done.7 = f32[16,128]{1,0:T(8,128)S(1)} copy-done((f32[16,128]{1,0:T(8,128)S(1)}, f32[16,128]{1,0:T(8,128)}, u32[]{:S(2)}) %copy-start.7) | copy-done | bytes 8216
  13.2 0.7 %copy-done.14 = f32[16,128]{1,0:T(8,128)S(1)} copy-done((f32[16,128]{1,0:T(8,128)S(1)}, f32[16,128]{1,0:T(8,128)}, u32[]{:S(2)}) %copy-start.14) | copy-done | bytes 8216
  13.9 0.7 %copy-done.15 = f32[16,128]{1,0:T(8,128)S(1)} copy-done((f32[16,128]{1,0:T(8,128)S(1)}, f32[16,128]{1,0:T(8,128)}, u32[]{:S(2)}) %copy-start.15) | copy-done | bytes 8216
  14.6 0.7 %copy-done.16 = s32[16,128]{1,0:T(8,128)S(1)} copy-done((s32[16,128]{1,0:T(8,128)S(1)}, s32[16,128]{1,0:T(8,128)}, u32[]{:S(2)}) %copy-start.16) | copy-done | bytes 8216
  15.3 0.7 %copy-done.20 = s32[16,2]{0,1:T(2,128)S(1)} copy-done((s32[16,2]{0,1:T(2,128)S(1)}, s32[16,2]{0,1:T(2,128)}, u32[]{:S(2)}) %copy-start.20) | copy-done | bytes 152
  15.9 4.6 %local_density.1 = (f32[14,16,128]{2,1,0:T(8,128)S(1)}, bf16[16,48,128]{2,1,0:T(8,128)(2,1)S(1)}, f32[16,8,128]{2,1,0:T(8,128)S(1)}) custom-call(s32[2,16]{1,0:T(2,128)S(1)} %bitcast.18, f32[3,16,128]{2,1,0:T(8,128)S(1)} %bitcast.10, f32[16,128]{1,0:T(8,128)S(1)} %copy-done.5, f32[16,128]{1,0:T(8,128)S(1)} %copy-done.7, f32[16,128]{1,0:T(8,128)S(1)} %copy-done.14, ...), custom_call_target="tpu_custom_call" | custom-call | flops 7864320 | bytes 65536 | tf_op jit(solution)/shard_map/local_density/pallas_call | solution.py:231
  20.5 0.8 %all-to-all-done.near_ref = f32[8,80,128]{2,1,0:T(8,128)S(1)} async-done(((f32[8,80,128]{2,1,0:T(8,128)}), f32[8,80,128]{2,1,0:T(8,128)S(1)}, u32[]{:S(2)}, u32[]{:S(2)}) %all-to-all-start) | async-done | bytes 327712 | tf_op jit(solution)/shard_map/all_to_all | solution.py:176
  21.3 1.6 %collective-permute-done.peer_ref = f32[8,80,128]{2,1,0:T(8,128)S(1)} collective-permute-done((f32[8,80,128]{2,1,0:T(8,128)S(1)}, f32[8,80,128]{2,1,0:T(8,128)S(1)}, u32[]{:S(2)}, u32[]{:S(2)}) %collective-permute-start) | collective-permute-done | bytes 327712 | tf_op jit(solution)/shard_map/ppermute | solution.py:245
  23.0 0.7 %copy-done.11 = s32[24,2]{0,1:T(2,128)S(1)} copy-done((s32[24,2]{0,1:T(2,128)S(1)}, s32[24,2]{0,1:T(2,128)}, u32[]{:S(2)}) %copy-start.11) | copy-done | bytes 216
  23.7 0.7 %copy-done.17 = s32[24,1]{0,1:T(1,128)S(1)} copy-done((s32[24,1]{0,1:T(1,128)S(1)}, s32[24,1]{0,1:T(1,128)}, u32[]{:S(2)}) %copy-start.17) | copy-done | bytes 120
  24.3 4.0 %remote_density.1 = (f32[16,128]{1,0:T(8,128)}, f32[16,128]{1,0:T(8,128)S(1)}, f32[16,16,128]{2,1,0:T(8,128)}) custom-call(s32[2,24]{1,0:T(2,128)S(1)} %bitcast.12, s32[1,24]{1,0:T(1,128)S(1)} %bitcast.15, f32[14,16,128]{2,1,0:T(8,128)S(1)} %get-tuple-element.17.own_ref, bf16[16,48,128]{2,1,0:T(8,128)(2,1)S(1)} %get-tuple-element.18.right_ref, ...), custom_call_target="tpu_custom_call" | custom-call | flops 11796480 | bytes 65536 | tf_op jit(solution)/shard_map/remote_density/pallas_call | solution.py:290
  28.9 5.4 %all-to-all-start.1 = ((f32[16,16,128]{2,1,0:T(8,128)}), f32[16,16,128]{2,1,0:T(8,128)S(1)}, u32[]{:S(2)}, u32[]{:S(2)}) async-start(f32[16,16,128]{2,1,0:T(8,128)} %get-tuple-element.23), calls=%async_computation.1 | async-start | bytes 262144 | tf_op jit(solution)/shard_map/all_to_all | solution.py:299
  34.3 0.7 %copy-done.9 = f32[16,128]{1,0:T(8,128)S(1)} copy-done((f32[16,128]{1,0:T(8,128)S(1)}, f32[16,128]{1,0:T(8,128)}, u32[]{:S(2)}) %copy-start.9) | copy-done | bytes 8216
  34.9 0.7 %copy-done.12 = s32[24,2]{0,1:T(2,128)S(1)} copy-done((s32[24,2]{0,1:T(2,128)S(1)}, s32[24,2]{0,1:T(2,128)}, u32[]{:S(2)}) %copy-start.12) | copy-done | bytes 216
  35.6 0.7 %copy-done.18 = s32[24,1]{0,1:T(1,128)S(1)} copy-done((s32[24,1]{0,1:T(1,128)S(1)}, s32[24,1]{0,1:T(1,128)}, u32[]{:S(2)}) %copy-start.18) | copy-done | bytes 120
  36.3 0.7 %copy-done.21 = s32[16,2]{0,1:T(2,128)S(1)} copy-done((s32[16,2]{0,1:T(2,128)S(1)}, s32[16,2]{0,1:T(2,128)}, u32[]{:S(2)}) %copy-start.21) | copy-done | bytes 152
  37.0 8.3 %prepare_force.1 = (f32[16,4,128]{2,1,0:T(4,128)S(1)}, bf16[24,384,128]{2,1,0:T(8,128)(2,1)S(1)}, f32[24,8,128]{2,1,0:T(8,128)S(1)}) custom-call(s32[2,16]{1,0:T(2,128)S(1)} %bitcast.19, s32[2,24]{1,0:T(2,128)S(1)} %bitcast.13, s32[1,24]{1,0:T(1,128)S(1)} %bitcast.16, f32[14,16,128]{2,1,0:T(8,128)S(1)} %get-tuple-element.17.own_ref, ...), custom_call_target="tpu_custom_call" | custom-call | flops 39321600 | bytes 65536 | tf_op jit(solution)/shard_map/prepare_force/pallas_call | solution.py:341
  45.2 0.6 copy-done
  45.9 0.9 %copy-done.1 = f32[24,8,128]{2,1,0:T(8,128)S(1)} copy-done((f32[24,8,128]{2,1,0:T(8,128)S(1)}, f32[24,8,128]{2,1,0:T(8,128)}, u32[]{:S(2)}) %copy-start.1) | copy-done | bytes 98328
  46.8 0.7 %copy-done.10 = f32[16,128]{1,0:T(8,128)S(1)} copy-done((f32[16,128]{1,0:T(8,128)S(1)}, f32[16,128]{1,0:T(8,128)}, u32[]{:S(2)}) %copy-start.10) | copy-done | bytes 8216
  47.5 0.7 %copy-done.13 = s32[24,2]{0,1:T(2,128)S(1)} copy-done((s32[24,2]{0,1:T(2,128)S(1)}, s32[24,2]{0,1:T(2,128)}, u32[]{:S(2)}) %copy-start.13) | copy-done | bytes 216
  48.1 0.7 %copy-done.19 = s32[24,1]{0,1:T(1,128)S(1)} copy-done((s32[24,1]{0,1:T(1,128)S(1)}, s32[24,1]{0,1:T(1,128)}, u32[]{:S(2)}) %copy-start.19) | copy-done | bytes 120
  48.8 2.4 %finish_force.1 = (f32[3,16,128]{2,1,0:T(8,128)}, f32[32,128]{1,0:T(8,128)S(1)}) custom-call(s32[2,24]{1,0:T(2,128)S(1)} %bitcast.14, s32[1,24]{1,0:T(1,128)S(1)} %bitcast.17, f32[14,16,128]{2,1,0:T(8,128)S(1)} %get-tuple-element.17.own_ref, f32[16,8,128]{2,1,0:T(8,128)S(1)} %get-tuple-element.21.centred_ref, f32[16,128]{1,0:T(8,128)S(1)} %copy-done.10, ...), custom_call_target="tpu_custom_call" | custom-call | flops 6291456 | bytes 65536 | tf_op jit(solution)/shard_map/finish_force/pallas_call | solution.py:393
  51.2 12.9 %all_to_all.19 = f32[32,1,128]{2,1,0:T(1,128)S(1)} all-to-all(f32[32,1,128]{2,1,0:T(1,128)S(1)} %bitcast.11), channel_id=1, replica_groups=mesh['grp'=2,'chip'=8,'core'=2] {'grp','chip','core'}, dimensions={0} | all-to-all | bytes 32768 | tf_op jit(solution)/shard_map/all_to_all | solution.py:403
  64.1 0.6 reduce_min.9
  (25 shorter events, 0.6 us)
Async XLA Ops:
  0.6 0.7 %copy-start.2 = (f32[16,3,128]{2,0,1:T(8,128)S(1)}, f32[16,3,128]{2,0,1:T(8,128)}, u32[]{:S(2)}) copy-start(f32[16,3,128]{2,0,1:T(8,128)} %param.9) | copy-start | bytes 73732
  1.4 0.7 %copy-start.4 = (f32[16,128]{1,0:T(8,128)S(1)}, f32[16,128]{1,0:T(8,128)}, u32[]{:S(2)}) copy-start(f32[16,128]{1,0:T(8,128)} %h_hbm.1) | copy-start | bytes 24580
  2.1 0.7 %copy-start.6 = (f32[16,128]{1,0:T(8,128)S(1)}, f32[16,128]{1,0:T(8,128)}, u32[]{:S(2)}) copy-start(f32[16,128]{1,0:T(8,128)} %mass_hbm.1) | copy-start | bytes 24580
  3.7 17.6 %all-to-all-start = ((f32[8,80,128]{2,1,0:T(8,128)}), f32[8,80,128]{2,1,0:T(8,128)S(1)}, u32[]{:S(2)}, u32[]{:S(2)}) async-start(f32[8,80,128]{2,1,0:T(8,128)} %bitcast.3), calls=%async_computation | async-start | bytes 655360 | tf_op jit(solution)/shard_map/all_to_all | solution.py:176
  11.0 0.7 %copy-start.3 = (f32[16,3,128]{2,0,1:T(8,128)S(1)}, f32[16,3,128]{2,0,1:T(8,128)}, u32[]{:S(2)}) copy-start(f32[16,3,128]{2,0,1:T(8,128)} %param.9) | copy-start | bytes 73732
  11.8 0.7 %copy-start.5 = (f32[16,128]{1,0:T(8,128)S(1)}, f32[16,128]{1,0:T(8,128)}, u32[]{:S(2)}) copy-start(f32[16,128]{1,0:T(8,128)} %h_hbm.1) | copy-start | bytes 24580
  12.5 0.7 %copy-start.7 = (f32[16,128]{1,0:T(8,128)S(1)}, f32[16,128]{1,0:T(8,128)}, u32[]{:S(2)}) copy-start(f32[16,128]{1,0:T(8,128)} %mass_hbm.1) | copy-start | bytes 24580
  13.2 0.7 %copy-start.14 = (f32[16,128]{1,0:T(8,128)S(1)}, f32[16,128]{1,0:T(8,128)}, u32[]{:S(2)}) copy-start(f32[16,128]{1,0:T(8,128)} %energy_hbm.1) | copy-start | bytes 24580
  13.9 0.7 %copy-start.15 = (f32[16,128]{1,0:T(8,128)S(1)}, f32[16,128]{1,0:T(8,128)}, u32[]{:S(2)}) copy-start(f32[16,128]{1,0:T(8,128)} %old_hbm.1) | copy-start | bytes 24580
  14.6 0.7 %copy-start.16 = (s32[16,128]{1,0:T(8,128)S(1)}, s32[16,128]{1,0:T(8,128)}, u32[]{:S(2)}) copy-start(s32[16,128]{1,0:T(8,128)} %active_hbm.1) | copy-start | bytes 24580
  15.3 0.7 %copy-start.20 = (s32[16,2]{0,1:T(2,128)S(1)}, s32[16,2]{0,1:T(2,128)}, u32[]{:S(2)}) copy-start(s32[16,2]{0,1:T(2,128)} %param.15) | copy-start | bytes 388
  21.3 1.6 %collective-permute-start = (f32[8,80,128]{2,1,0:T(8,128)S(1)}, f32[8,80,128]{2,1,0:T(8,128)S(1)}, u32[]{:S(2)}, u32[]{:S(2)}) collective-permute-start(f32[8,80,128]{2,1,0:T(8,128)S(1)} %all-to-all-done.near_ref), channel_id=1, source_target_pairs={{0,1},{1,0},{2,3},{3,2},{4,5},{5,4},{6,7},{7,6},{8,9},{9,8},{10,11... | collective-permute-start | bytes 983048 | tf_op jit(solution)/shard_map/ppermute | solution.py:245
  23.0 0.7 %copy-start.11 = (s32[24,2]{0,1:T(2,128)S(1)}, s32[24,2]{0,1:T(2,128)}, u32[]{:S(2)}) copy-start(s32[24,2]{0,1:T(2,128)} %param.16) | copy-start | bytes 580
  23.6 0.7 %copy-start.17 = (s32[24,1]{0,1:T(1,128)S(1)}, s32[24,1]{0,1:T(1,128)}, u32[]{:S(2)}) copy-start(s32[24,1]{0,1:T(1,128)} %param.17) | copy-start | bytes 292
  28.3 0.6 copy-start.8
  28.9 17.0 %all-to-all-start.1 = ((f32[16,16,128]{2,1,0:T(8,128)}), f32[16,16,128]{2,1,0:T(8,128)S(1)}, u32[]{:S(2)}, u32[]{:S(2)}) async-start(f32[16,16,128]{2,1,0:T(8,128)} %get-tuple-element.23), calls=%async_computation.1 | async-start | bytes 262144 | tf_op jit(solution)/shard_map/all_to_all | solution.py:299
  34.2 0.7 %copy-start.9 = (f32[16,128]{1,0:T(8,128)S(1)}, f32[16,128]{1,0:T(8,128)}, u32[]{:S(2)}) copy-start(f32[16,128]{1,0:T(8,128)} %copy-done.8) | copy-start | bytes 24580
  34.9 0.7 %copy-start.12 = (s32[24,2]{0,1:T(2,128)S(1)}, s32[24,2]{0,1:T(2,128)}, u32[]{:S(2)}) copy-start(s32[24,2]{0,1:T(2,128)} %param.16) | copy-start | bytes 580
  35.6 0.7 %copy-start.18 = (s32[24,1]{0,1:T(1,128)S(1)}, s32[24,1]{0,1:T(1,128)}, u32[]{:S(2)}) copy-start(s32[24,1]{0,1:T(1,128)} %param.17) | copy-start | bytes 292
  36.3 0.7 %copy-start.21 = (s32[16,2]{0,1:T(2,128)S(1)}, s32[16,2]{0,1:T(2,128)}, u32[]{:S(2)}) copy-start(s32[16,2]{0,1:T(2,128)} %param.15) | copy-start | bytes 388
  45.2 0.6 copy-start
  45.9 0.9 %copy-start.1 = (f32[24,8,128]{2,1,0:T(8,128)S(1)}, f32[24,8,128]{2,1,0:T(8,128)}, u32[]{:S(2)}) copy-start(f32[24,8,128]{2,1,0:T(8,128)} %copy-done) | copy-start | bytes 294916
  46.8 0.7 %copy-start.10 = (f32[16,128]{1,0:T(8,128)S(1)}, f32[16,128]{1,0:T(8,128)}, u32[]{:S(2)}) copy-start(f32[16,128]{1,0:T(8,128)} %copy-done.8) | copy-start | bytes 24580
  47.5 0.7 %copy-start.13 = (s32[24,2]{0,1:T(2,128)S(1)}, s32[24,2]{0,1:T(2,128)}, u32[]{:S(2)}) copy-start(s32[24,2]{0,1:T(2,128)} %param.16) | copy-start | bytes 580
  48.1 0.7 %copy-start.19 = (s32[24,1]{0,1:T(1,128)S(1)}, s32[24,1]{0,1:T(1,128)}, u32[]{:S(2)}) copy-start(s32[24,1]{0,1:T(1,128)} %param.17) | copy-start | bytes 292

commit v5 on v4

--- a/solution.py
+++ b/solution.py
@@ -9,7 +9,7 @@
 
 ADIABATIC = 5.0 / 3.0
 COURANT = 0.3
-GROUP = 4
+GROUP = 24
 TINY = 1e-30
 NORM = 8.0 / math.pi
 MIB = 1 << 20
@@ -102,7 +102,7 @@
 
 
 def grouped(count, body, group=GROUP):
-    step = math.gcd(group, count)
+    step = max(d for d in range(1, min(group, count) + 1) if count % d == 0)
 
     def run(group, carry):
         for k in range(step):
@@ -152,10 +152,17 @@
         def shape(*sizes):
             return jax.ShapeDtypeStruct(sizes, f32)
 
-        place = positions.transpose(1, 0, 2)
-        pair_list, export_leaves, export_route = pair_list.T, export_leaves.T, export_route.T
+        def kept(item):
+            return pltpu.with_memory_space_constraint(item, pltpu.HBM)
+
+        place = kept(positions.transpose(1, 0, 2))
+        smoothing, energy, mass = kept(smoothing), kept(energy), kept(mass)
+        old_density, active = kept(old_density), kept(active)
+        pair_list, export_leaves = kept(pair_list.T), kept(export_leaves.T)
+        export_route = kept(export_route.T)
         pair_table, leaf_table = pltpu.SMEM((2, pairs), s32), pltpu.SMEM((2, exports), s32)
         route_table = pltpu.SMEM((1, exports), s32)
+        sheet = pltpu.VMEM((leaves, width), f32)
 
         def copy_out(place_ref, h_ref, mass_ref, out_ref, sems):
             copies = []
@@ -290,19 +297,26 @@
         density, term, outgoing = call(
             remote_density,
             "remote_density",
-            (shape(leaves, width), shape(leaves, width), shape(domains, leaves, width)),
+            (shape(leaves, width), pltpu.HBM((leaves, width), f32), shape(domains, leaves, width)),
             [hbm] * 2 + [vmem] * 4,
-            [pltpu.VMEM((leaves, width), f32), leaf_table, route_table, pltpu.SemaphoreType.DMA((2,))],
+            [sheet, leaf_table, route_table, pltpu.SemaphoreType.DMA((2,))],
             exports * tile_flops * 30,
             6 + wire_mib,
         )(export_leaves, export_route, own, right, near, peer)
+        term = kept(term)
         terms = lax.all_to_all(outgoing, ("chip", "core"), split_axis=0, concat_axis=0, tiled=True)
 
         def prepare(
-            pair_hbm, leaf_hbm, route_hbm, own_ref, right_ref, centred_ref, near_ref, peer_ref,
-            term_ref, sum_ref, weight_ref, moment_ref, pair_ref, leaf_ref, route_ref, sems
+            pair_hbm, leaf_hbm, route_hbm, term_hbm, own_ref, right_ref, centred_ref, near_ref,
+            peer_ref, sum_ref, weight_ref, moment_ref, pair_ref, leaf_ref, route_ref, term_ref, sems
         ):
-            fetch(sems, (pair_hbm, pair_ref), (leaf_hbm, leaf_ref), (route_hbm, route_ref))
+            fetch(
+                sems,
+                (pair_hbm, pair_ref),
+                (leaf_hbm, leaf_ref),
+                (route_hbm, route_ref),
+                (term_hbm, term_ref),
+            )
             sum_ref[...] = jnp.zeros_like(sum_ref)
 
             def weigh(mine, spot, inverse, scale):
@@ -344,19 +358,25 @@
             (
                 shape(leaves, 4, width),
                 jax.ShapeDtypeStruct((exports, 3 * width, width), jnp.bfloat16),
-                shape(exports, 8, width),
+                pltpu.HBM((exports, 8, width), f32),
             ),
-            [hbm] * 3 + [vmem] * 6,
-            [pair_table, leaf_table, route_table, pltpu.SemaphoreType.DMA((3,))],
+            [hbm] * 4 + [vmem] * 5,
+            [pair_table, leaf_table, route_table, sheet, pltpu.SemaphoreType.DMA((4,))],
             (pairs + exports) * tile_flops * 60,
             6 + stash_mib + wire_mib,
-        )(pair_list, export_leaves, export_route, own, right, centred, near, peer, term)
+        )(pair_list, export_leaves, export_route, term, own, right, centred, near, peer)
 
         def finish(
-            leaf_hbm, route_hbm, own_ref, centred_ref, term_ref, terms_ref, partial_ref, weight_ref,
-            moment_ref, accel_ref, least_ref, total, leaf_ref, route_ref, sems
+            leaf_hbm, route_hbm, term_hbm, moment_hbm, own_ref, centred_ref, terms_ref, partial_ref,
+            weight_ref, accel_ref, least_ref, total, leaf_ref, route_ref, term_ref, moment_ref, sems
         ):
-            fetch(sems, (leaf_hbm, leaf_ref), (route_hbm, route_ref))
+            fetch(
+                sems,
+                (leaf_hbm, leaf_ref),
+                (route_hbm, route_ref),
+                (term_hbm, term_ref),
+                (moment_hbm, moment_ref),
+            )
             total[...] = partial_ref[...]
             me = lax.axis_index("chip") * 2 + lax.axis_index("core")
 
@@ -394,11 +414,18 @@
             finish,
             "finish_force",
             (shape(3, leaves, width), shape(members, width)),
-            [hbm] * 2 + [vmem] * 7,
-            [pltpu.VMEM((leaves, 4, width), f32), leaf_table, route_table, pltpu.SemaphoreType.DMA((2,))],
+            [hbm] * 4 + [vmem] * 5,
+            [
+                pltpu.VMEM((leaves, 4, width), f32),
+                leaf_table,
+                route_table,
+                sheet,
+                pltpu.VMEM((exports, 8, width), f32),
+                pltpu.SemaphoreType.DMA((4,)),
+            ],
             exports * tile_flops * 16,
             6 + stash_mib + wire_mib,
-        )(export_leaves, export_route, own, centred, term, terms, partial, weights, rows)
+        )(export_leaves, export_route, term, kept(rows), own, centred, terms, partial, weights)
 
         everywhere = lax.all_to_all(least, everyone, split_axis=0, concat_axis=0, tiled=True)
         return density, accel.transpose(1, 0, 2), jnp.min(everywhere)

time: 65.7 us -> 60.1 us (0.915)
  local copies, waits for them, and re-layouts: 15.2 us -> 0 us
  Pallas kernels: 20.1 us -> 27.2 us
  waiting for transfers between devices: 2.44 us -> 8.8 us
  blocking collectives: 12.9 us -> 11.3 us
  starting transfers between devices: 12.7 us -> 11.1 us
    unnamed x44 -> x0, local copies, waits for them, and re-layouts: 15.2 us -> none
    pallas_call x1, Pallas kernels: 0.95 us -> 11.3 us  [body(): pl.pallas_call(copy_out, out_shape=shape(chips, 5, leaves, width), in_spe...]
    all_to_all x1, waiting for transfers between devices: 0.81 us -> 5.52 us  [body(): lax.all_to_all(outgoing, 'chip', split_axis=0, concat_axis=0, tiled=True)]
    pallas_call x1, Pallas kernels: 8.26 us -> 6.24 us  [body(): call(prepare, 'prepare_force', (shape(leaves, 4, width), jax.ShapeDtypeSt...]
    all_to_all x1, waiting for transfers between devices: 0.01 us -> 1.65 us  [body(): lax.all_to_all(outgoing, ('chip', 'core'), split_axis=0, concat_axis=0, t...]
    all_to_all x1, blocking collectives: 12.9 us -> 11.3 us  [body(): lax.all_to_all(least, everyone, split_axis=0, concat_axis=0, tiled=True)]
    all_to_all x1, starting transfers between devices: 5.37 us -> 3.74 us  [body(): lax.all_to_all(outgoing, ('chip', 'core'), split_axis=0, concat_axis=0, t...]
    pallas_call x1, Pallas kernels: 3.95 us -> 2.86 us  [body(): call(remote_density, 'remote_density', (shape(leaves, width), pltpu.HBM((...]
  transfers between devices with their start and end apart: 3 -> 3, of which waited for: 2 -> 3; matrix products, arithmetic and copies ran while one was open for 0% -> 0% of each run, Pallas kernels for 20% -> 18%
where the time goes in v5:
time: 60.1 us; the launch traced here: 59.7 us
  Pallas kernels  27.2 us (45%)
  blocking collectives  11.3 us (19%)
  starting transfers between devices  11.1 us (18%)
  waiting for transfers between devices  8.8 us (15%)
  between operations  0.68 us (1%)
  other arithmetic  0.63 us (1%)
    all_to_all x1, blocking collectives, body(): lax.all_to_all(least, everyone, split_axis=0, concat_axis=0, tiled=True)  11.3 us
    pallas_call x1, Pallas kernels, body(): pl.pallas_call(copy_out, out_shape=shape(chips, 5, leaves, width), in_spe...  11.3 us
    all_to_all x1, starting transfers between devices, body(): lax.all_to_all(outgoing, 'chip', split_axis=0, concat_axis=0, tiled=True)  7.32 us
    pallas_call x1, Pallas kernels, body(): call(prepare, 'prepare_force', (shape(leaves, 4, width), jax.ShapeDtypeSt...  6.24 us
    all_to_all x1, waiting for transfers between devices, body(): lax.all_to_all(outgoing, 'chip', split_axis=0, concat_axis=0, tiled=True)  5.52 us
    pallas_call x1, Pallas kernels, body(): call(local_density, 'local_density', (shape(TABLE, leaves, width), jax.Sh...  4.77 us
    all_to_all x1, starting transfers between devices, body(): lax.all_to_all(outgoing, ('chip', 'core'), split_axis=0, concat_axis=0, t...  3.74 us
    pallas_call x1, Pallas kernels, body(): call(remote_density, 'remote_density', (shape(leaves, width), pltpu.HBM((...  2.86 us
  transfers between devices with their start and end apart: 3, of which 3 were waited for; matrix products, arithmetic and copies ran while one was open for 0% of the time, Pallas kernels for 18%

profile of v5, /device:TPU:0, one launch (start us, length us, event | category | flops | bytes accessed | tf_op | source)
XLA Modules:
  0.0 59.7 jit_solution(8904068534632510411)
XLA Ops:
  0.6 11.3 %copy_out.1 = f32[8,5,16,128]{3,2,1,0:T(8,128)} custom-call(f32[3,16,128]{2,1,0:T(8,128)} %bitcast.10, f32[16,128]{1,0:T(8,128)} %h_hbm.1, f32[16,128]{1,0:T(8,128)} %mass_hbm.1), custom_call_target="tpu_custom_call" | custom-call | tf_op jit(solution)/shard_map/copy_out/pallas_call | solution.py:174
  11.9 7.3 %all-to-all-start = ((f32[8,80,128]{2,1,0:T(8,128)}), f32[8,80,128]{2,1,0:T(8,128)S(1)}, u32[]{:S(2)}, u32[]{:S(2)}) async-start(f32[8,80,128]{2,1,0:T(8,128)} %bitcast.3), calls=%async_computation | async-start | bytes 655360 | tf_op jit(solution)/shard_map/all_to_all | solution.py:183
  19.2 4.8 %local_density.1 = (f32[14,16,128]{2,1,0:T(8,128)S(1)}, bf16[16,48,128]{2,1,0:T(8,128)(2,1)S(1)}, f32[16,8,128]{2,1,0:T(8,128)S(1)}) custom-call(s32[2,16]{1,0:T(2,128)} %bitcast.18, f32[3,16,128]{2,1,0:T(8,128)} %bitcast.11, f32[16,128]{1,0:T(8,128)} %h_hbm.1, f32[16,128]{1,0:T(8,128)} %mass_hbm.1, f32[16,128]{1,0:T(8,128)} %energy_hbm.1, ...), custom_call_target="tpu_custom_call" | custom-call | flops 7864320 | bytes 65536 | tf_op jit(solution)/shard_map/local_density/pallas_call | solution.py:238
  24.0 5.5 %all-to-all-done.near_ref = f32[8,80,128]{2,1,0:T(8,128)S(1)} async-done(((f32[8,80,128]{2,1,0:T(8,128)}), f32[8,80,128]{2,1,0:T(8,128)S(1)}, u32[]{:S(2)}, u32[]{:S(2)}) %all-to-all-start) | async-done | bytes 327712 | tf_op jit(solution)/shard_map/all_to_all | solution.py:183
  29.5 0.0 collective-permute-start
  29.5 1.6 %collective-permute-done.peer_ref = f32[8,80,128]{2,1,0:T(8,128)S(1)} collective-permute-done((f32[8,80,128]{2,1,0:T(8,128)S(1)}, f32[8,80,128]{2,1,0:T(8,128)S(1)}, u32[]{:S(2)}, u32[]{:S(2)}) %collective-permute-start) | collective-permute-done | bytes 327712 | tf_op jit(solution)/shard_map/ppermute | solution.py:252
  31.1 2.9 %remote_density.1 = (f32[16,128]{1,0:T(8,128)}, f32[16,128]{1,0:T(8,128)}, f32[16,16,128]{2,1,0:T(8,128)}) custom-call(s32[2,24]{1,0:T(2,128)} %bitcast.12, s32[1,24]{1,0:T(1,128)} %bitcast.15, f32[14,16,128]{2,1,0:T(8,128)S(1)} %get-tuple-element.17.own_ref, bf16[16,48,128]{2,1,0:T(8,128)(2,1)S(1)} %get-tuple-element.18.right_ref, ...), custom_call_target="tpu_custom_call" | custom-call | flops 11796480 | bytes 65536 | tf_op jit(solution)/shard_map/remote_density/pallas_call | solution.py:297
  34.0 3.7 %all-to-all-start.1 = ((f32[16,16,128]{2,1,0:T(8,128)}), f32[16,16,128]{2,1,0:T(8,128)S(1)}, u32[]{:S(2)}, u32[]{:S(2)}) async-start(f32[16,16,128]{2,1,0:T(8,128)} %get-tuple-element.24), calls=%async_computation.1 | async-start | bytes 262144 | tf_op jit(solution)/shard_map/all_to_all | solution.py:307
  37.8 6.2 %prepare_force.1 = (f32[16,4,128]{2,1,0:T(4,128)S(1)}, bf16[24,384,128]{2,1,0:T(8,128)(2,1)S(1)}, f32[24,8,128]{2,1,0:T(8,128)}) custom-call(s32[2,16]{1,0:T(2,128)} %bitcast.19, s32[2,24]{1,0:T(2,128)} %bitcast.13, s32[1,24]{1,0:T(1,128)} %bitcast.16, f32[16,128]{1,0:T(8,128)} %get-tuple-element.21.term_hbm, f32[14,16,128]{2,1,0:T(8,128)S(1)} %get-tuple-element.17.own_ref, ...), custom_call_target="tpu_custom_call" | custom-call | flops 39321600 | bytes 65536 | tf_op jit(solution)/shard_map/prepare_force/pallas_call | solution.py:355
  44.0 1.7 %all-to-all-done.1.terms_ref = f32[16,16,128]{2,1,0:T(8,128)S(1)} async-done(((f32[16,16,128]{2,1,0:T(8,128)}), f32[16,16,128]{2,1,0:T(8,128)S(1)}, u32[]{:S(2)}, u32[]{:S(2)}) %all-to-all-start.1) | async-done | bytes 131104 | tf_op jit(solution)/shard_map/all_to_all | solution.py:307
  45.7 2.1 %finish_force.1 = (f32[3,16,128]{2,1,0:T(8,128)}, f32[32,128]{1,0:T(8,128)S(1)}) custom-call(s32[2,24]{1,0:T(2,128)} %bitcast.14, s32[1,24]{1,0:T(1,128)} %bitcast.17, f32[16,128]{1,0:T(8,128)} %get-tuple-element.21.term_hbm, f32[24,8,128]{2,1,0:T(8,128)} %get-tuple-element.23.moment_hbm, f32[14,16,128]{2,1,0:T(8,128)S(1)} %get-tuple-element.17.own_ref, ...), custom_call_target="tpu_custom_call" | custom-call | flops 6291456 | bytes 65536 | tf_op jit(solution)/shard_map/finish_force/pallas_call | solution.py:413
  47.8 11.3 %all_to_all.19 = f32[32,1,128]{2,1,0:T(1,128)S(1)} all-to-all(f32[32,1,128]{2,1,0:T(1,128)S(1)} %bitcast.9), channel_id=1, replica_groups=mesh['grp'=2,'chip'=8,'core'=2] {'grp','chip','core'}, dimensions={0} | all-to-all | bytes 32768 | tf_op jit(solution)/shard_map/all_to_all | solution.py:430
  59.0 0.6 %reduce_min.9 = f32[]{:T(128)} reduce(f32[32,1,128]{2,1,0:T(1,128)S(1)} %all_to_all.19, f32[]{:T(128)} %constant.0.clone.1), dimensions={0,1,2}, to_apply=%region_0.0 | reduce | flops 4095 | bytes 16392 | tf_op jit(solution)/shard_map/reduce_min | solution.py:431
Async XLA Ops:
  11.9 17.6 %all-to-all-start = ((f32[8,80,128]{2,1,0:T(8,128)}), f32[8,80,128]{2,1,0:T(8,128)S(1)}, u32[]{:S(2)}, u32[]{:S(2)}) async-start(f32[8,80,128]{2,1,0:T(8,128)} %bitcast.3), calls=%async_computation | async-start | bytes 655360 | tf_op jit(solution)/shard_map/all_to_all | solution.py:183
  29.5 1.6 %collective-permute-start = (f32[8,80,128]{2,1,0:T(8,128)S(1)}, f32[8,80,128]{2,1,0:T(8,128)S(1)}, u32[]{:S(2)}, u32[]{:S(2)}) collective-permute-start(f32[8,80,128]{2,1,0:T(8,128)S(1)} %all-to-all-done.near_ref), channel_id=1, source_target_pairs={{0,1},{1,0},{2,3},{3,2},{4,5},{5,4},{6,7},{7,6},{8,9},{9,8},{10,11... | collective-permute-start | bytes 983048 | tf_op jit(solution)/shard_map/ppermute | solution.py:252
  34.0 11.6 %all-to-all-start.1 = ((f32[16,16,128]{2,1,0:T(8,128)}), f32[16,16,128]{2,1,0:T(8,128)S(1)}, u32[]{:S(2)}, u32[]{:S(2)}) async-start(f32[16,16,128]{2,1,0:T(8,128)} %get-tuple-element.24), calls=%async_computation.1 | async-start | bytes 262144 | tf_op jit(solution)/shard_map/all_to_all | solution.py:307

commit v6 on v5

--- a/solution.py
+++ b/solution.py
@@ -152,9 +152,14 @@
         def shape(*sizes):
             return jax.ShapeDtypeStruct(sizes, f32)
 
+        def near_core(*sizes):
+            small = math.prod(sizes) * 4 <= MIB // 2
+            return (pltpu.VMEM if small else pltpu.HBM)(sizes, f32)
+
         def kept(item):
             return pltpu.with_memory_space_constraint(item, pltpu.HBM)
 
+        awake = active
         place = kept(positions.transpose(1, 0, 2))
         smoothing, energy, mass = kept(smoothing), kept(energy), kept(mass)
         old_density, active = kept(old_density), kept(active)
@@ -171,14 +176,14 @@
                 copies += [(place_ref, to.at[pl.ds(0, 3)]), (h_ref, to.at[3]), (mass_ref, to.at[4])]
             fetch(sems, *copies)
 
-        outgoing = pl.pallas_call(
+        outgoing = call(
             copy_out,
-            out_shape=shape(chips, 5, leaves, width),
-            in_specs=[hbm] * 3,
-            out_specs=hbm,
-            scratch_shapes=[pltpu.SemaphoreType.DMA((3 * chips,))],
-            compiler_params=pltpu.CompilerParams(vmem_limit_bytes=MIB),
-            name="copy_out",
+            "copy_out",
+            near_core(chips, 5, leaves, width),
+            [hbm] * 3,
+            [pltpu.SemaphoreType.DMA((3 * chips,))],
+            1,
+            4 + 2 * chips * 5 * leaves * width * 4 // MIB,
         )(place, smoothing, mass).reshape(chips, 5 * leaves, width)
         near = lax.all_to_all(outgoing, "chip", split_axis=0, concat_axis=0, tiled=True)
 
@@ -268,8 +273,8 @@
             return mine, spot, [get(c) for c in items]
 
         def remote_density(
-            leaf_hbm, route_hbm, own_ref, right_ref, near_ref, peer_ref, density_ref, term_ref,
-            spread_ref, total, leaf_ref, route_ref, sems
+            leaf_hbm, route_hbm, own_ref, right_ref, near_ref, peer_ref, spread_ref, total, leaf_ref,
+            route_ref, sems
         ):
             fetch(sems, (leaf_hbm, leaf_ref), (route_hbm, route_ref))
             total[...] = own_ref[SUM]
@@ -288,35 +293,34 @@
             summed = (total[...] + own_ref[MASS]) * (NORM * (inverse * inverse * inverse))
             density = jnp.where(own_ref[ACTIVE] == 1.0, summed, own_ref[OLD])
             term = (ADIABATIC - 1.0) * own_ref[ENERGY] / density
-            density_ref[...] = density
-            term_ref[...] = term
             for d in range(domains):
                 spread_ref[d] = term
 
         wire_mib = 2 * domains * leaves * width * 20 // MIB
-        density, term, outgoing = call(
+        outgoing = call(
             remote_density,
             "remote_density",
-            (shape(leaves, width), pltpu.HBM((leaves, width), f32), shape(domains, leaves, width)),
+            near_core(domains, leaves, width),
             [hbm] * 2 + [vmem] * 4,
             [sheet, leaf_table, route_table, pltpu.SemaphoreType.DMA((2,))],
             exports * tile_flops * 30,
             6 + wire_mib,
         )(export_leaves, export_route, own, right, near, peer)
-        term = kept(term)
         terms = lax.all_to_all(outgoing, ("chip", "core"), split_axis=0, concat_axis=0, tiled=True)
 
         def prepare(
-            pair_hbm, leaf_hbm, route_hbm, term_hbm, own_ref, right_ref, centred_ref, near_ref,
-            peer_ref, sum_ref, weight_ref, moment_ref, pair_ref, leaf_ref, route_ref, term_ref, sems
+            pair_hbm, leaf_hbm, route_hbm, spread_ref, own_ref, right_ref, centred_ref, near_ref,
+            peer_ref, density_ref, sum_ref, weight_ref, moment_ref, pair_ref, leaf_ref, route_ref, sems
         ):
             fetch(
                 sems,
                 (pair_hbm, pair_ref),
                 (leaf_hbm, leaf_ref),
                 (route_hbm, route_ref),
-                (term_hbm, term_ref),
             )
+            term_ref = spread_ref.at[0]
+            fresh = (ADIABATIC - 1.0) * own_ref[ENERGY] / term_ref[...]
+            density_ref[...] = jnp.where(own_ref[ACTIVE] == 1.0, fresh, own_ref[OLD])
             sum_ref[...] = jnp.zeros_like(sum_ref)
 
             def weigh(mine, spot, inverse, scale):
@@ -352,29 +356,29 @@
             grouped(exports, remote_tile)
 
         stash_mib = 2 * exports * width * (6 * width + 32) // MIB
-        partial, weights, rows = call(
+        density, partial, weights, rows = call(
             prepare,
             "prepare_force",
             (
+                shape(leaves, width),
                 shape(leaves, 4, width),
                 jax.ShapeDtypeStruct((exports, 3 * width, width), jnp.bfloat16),
                 pltpu.HBM((exports, 8, width), f32),
             ),
-            [hbm] * 4 + [vmem] * 5,
-            [pair_table, leaf_table, route_table, sheet, pltpu.SemaphoreType.DMA((4,))],
+            [hbm] * 3 + [vmem] * 6,
+            [pair_table, leaf_table, route_table, pltpu.SemaphoreType.DMA((3,))],
             (pairs + exports) * tile_flops * 60,
             6 + stash_mib + wire_mib,
-        )(pair_list, export_leaves, export_route, term, own, right, centred, near, peer)
+        )(pair_list, export_leaves, export_route, outgoing, own, right, centred, near, peer)
 
         def finish(
-            leaf_hbm, route_hbm, term_hbm, moment_hbm, own_ref, centred_ref, terms_ref, partial_ref,
-            weight_ref, accel_ref, least_ref, total, leaf_ref, route_ref, term_ref, moment_ref, sems
+            leaf_hbm, route_hbm, moment_hbm, own_ref, centred_ref, terms_ref, partial_ref, weight_ref,
+            accel_ref, least_ref, total, leaf_ref, route_ref, moment_ref, sems
         ):
             fetch(
                 sems,
                 (leaf_hbm, leaf_ref),
                 (route_hbm, route_ref),
-                (term_hbm, term_ref),
                 (moment_hbm, moment_ref),
             )
             total[...] = partial_ref[...]
@@ -389,7 +393,7 @@
                     weight_ref[e],
                     moment_ref[e],
                     far_term,
-                    term_ref[pl.ds(mine, 1), :],
+                    terms_ref[me, pl.ds(mine, 1), :],
                     centred_ref[mine],
                 )
 
@@ -398,11 +402,8 @@
                 for leaf in range(leaves):
                     accel_ref[c, leaf : leaf + 1, :] = total[leaf, c + 1 : c + 2, :]
             awake = own_ref[ACTIVE] == 1.0
-            square = jnp.zeros((leaves, width), f32)
-            for c in range(3):
-                part = jnp.where(awake, accel_ref[c], 0.0)
-                accel_ref[c] = part
-                square = square + part * part
+            square = accel_ref[0] * accel_ref[0] + accel_ref[1] * accel_ref[1]
+            square = square + accel_ref[2] * accel_ref[2]
             h = own_ref[H]
             speed = jnp.sqrt(ADIABATIC * (ADIABATIC - 1.0) * own_ref[ENERGY])
             step = COURANT * h / (speed + jnp.sqrt(h * jnp.sqrt(square)))
@@ -413,22 +414,22 @@
         accel, least = call(
             finish,
             "finish_force",
-            (shape(3, leaves, width), shape(members, width)),
-            [hbm] * 4 + [vmem] * 5,
+            (near_core(3, leaves, width), near_core(members, width)),
+            [hbm] * 3 + [vmem] * 5,
             [
                 pltpu.VMEM((leaves, 4, width), f32),
                 leaf_table,
                 route_table,
-                sheet,
                 pltpu.VMEM((exports, 8, width), f32),
-                pltpu.SemaphoreType.DMA((4,)),
+                pltpu.SemaphoreType.DMA((3,)),
             ],
             exports * tile_flops * 16,
             6 + stash_mib + wire_mib,
-        )(export_leaves, export_route, term, kept(rows), own, centred, terms, partial, weights)
+        )(export_leaves, export_route, kept(rows), own, centred, terms, partial, weights)
 
         everywhere = lax.all_to_all(least, everyone, split_axis=0, concat_axis=0, tiled=True)
-        return density, accel.transpose(1, 0, 2), jnp.min(everywhere)
+        accel = jnp.where((awake == 1)[:, None, :], accel.transpose(1, 0, 2), 0.0)
+        return density, accel, jnp.min(everywhere)
 
     flat = P(everyone, None)
     deep = P(everyone, None, None)

time: 60.1 us -> 53.5 us (0.89)
  blocking collectives: 11.3 us -> 0 us
  Pallas kernels: 27.2 us -> 19.7 us
  starting transfers between devices: 11.1 us -> 17 us
  waiting for transfers between devices: 8.8 us -> 13.7 us
  other arithmetic: 0.63 us -> 1.83 us
    all_to_all x1 -> x0, blocking collectives: 11.3 us -> none  [body(): lax.all_to_all(least, everyone, split_axis=0, concat_axis=0, tiled=True)]
    pallas_call x4, Pallas kernels: 22.5 us -> 14.9 us  [the longest x1 7.69 us: body(): call(prepare, 'prepare_force', (shape(leaves, width), shape(leaves, 4, wi...]
    all_to_all x0 -> x1, waiting for transfers between devices: none -> 6.54 us  [body(): lax.all_to_all(least, everyone, split_axis=0, concat_axis=0, tiled=True)]
    all_to_all x0 -> x1, starting transfers between devices: none -> 5.93 us  [body(): lax.all_to_all(least, everyone, split_axis=0, concat_axis=0, tiled=True)]
    all_to_all x1, waiting for transfers between devices: 1.65 us -> 0.01 us  [body(): lax.all_to_all(outgoing, ('chip', 'core'), split_axis=0, concat_axis=0, t...]
    select_n x0 -> x1, other arithmetic: none -> 0.61 us  [body(): accel = jnp.where((awake == 1)[:, None, :], accel.transpose(1, 0, 2), 0.0)]
  transfers between devices with their start and end apart: 3 -> 4, of which waited for: 3 -> 3; matrix products, arithmetic and copies ran while one was open for 0% -> 2% of each run, Pallas kernels for 18% -> 24%
where the time goes in v6:
time: 53.5 us; the launch traced here: 52.9 us
  Pallas kernels  19.7 us (37%)
  starting transfers between devices  17 us (32%)
  waiting for transfers between devices  13.7 us (26%)
  other arithmetic  1.83 us (3%)
  between operations  0.73 us (1%)
    pallas_call x1, Pallas kernels, body(): call(prepare, 'prepare_force', (shape(leaves, width), shape(leaves, 4, wi...  7.69 us
    all_to_all x1, starting transfers between devices, body(): lax.all_to_all(outgoing, 'chip', split_axis=0, concat_axis=0, tiled=True)  7.32 us
    all_to_all x1, waiting for transfers between devices, body(): lax.all_to_all(least, everyone, split_axis=0, concat_axis=0, tiled=True)  6.54 us
    all_to_all x1, starting transfers between devices, body(): lax.all_to_all(least, everyone, split_axis=0, concat_axis=0, tiled=True)  5.93 us
    all_to_all x1, waiting for transfers between devices, body(): lax.all_to_all(outgoing, 'chip', split_axis=0, concat_axis=0, tiled=True)  5.52 us
    pallas_call x1, Pallas kernels, body(): call(local_density, 'local_density', (shape(TABLE, leaves, width), jax.Sh...  4.78 us
    all_to_all x1, starting transfers between devices, body(): lax.all_to_all(outgoing, ('chip', 'core'), split_axis=0, concat_axis=0, t...  3.73 us
    pallas_call x1, Pallas kernels, body(): call(remote_density, 'remote_density', near_core(domains, leaves, width),...  2.86 us
  transfers between devices with their start and end apart: 4, of which 3 were waited for; matrix products, arithmetic and copies ran while one was open for 2% of the time, Pallas kernels for 24%

profile of v6, /device:TPU:0, one launch (start us, length us, event | category | flops | bytes accessed | tf_op | source)
XLA Modules:
  0.0 52.9 jit_solution(13869106539667239108)
XLA Ops:
  0.6 0.0 copy-start
  0.6 2.1 %copy_out.1 = f32[8,5,16,128]{3,2,1,0:T(8,128)} custom-call(f32[3,16,128]{2,1,0:T(8,128)} %bitcast.10, f32[16,128]{1,0:T(8,128)} %h_hbm.1, f32[16,128]{1,0:T(8,128)} %mass_hbm.1), custom_call_target="tpu_custom_call" | custom-call | flops 1 | bytes 65536 | tf_op jit(solution)/shard_map/copy_out/pallas_call | solution.py:179
  2.8 7.3 %all-to-all-start = ((f32[8,80,128]{2,1,0:T(8,128)}), f32[8,80,128]{2,1,0:T(8,128)S(1)}, u32[]{:S(2)}, u32[]{:S(2)}) async-start(f32[8,80,128]{2,1,0:T(8,128)} %bitcast.4), calls=%async_computation | async-start | bytes 655360 | tf_op jit(solution)/shard_map/all_to_all | solution.py:188
  10.1 4.8 %local_density.1 = (f32[14,16,128]{2,1,0:T(8,128)S(1)}, bf16[16,48,128]{2,1,0:T(8,128)(2,1)S(1)}, f32[16,8,128]{2,1,0:T(8,128)S(1)}) custom-call(s32[2,16]{1,0:T(2,128)} %bitcast.18, f32[3,16,128]{2,1,0:T(8,128)} %bitcast.11, f32[16,128]{1,0:T(8,128)} %h_hbm.1, f32[16,128]{1,0:T(8,128)} %mass_hbm.1, f32[16,128]{1,0:T(8,128)} %energy_hbm.1, ...), custom_call_target="tpu_custom_call" | custom-call | flops 7864320 | bytes 65536 | tf_op jit(solution)/shard_map/local_density/pallas_call | solution.py:243
  14.9 5.5 %all-to-all-done.near_ref = f32[8,80,128]{2,1,0:T(8,128)S(1)} async-done(((f32[8,80,128]{2,1,0:T(8,128)}), f32[8,80,128]{2,1,0:T(8,128)S(1)}, u32[]{:S(2)}, u32[]{:S(2)}) %all-to-all-start) | async-done | bytes 327712 | tf_op jit(solution)/shard_map/all_to_all | solution.py:188
  20.4 0.0 collective-permute-start
  20.4 1.6 %collective-permute-done.peer_ref = f32[8,80,128]{2,1,0:T(8,128)S(1)} collective-permute-done((f32[8,80,128]{2,1,0:T(8,128)S(1)}, f32[8,80,128]{2,1,0:T(8,128)S(1)}, u32[]{:S(2)}, u32[]{:S(2)}) %collective-permute-start) | collective-permute-done | bytes 327712 | tf_op jit(solution)/shard_map/ppermute | solution.py:257
  22.0 2.9 %remote_density.1.spread_ref = f32[16,16,128]{2,1,0:T(8,128)} custom-call(s32[2,24]{1,0:T(2,128)} %bitcast.12, s32[1,24]{1,0:T(1,128)} %bitcast.15, f32[14,16,128]{2,1,0:T(8,128)S(1)} %get-tuple-element.15.own_ref, bf16[16,48,128]{2,1,0:T(8,128)(2,1)S(1)} %get-tuple-element.16.right_ref, f32[8,80,128]{2,1,0:T(8,128)S(1)} %all-to-all-done.near_ref, ...), custom_call_target="tpu_custom_call" | custom-call | flops 11796480 | bytes 65536 | tf_op jit(solution)/shard_map/remote_density/pallas_call | solution.py:300
  24.9 3.7 %all-to-all-start.1 = ((f32[16,16,128]{2,1,0:T(8,128)}), f32[16,16,128]{2,1,0:T(8,128)S(1)}, u32[]{:S(2)}, u32[]{:S(2)}) async-start(f32[16,16,128]{2,1,0:T(8,128)} %remote_density.1.spread_ref), calls=%async_computation.1 | async-start | bytes 262144 | tf_op jit(solution)/shard_map/all_to_all | solution.py:309
  28.6 0.0 copy-done
  28.6 0.6 %broadcast_compare_fusion = pred[16,128]{1,0:T(8,128)(4,1)} fusion(s32[16,128]{1,0:T(8,128)S(1)} %copy-done), kind=kLoop, calls=%fused_computation.1 | loop fusion | flops 2048 | bytes 10240 | tf_op jit(solution)/shard_map/eq | solution.py:431
  29.2 7.7 %prepare_force.1 = (f32[16,128]{1,0:T(8,128)}, f32[16,4,128]{2,1,0:T(4,128)S(1)}, bf16[24,384,128]{2,1,0:T(8,128)(2,1)S(1)}, f32[24,8,128]{2,1,0:T(8,128)}) custom-call(s32[2,16]{1,0:T(2,128)} %bitcast.19, s32[2,24]{1,0:T(2,128)} %bitcast.13, s32[1,24]{1,0:T(1,128)} %bitcast.16, f32[16,16,128]{2,1,0:T(8,128)} %remote_density.1.spread_ref, ...), custom_call_target="tpu_custom_call" | custom-call | flops 39321600 | bytes 65536 | tf_op jit(solution)/shard_map/prepare_force/pallas_call | solution.py:359
  36.9 0.0 copy-start.1
  36.9 0.0 all-to-all-done.1.terms_ref
  36.9 2.2 %finish_force.1 = (f32[3,16,128]{2,1,0:T(8,128)S(1)}, f32[32,128]{1,0:T(8,128)}) custom-call(s32[2,24]{1,0:T(2,128)} %bitcast.14, s32[1,24]{1,0:T(1,128)} %bitcast.17, f32[24,8,128]{2,1,0:T(8,128)} %get-tuple-element.20.moment_hbm, f32[14,16,128]{2,1,0:T(8,128)S(1)} %get-tuple-element.15.own_ref, f32[16,8,128]{2,1,0:T(8,128)S(1)} %get-tuple-element.18.centred_ref, ...), custom_call_target="tpu_custom_call" | custom-call | flops 6291456 | bytes 65536 | tf_op jit(solution)/shard_map/finish_force/pallas_call | solution.py:414
  39.2 5.9 %all-to-all-start.2 = ((f32[32,1,128]{2,1,0:T(1,128)}), f32[32,1,128]{2,1,0:T(1,128)S(1)}, u32[]{:S(2)}, u32[]{:S(2)}) async-start(f32[32,1,128]{2,1,0:T(1,128)} %bitcast.7), calls=%async_computation.2 | async-start | bytes 32768 | tf_op jit(solution)/shard_map/all_to_all | solution.py:430
  45.1 0.0 copy-done.1
  45.1 0.6 %select_bitcast_fusion = f32[16,3,128]{2,0,1:T(8,128)} fusion(f32[3,16,128]{2,1,0:T(8,128)S(1)} %get-tuple-element.23, pred[16,128]{1,0:T(8,128)(4,1)S(1)} %copy-done.1), kind=kLoop, calls=%fused_computation | loop fusion | flops 6144 | bytes 51200 | tf_op jit(solution)/shard_map/jit(_where)/select_n | solution.py:431
  45.7 6.5 %all-to-all-done.2 = f32[32,1,128]{2,1,0:T(1,128)S(1)} async-done(((f32[32,1,128]{2,1,0:T(1,128)}), f32[32,1,128]{2,1,0:T(1,128)S(1)}, u32[]{:S(2)}, u32[]{:S(2)}) %all-to-all-start.2) | async-done | bytes 16416 | tf_op jit(solution)/shard_map/all_to_all | solution.py:430
  52.3 0.6 %reduce_min.9 = f32[]{:T(128)} reduce(f32[32,1,128]{2,1,0:T(1,128)S(1)} %all-to-all-done.2, f32[]{:T(128)} %constant.2.clone.1), dimensions={0,1,2}, to_apply=%region_0.1 | reduce | flops 4095 | bytes 16392 | tf_op jit(solution)/shard_map/reduce_min | solution.py:432
Async XLA Ops:
  0.6 28.0 %copy-start = (s32[16,128]{1,0:T(8,128)S(1)}, s32[16,128]{1,0:T(8,128)}, u32[]{:S(2)}) copy-start(s32[16,128]{1,0:T(8,128)} %active_hbm.1) | copy-start | bytes 24580
  2.8 17.6 %all-to-all-start = ((f32[8,80,128]{2,1,0:T(8,128)}), f32[8,80,128]{2,1,0:T(8,128)S(1)}, u32[]{:S(2)}, u32[]{:S(2)}) async-start(f32[8,80,128]{2,1,0:T(8,128)} %bitcast.4), calls=%async_computation | async-start | bytes 655360 | tf_op jit(solution)/shard_map/all_to_all | solution.py:188
  20.4 1.6 %collective-permute-start = (f32[8,80,128]{2,1,0:T(8,128)S(1)}, f32[8,80,128]{2,1,0:T(8,128)S(1)}, u32[]{:S(2)}, u32[]{:S(2)}) collective-permute-start(f32[8,80,128]{2,1,0:T(8,128)S(1)} %all-to-all-done.near_ref), channel_id=1, source_target_pairs={{0,1},{1,0},{2,3},{3,2},{4,5},{5,4},{6,7},{7,6},{8,9},{9,8},{10,11... | collective-permute-start | bytes 983048 | tf_op jit(solution)/shard_map/ppermute | solution.py:257
  24.9 12.0 %all-to-all-start.1 = ((f32[16,16,128]{2,1,0:T(8,128)}), f32[16,16,128]{2,1,0:T(8,128)S(1)}, u32[]{:S(2)}, u32[]{:S(2)}) async-start(f32[16,16,128]{2,1,0:T(8,128)} %remote_density.1.spread_ref), calls=%async_computation.1 | async-start | bytes 262144 | tf_op jit(solution)/shard_map/all_to_all | solution.py:309
  36.9 8.2 %copy-start.1 = (pred[16,128]{1,0:T(8,128)(4,1)S(1)}, pred[16,128]{1,0:T(8,128)(4,1)}, u32[]{:S(2)}) copy-start(pred[16,128]{1,0:T(8,128)(4,1)} %broadcast_compare_fusion) | copy-start | bytes 6148
  39.2 13.1 %all-to-all-start.2 = ((f32[32,1,128]{2,1,0:T(1,128)}), f32[32,1,128]{2,1,0:T(1,128)S(1)}, u32[]{:S(2)}, u32[]{:S(2)}) async-start(f32[32,1,128]{2,1,0:T(1,128)} %bitcast.7), calls=%async_computation.2 | async-start | bytes 32768 | tf_op jit(solution)/shard_map/all_to_all | solution.py:430

commit v7 on v6

--- a/solution.py
+++ b/solution.py
@@ -152,14 +152,9 @@
         def shape(*sizes):
             return jax.ShapeDtypeStruct(sizes, f32)
 
-        def near_core(*sizes):
-            small = math.prod(sizes) * 4 <= MIB // 2
-            return (pltpu.VMEM if small else pltpu.HBM)(sizes, f32)
-
         def kept(item):
             return pltpu.with_memory_space_constraint(item, pltpu.HBM)
 
-        awake = active
         place = kept(positions.transpose(1, 0, 2))
         smoothing, energy, mass = kept(smoothing), kept(energy), kept(mass)
         old_density, active = kept(old_density), kept(active)
@@ -169,21 +164,26 @@
         route_table = pltpu.SMEM((1, exports), s32)
         sheet = pltpu.VMEM((leaves, width), f32)
 
-        def copy_out(place_ref, h_ref, mass_ref, out_ref, sems):
-            copies = []
-            for k in range(chips):
-                to = out_ref.at[k]
-                copies += [(place_ref, to.at[pl.ds(0, 3)]), (h_ref, to.at[3]), (mass_ref, to.at[4])]
-            fetch(sems, *copies)
-
-        outgoing = call(
+        def copy_out(place_ref, h_ref, mass_ref, out_ref, mine_ref, sems):
+            fetch(
+                sems,
+                (place_ref, mine_ref.at[pl.ds(0, 3)]),
+                (h_ref, mine_ref.at[3]),
+                (mass_ref, mine_ref.at[4]),
+            )
+            fetch(sems, *[(mine_ref, out_ref.at[k]) for k in range(chips)])
+
+        outgoing = pl.pallas_call(
             copy_out,
-            "copy_out",
-            near_core(chips, 5, leaves, width),
-            [hbm] * 3,
-            [pltpu.SemaphoreType.DMA((3 * chips,))],
-            1,
-            4 + 2 * chips * 5 * leaves * width * 4 // MIB,
+            out_shape=pltpu.HBM((chips, 5, leaves, width), f32),
+            in_specs=[hbm] * 3,
+            out_specs=hbm,
+            scratch_shapes=[
+                pltpu.VMEM((5, leaves, width), f32),
+                pltpu.SemaphoreType.DMA((max(3, chips),)),
+            ],
+            compiler_params=pltpu.CompilerParams(vmem_limit_bytes=2 * MIB),
+            name="copy_out",
         )(place, smoothing, mass).reshape(chips, 5 * leaves, width)
         near = lax.all_to_all(outgoing, "chip", split_axis=0, concat_axis=0, tiled=True)
 
@@ -300,7 +300,7 @@
         outgoing = call(
             remote_density,
             "remote_density",
-            near_core(domains, leaves, width),
+            pltpu.HBM((domains, leaves, width), f32),
             [hbm] * 2 + [vmem] * 4,
             [sheet, leaf_table, route_table, pltpu.SemaphoreType.DMA((2,))],
             exports * tile_flops * 30,
@@ -309,16 +309,17 @@
         terms = lax.all_to_all(outgoing, ("chip", "core"), split_axis=0, concat_axis=0, tiled=True)
 
         def prepare(
-            pair_hbm, leaf_hbm, route_hbm, spread_ref, own_ref, right_ref, centred_ref, near_ref,
-            peer_ref, density_ref, sum_ref, weight_ref, moment_ref, pair_ref, leaf_ref, route_ref, sems
+            pair_hbm, leaf_hbm, route_hbm, spread_hbm, own_ref, right_ref, centred_ref, near_ref,
+            peer_ref, density_ref, sum_ref, weight_ref, moment_ref, pair_ref, leaf_ref, route_ref,
+            term_ref, sems
         ):
             fetch(
                 sems,
                 (pair_hbm, pair_ref),
                 (leaf_hbm, leaf_ref),
                 (route_hbm, route_ref),
+                (spread_hbm.at[0], term_ref),
             )
-            term_ref = spread_ref.at[0]
             fresh = (ADIABATIC - 1.0) * own_ref[ENERGY] / term_ref[...]
             density_ref[...] = jnp.where(own_ref[ACTIVE] == 1.0, fresh, own_ref[OLD])
             sum_ref[...] = jnp.zeros_like(sum_ref)
@@ -365,11 +366,11 @@
                 jax.ShapeDtypeStruct((exports, 3 * width, width), jnp.bfloat16),
                 pltpu.HBM((exports, 8, width), f32),
             ),
-            [hbm] * 3 + [vmem] * 6,
-            [pair_table, leaf_table, route_table, pltpu.SemaphoreType.DMA((3,))],
+            [hbm] * 4 + [vmem] * 5,
+            [pair_table, leaf_table, route_table, sheet, pltpu.SemaphoreType.DMA((4,))],
             (pairs + exports) * tile_flops * 60,
             6 + stash_mib + wire_mib,
-        )(pair_list, export_leaves, export_route, outgoing, own, right, centred, near, peer)
+        )(pair_list, export_leaves, export_route, kept(outgoing), own, right, centred, near, peer)
 
         def finish(
             leaf_hbm, route_hbm, moment_hbm, own_ref, centred_ref, terms_ref, partial_ref, weight_ref,
@@ -402,8 +403,11 @@
                 for leaf in range(leaves):
                     accel_ref[c, leaf : leaf + 1, :] = total[leaf, c + 1 : c + 2, :]
             awake = own_ref[ACTIVE] == 1.0
-            square = accel_ref[0] * accel_ref[0] + accel_ref[1] * accel_ref[1]
-            square = square + accel_ref[2] * accel_ref[2]
+            square = jnp.zeros((leaves, width), f32)
+            for c in range(3):
+                part = jnp.where(awake, accel_ref[c], 0.0)
+                accel_ref[c] = part
+                square = square + part * part
             h = own_ref[H]
             speed = jnp.sqrt(ADIABATIC * (ADIABATIC - 1.0) * own_ref[ENERGY])
             step = COURANT * h / (speed + jnp.sqrt(h * jnp.sqrt(square)))
@@ -414,7 +418,7 @@
         accel, least = call(
             finish,
             "finish_force",
-            (near_core(3, leaves, width), near_core(members, width)),
+            (shape(3, leaves, width), shape(members, width)),
             [hbm] * 3 + [vmem] * 5,
             [
                 pltpu.VMEM((leaves, 4, width), f32),
@@ -428,8 +432,7 @@
         )(export_leaves, export_route, kept(rows), own, centred, terms, partial, weights)
 
         everywhere = lax.all_to_all(least, everyone, split_axis=0, concat_axis=0, tiled=True)
-        accel = jnp.where((awake == 1)[:, None, :], accel.transpose(1, 0, 2), 0.0)
-        return density, accel, jnp.min(everywhere)
+        return density, accel.transpose(1, 0, 2), jnp.min(everywhere)
 
     flat = P(everyone, None)
     deep = P(everyone, None, None)

time: 53.5 us -> 51 us (0.953)
  blocking collectives: 0 us -> 11.8 us
  starting transfers between devices: 17 us -> 11.1 us
  waiting for transfers between devices: 13.7 us -> 8.23 us
  Pallas kernels: 19.7 us -> 18.1 us
  other arithmetic: 1.83 us -> 0.63 us
    all_to_all x0 -> x1, blocking collectives: none -> 11.8 us  [body(): lax.all_to_all(least, everyone, split_axis=0, concat_axis=0, tiled=True)]
    all_to_all x1 -> x0, waiting for transfers between devices: 6.54 us -> none  [body(): lax.all_to_all(least, everyone, split_axis=0, concat_axis=0, tiled=True)]
    all_to_all x1 -> x0, starting transfers between devices: 5.93 us -> none  [body(): lax.all_to_all(least, everyone, split_axis=0, concat_axis=0, tiled=True)]
    all_to_all x1, waiting for transfers between devices: 0.01 us -> 1.09 us  [body(): lax.all_to_all(outgoing, ('chip', 'core'), split_axis=0, concat_axis=0, t...]
    pallas_call x1, Pallas kernels: 7.69 us -> 6.81 us  [body(): call(prepare, 'prepare_force', (shape(leaves, width), shape(leaves, 4, wi...]
    pallas_call x3, Pallas kernels: 7.2 us -> 6.49 us  [the longest x1 2.86 us: body(): call(remote_density, 'remote_density', pltpu.HBM((domains, leaves, width)...]
    select_n x1 -> x0, other arithmetic: 0.61 us -> none  [body(): accel = jnp.where((awake == 1)[:, None, :], accel.transpose(1, 0, 2), 0.0)]
    eq x1 -> x0, other arithmetic: 0.58 us -> none  [body(): accel = jnp.where((awake == 1)[:, None, :], accel.transpose(1, 0, 2), 0.0)]
  transfers between devices with their start and end apart: 4 -> 3, of which waited for: 3 -> 3; matrix products, arithmetic and copies ran while one was open for 2% -> 0% of each run, Pallas kernels for 24% -> 23%
where the time goes in v7:
time: 51 us; the launch traced here: 50.5 us
  Pallas kernels  18.1 us (35%)
  blocking collectives  11.8 us (23%)
  starting transfers between devices  11.1 us (22%)
  waiting for transfers between devices  8.23 us (16%)
  between operations  0.68 us (1%)
  other arithmetic  0.63 us (1%)
    all_to_all x1, blocking collectives, body(): lax.all_to_all(least, everyone, split_axis=0, concat_axis=0, tiled=True)  11.8 us
    all_to_all x1, starting transfers between devices, body(): lax.all_to_all(outgoing, 'chip', split_axis=0, concat_axis=0, tiled=True)  7.32 us
    pallas_call x1, Pallas kernels, body(): call(prepare, 'prepare_force', (shape(leaves, width), shape(leaves, 4, wi...  6.81 us
    all_to_all x1, waiting for transfers between devices, body(): lax.all_to_all(outgoing, 'chip', split_axis=0, concat_axis=0, tiled=True)  5.52 us
    pallas_call x1, Pallas kernels, body(): call(local_density, 'local_density', (shape(TABLE, leaves, width), jax.Sh...  4.77 us
    all_to_all x1, starting transfers between devices, body(): lax.all_to_all(outgoing, ('chip', 'core'), split_axis=0, concat_axis=0, t...  3.74 us
    pallas_call x1, Pallas kernels, body(): call(remote_density, 'remote_density', pltpu.HBM((domains, leaves, width)...  2.86 us
    pallas_call x1, Pallas kernels, body(): call(finish, 'finish_force', (shape(3, leaves, width), shape(members, wid...  2.1 us
  transfers between devices with their start and end apart: 3, of which 3 were waited for; matrix products, arithmetic and copies ran while one was open for 0% of the time, Pallas kernels for 23%

profile of v7, /device:TPU:0, one launch (start us, length us, event | category | flops | bytes accessed | tf_op | source)
XLA Modules:
  0.0 50.5 jit_solution(7372942430173979031)
XLA Ops:
  0.6 1.5 %copy_out.1 = f32[8,5,16,128]{3,2,1,0:T(8,128)} custom-call(f32[3,16,128]{2,1,0:T(8,128)} %bitcast.11, f32[16,128]{1,0:T(8,128)} %h_hbm.1, f32[16,128]{1,0:T(8,128)} %mass_hbm.1), custom_call_target="tpu_custom_call" | custom-call | tf_op jit(solution)/shard_map/copy_out/pallas_call | solution.py:176
  2.2 7.3 %all-to-all-start = ((f32[8,80,128]{2,1,0:T(8,128)}), f32[8,80,128]{2,1,0:T(8,128)S(1)}, u32[]{:S(2)}, u32[]{:S(2)}) async-start(f32[8,80,128]{2,1,0:T(8,128)} %bitcast.10), calls=%async_computation | async-start | bytes 655360 | tf_op jit(solution)/shard_map/all_to_all | solution.py:188
  9.5 4.8 %local_density.1 = (f32[14,16,128]{2,1,0:T(8,128)S(1)}, bf16[16,48,128]{2,1,0:T(8,128)(2,1)S(1)}, f32[16,8,128]{2,1,0:T(8,128)S(1)}) custom-call(s32[2,16]{1,0:T(2,128)} %bitcast.19, f32[3,16,128]{2,1,0:T(8,128)} %bitcast.12, f32[16,128]{1,0:T(8,128)} %h_hbm.1, f32[16,128]{1,0:T(8,128)} %mass_hbm.1, f32[16,128]{1,0:T(8,128)} %energy_hbm.1, ...), custom_call_target="tpu_custom_call" | custom-call | flops 7864320 | bytes 65536 | tf_op jit(solution)/shard_map/local_density/pallas_call | solution.py:243
  14.3 5.5 %all-to-all-done.near_ref = f32[8,80,128]{2,1,0:T(8,128)S(1)} async-done(((f32[8,80,128]{2,1,0:T(8,128)}), f32[8,80,128]{2,1,0:T(8,128)S(1)}, u32[]{:S(2)}, u32[]{:S(2)}) %all-to-all-start) | async-done | bytes 327712 | tf_op jit(solution)/shard_map/all_to_all | solution.py:188
  19.8 0.0 collective-permute-start
  19.8 1.6 %collective-permute-done.peer_ref = f32[8,80,128]{2,1,0:T(8,128)S(1)} collective-permute-done((f32[8,80,128]{2,1,0:T(8,128)S(1)}, f32[8,80,128]{2,1,0:T(8,128)S(1)}, u32[]{:S(2)}, u32[]{:S(2)}) %collective-permute-start) | collective-permute-done | bytes 327712 | tf_op jit(solution)/shard_map/ppermute | solution.py:257
  21.4 2.9 %remote_density.1.spread_hbm = f32[16,16,128]{2,1,0:T(8,128)} custom-call(s32[2,24]{1,0:T(2,128)} %bitcast.13, s32[1,24]{1,0:T(1,128)} %bitcast.16, f32[14,16,128]{2,1,0:T(8,128)S(1)} %get-tuple-element.15.own_ref, bf16[16,48,128]{2,1,0:T(8,128)(2,1)S(1)} %get-tuple-element.16.right_ref, f32[8,80,128]{2,1,0:T(8,128)S(1)} %all-to-all-done.near_ref, ...), custom_call_target="tpu_custom_call" | custom-call | flops 11796480 | bytes 65536 | tf_op jit(solution)/shard_map/remote_density/pallas_call | solution.py:300
  24.3 3.7 %all-to-all-start.1 = ((f32[16,16,128]{2,1,0:T(8,128)}), f32[16,16,128]{2,1,0:T(8,128)S(1)}, u32[]{:S(2)}, u32[]{:S(2)}) async-start(f32[16,16,128]{2,1,0:T(8,128)} %remote_density.1.spread_hbm), calls=%async_computation.1 | async-start | bytes 262144 | tf_op jit(solution)/shard_map/all_to_all | solution.py:309
  28.0 6.8 %prepare_force.1 = (f32[16,128]{1,0:T(8,128)}, f32[16,4,128]{2,1,0:T(4,128)S(1)}, bf16[24,384,128]{2,1,0:T(8,128)(2,1)S(1)}, f32[24,8,128]{2,1,0:T(8,128)}) custom-call(s32[2,16]{1,0:T(2,128)} %bitcast.20, s32[2,24]{1,0:T(2,128)} %bitcast.14, s32[1,24]{1,0:T(1,128)} %bitcast.17, f32[16,16,128]{2,1,0:T(8,128)} %remote_density.1.spread_hbm, ...), custom_call_target="tpu_custom_call" | custom-call | flops 39321600 | bytes 65536 | tf_op jit(solution)/shard_map/prepare_force/pallas_call | solution.py:360
  34.8 1.1 %all-to-all-done.1.terms_ref = f32[16,16,128]{2,1,0:T(8,128)S(1)} async-done(((f32[16,16,128]{2,1,0:T(8,128)}), f32[16,16,128]{2,1,0:T(8,128)S(1)}, u32[]{:S(2)}, u32[]{:S(2)}) %all-to-all-start.1) | async-done | bytes 131104 | tf_op jit(solution)/shard_map/all_to_all | solution.py:309
  35.9 2.1 %finish_force.1 = (f32[3,16,128]{2,1,0:T(8,128)}, f32[32,128]{1,0:T(8,128)S(1)}) custom-call(s32[2,24]{1,0:T(2,128)} %bitcast.15, s32[1,24]{1,0:T(1,128)} %bitcast.18, f32[24,8,128]{2,1,0:T(8,128)} %get-tuple-element.20.moment_hbm, f32[14,16,128]{2,1,0:T(8,128)S(1)} %get-tuple-element.15.own_ref, f32[16,8,128]{2,1,0:T(8,128)S(1)} %get-tuple-element.18.centred_ref, ...), custom_call_target="tpu_custom_call" | custom-call | flops 6291456 | bytes 65536 | tf_op jit(solution)/shard_map/finish_force/pallas_call | solution.py:418
  38.0 11.8 %all_to_all.19 = f32[32,1,128]{2,1,0:T(1,128)S(1)} all-to-all(f32[32,1,128]{2,1,0:T(1,128)S(1)} %bitcast.9), channel_id=1, replica_groups=mesh['grp'=2,'chip'=8,'core'=2] {'grp','chip','core'}, dimensions={0} | all-to-all | bytes 32768 | tf_op jit(solution)/shard_map/all_to_all | solution.py:434
  49.9 0.6 %reduce_min.9 = f32[]{:T(128)} reduce(f32[32,1,128]{2,1,0:T(1,128)S(1)} %all_to_all.19, f32[]{:T(128)} %constant.0.clone.1), dimensions={0,1,2}, to_apply=%region_0.0 | reduce | flops 4095 | bytes 16392 | tf_op jit(solution)/shard_map/reduce_min | solution.py:435
Async XLA Ops:
  2.2 17.6 %all-to-all-start = ((f32[8,80,128]{2,1,0:T(8,128)}), f32[8,80,128]{2,1,0:T(8,128)S(1)}, u32[]{:S(2)}, u32[]{:S(2)}) async-start(f32[8,80,128]{2,1,0:T(8,128)} %bitcast.10), calls=%async_computation | async-start | bytes 655360 | tf_op jit(solution)/shard_map/all_to_all | solution.py:188
  19.8 1.6 %collective-permute-start = (f32[8,80,128]{2,1,0:T(8,128)S(1)}, f32[8,80,128]{2,1,0:T(8,128)S(1)}, u32[]{:S(2)}, u32[]{:S(2)}) collective-permute-start(f32[8,80,128]{2,1,0:T(8,128)S(1)} %all-to-all-done.near_ref), channel_id=1, source_target_pairs={{0,1},{1,0},{2,3},{3,2},{4,5},{5,4},{6,7},{7,6},{8,9},{9,8},{10,11... | collective-permute-start | bytes 983048 | tf_op jit(solution)/shard_map/ppermute | solution.py:257
  24.3 11.6 %all-to-all-start.1 = ((f32[16,16,128]{2,1,0:T(8,128)}), f32[16,16,128]{2,1,0:T(8,128)S(1)}, u32[]{:S(2)}, u32[]{:S(2)}) async-start(f32[16,16,128]{2,1,0:T(8,128)} %remote_density.1.spread_hbm), calls=%async_computation.1 | async-start | bytes 262144 | tf_op jit(solution)/shard_map/all_to_all | solution.py:309

commit v8 on v7

--- a/solution.py
+++ b/solution.py
@@ -94,6 +94,23 @@
 
 def stack(weights):
     return jnp.concatenate([part.astype(jnp.bfloat16) for part in split(weights)], axis=0)
+
+
+def flags(index, count):
+    rows, width = index.shape
+    lane = lax.broadcasted_iota(jnp.int32, (rows, width), 1).astype(jnp.float32)
+    blocks = [(lane + float(at) == index).astype(jnp.float32) for at in range(0, count, width)]
+    return jnp.concatenate(blocks, axis=1)[:, :count]
+
+
+def select(onehot, data):
+    onehot = jnp.concatenate([onehot] * 3, axis=1).astype(jnp.bfloat16)
+    return product(onehot, jnp.concatenate(split(data), axis=0).astype(jnp.bfloat16), ((1,), (0,)))
+
+
+def by_leaf(onehot, rows):
+    onehot = jnp.concatenate([onehot] * 3, axis=0).astype(jnp.bfloat16)
+    return product(onehot, jnp.concatenate(split(rows), axis=0).astype(jnp.bfloat16), ((0,), (0,)))
 
 
 def slope_scale(h):
@@ -194,8 +211,8 @@
             return [row(own_ref, X + c, other) - row(own_ref, ORIGIN + c, mine) for c in range(3)]
 
         def local_density(
-            pair_hbm, place_hbm, h_hbm, mass_hbm, energy_hbm, old_hbm, active_hbm, own_ref, right_ref,
-            centred_ref, pair_ref, active_ref, sems
+            pair_hbm, place_hbm, h_hbm, mass_hbm, energy_hbm, old_hbm, active_hbm, leaf_hbm, route_hbm,
+            own_ref, right_ref, centred_ref, right_by_ref, own_by_ref, pair_ref, active_ref, leaf_ref, route_ref, sems
         ):
             fetch(
                 sems,
@@ -206,6 +223,8 @@
                 (energy_hbm, own_ref.at[ENERGY]),
                 (old_hbm, own_ref.at[OLD]),
                 (active_hbm, active_ref),
+                (leaf_hbm, leaf_ref),
+                (route_hbm, route_ref),
             )
             h = own_ref[H]
             own_ref[ACTIVE] = active_ref[...].astype(f32)
@@ -229,6 +248,28 @@
                 right_ref[leaf] = right_terms(jnp.concatenate([item[at] for item in rights], axis=0))
                 centred_ref[leaf] = jnp.concatenate([item[at] for item in places], axis=0)
 
+            core = lax.axis_index("core")
+            me = lax.axis_index("chip") * 2 + core
+
+            def note(e):
+                mine, other = leaf_ref[0, e], leaf_ref[1, e]
+                target = me + 1 + route_ref[0, e]
+                target = jnp.where(target >= domains, target - domains, target)
+                chip = target // 2
+                spot = jnp.where(target - chip * 2 == core, chip, chip + chips) * leaves + other
+                at = pl.ds(e, 1)
+                sheet_of, within = e // leaves, pl.ds(e % leaves, 1)
+                for k, number in enumerate((spot, target * leaves + other, mine)):
+                    own_ref[TABLE + k * sheets + sheet_of, within, :] = jnp.full(
+                        (1, width), number.astype(f32)
+                    )
+                right_by_ref[e] = right_ref[mine]
+                own_by_ref[0, at, :] = row(own_ref, INVERSE, mine)
+                for c in range(3):
+                    own_by_ref[1 + c, at, :] = row(own_ref, ORIGIN + c, mine)
+
+            grouped(exports, note)
+
             def tile(e):
                 mine, other = pair_ref[0, e], pair_ref[1, e]
                 own_ref[SUM, pl.ds(mine, 1), :] = row(own_ref, SUM, mine) + density_tile(
@@ -240,19 +281,36 @@
 
             grouped(pairs, tile)
 
-        own, right, centred = call(
+        spots, sheets = domains * leaves, -(-exports // leaves)
+
+        def indices(own_ref, kind):
+            at = TABLE + kind * sheets
+            return own_ref[at : at + sheets].reshape(sheets * leaves, width)[:exports]
+
+        own, right, centred, right_by, own_by = call(
             local_density,
             "local_density",
             (
-                shape(TABLE, leaves, width),
+                shape(TABLE + 3 * sheets, leaves, width),
                 jax.ShapeDtypeStruct((leaves, 48, width), jnp.bfloat16),
-                shape(leaves, 8, width),
+                pltpu.HBM((leaves, 8, width), f32),
+                jax.ShapeDtypeStruct((exports, 48, width), jnp.bfloat16),
+                shape(4, exports, width),
             ),
-            [hbm] * 7,
-            [pair_table, pltpu.VMEM((leaves, width), s32), pltpu.SemaphoreType.DMA((7,))],
+            [hbm] * 9,
+            [
+                pair_table,
+                pltpu.VMEM((leaves, width), s32),
+                leaf_table,
+                route_table,
+                pltpu.SemaphoreType.DMA((9,)),
+            ],
             pairs * tile_flops * 30,
-            4,
-        )(pair_list, place, smoothing, mass, energy, old_density, active)
+            6 + exports * spots * 16 // MIB,
+        )(
+            pair_list, place, smoothing, mass, energy, old_density, active, export_leaves,
+            export_route,
+        )
         near, own = lax.optimization_barrier((near, own))
         peer = lax.ppermute(near, "core", [(0, 1), (1, 0)])
 
@@ -273,24 +331,29 @@
             return mine, spot, [get(c) for c in items]
 
         def remote_density(
-            leaf_hbm, route_hbm, own_ref, right_ref, near_ref, peer_ref, spread_ref, total, leaf_ref,
-            route_ref, sems
+            right_by_ref, own_by_ref, own_ref, near_ref, peer_ref, spread_ref, far_ref, rows_ref
         ):
-            fetch(sems, (leaf_hbm, leaf_ref), (route_hbm, route_ref))
-            total[...] = own_ref[SUM]
+            pick = flags(indices(own_ref, 0), spots)
+            owner = flags(indices(own_ref, 2), leaves)
+            for k, c in enumerate((0, 1, 2, 4)):
+                at = slice(c * leaves, (c + 1) * leaves)
+                data = [ref[:, at, :].reshape(spots // 2, width) for ref in (near_ref, peer_ref)]
+                far_ref[k] = select(pick, jnp.concatenate(data, axis=0))
+            for c in range(3):
+                far_ref[c] = far_ref[c] - own_by_ref[1 + c]
 
             def tile(e):
-                mine, spot, (far_mass,) = export(
-                    leaf_ref, route_ref, near_ref, peer_ref, own_ref, e, (4,)
-                )
-                at = pl.ds(mine, 1)
-                total[at, :] = total[at, :] + density_tile(
-                    right_ref[mine], row(own_ref, INVERSE, mine), spot, far_mass
+                rows_ref[pl.ds(e, 1), :] = density_tile(
+                    right_by_ref[e],
+                    row(own_by_ref, 0, e),
+                    [row(far_ref, c, e) for c in range(3)],
+                    row(far_ref, 3, e),
                 )
 
             grouped(exports, tile)
+            total = own_ref[SUM] + by_leaf(owner, rows_ref[...])
             inverse = own_ref[INVERSE]
-            summed = (total[...] + own_ref[MASS]) * (NORM * (inverse * inverse * inverse))
+            summed = (total + own_ref[MASS]) * (NORM * (inverse * inverse * inverse))
             density = jnp.where(own_ref[ACTIVE] == 1.0, summed, own_ref[OLD])
             term = (ADIABATIC - 1.0) * own_ref[ENERGY] / density
             for d in range(domains):
@@ -301,17 +364,17 @@
             remote_density,
             "remote_density",
             pltpu.HBM((domains, leaves, width), f32),
-            [hbm] * 2 + [vmem] * 4,
-            [sheet, leaf_table, route_table, pltpu.SemaphoreType.DMA((2,))],
+            [vmem] * 5,
+            [pltpu.VMEM((4, exports, width), f32), pltpu.VMEM((exports, width), f32)],
             exports * tile_flops * 30,
-            6 + wire_mib,
-        )(export_leaves, export_route, own, right, near, peer)
+            6 + 2 * wire_mib + exports * spots * 16 // MIB,
+        )(right_by, own_by, own, near, peer)
         terms = lax.all_to_all(outgoing, ("chip", "core"), split_axis=0, concat_axis=0, tiled=True)
 
         def prepare(
-            pair_hbm, leaf_hbm, route_hbm, spread_hbm, own_ref, right_ref, centred_ref, near_ref,
-            peer_ref, density_ref, sum_ref, weight_ref, moment_ref, pair_ref, leaf_ref, route_ref,
-            term_ref, sems
+            pair_hbm, leaf_hbm, route_hbm, spread_hbm, centred_hbm, own_ref, right_ref, near_ref,
+            peer_ref, density_ref, partial_ref, weight_ref, moment_ref, pair_ref, leaf_ref, route_ref,
+            term_ref, centred_ref, sum_ref, sems
         ):
             fetch(
                 sems,
@@ -319,6 +382,7 @@
                 (leaf_hbm, leaf_ref),
                 (route_hbm, route_ref),
                 (spread_hbm.at[0], term_ref),
+                (centred_hbm, centred_ref),
             )
             fresh = (ADIABATIC - 1.0) * own_ref[ENERGY] / term_ref[...]
             density_ref[...] = jnp.where(own_ref[ACTIVE] == 1.0, fresh, own_ref[OLD])
@@ -351,10 +415,14 @@
                     leaf_ref, route_ref, near_ref, peer_ref, own_ref, e, (3, 4)
                 )
                 weight_ref[e] = stack(weigh(mine, spot, 1.0 / h, slope_scale(h)))
-                moment_ref[e] = moments(far_mass, spot)
+                moment_ref[e, 0:8, :] = moments(far_mass, spot)
+                moment_ref[e, 8:16, :] = centred_ref[mine]
 
             grouped(pairs, local_tile)
             grouped(exports, remote_tile)
+            for c in range(3):
+                for leaf in range(leaves):
+                    partial_ref[c, leaf : leaf + 1, :] = sum_ref[leaf, c + 1 : c + 2, :]
 
         stash_mib = 2 * exports * width * (6 * width + 32) // MIB
         density, partial, weights, rows = call(
@@ -362,46 +430,54 @@
             "prepare_force",
             (
                 shape(leaves, width),
-                shape(leaves, 4, width),
+                pltpu.HBM((3, leaves, width), f32),
                 jax.ShapeDtypeStruct((exports, 3 * width, width), jnp.bfloat16),
-                pltpu.HBM((exports, 8, width), f32),
+                pltpu.HBM((exports, 16, width), f32),
             ),
-            [hbm] * 4 + [vmem] * 5,
-            [pair_table, leaf_table, route_table, sheet, pltpu.SemaphoreType.DMA((4,))],
+            [hbm] * 5 + [vmem] * 4,
+            [
+                pair_table,
+                leaf_table,
+                route_table,
+                sheet,
+                pltpu.VMEM((leaves, 8, width), f32),
+                pltpu.VMEM((leaves, 4, width), f32),
+                pltpu.SemaphoreType.DMA((5,)),
+            ],
             (pairs + exports) * tile_flops * 60,
             6 + stash_mib + wire_mib,
-        )(pair_list, export_leaves, export_route, kept(outgoing), own, right, centred, near, peer)
+        )(pair_list, export_leaves, export_route, kept(outgoing), kept(centred), own, right, near, peer)
 
         def finish(
-            leaf_hbm, route_hbm, moment_hbm, own_ref, centred_ref, terms_ref, partial_ref, weight_ref,
-            accel_ref, least_ref, total, leaf_ref, route_ref, moment_ref, sems
+            moment_hbm, partial_hbm, own_ref, terms_ref, weight_ref, accel_ref, least_ref, moment_ref,
+            partial_ref, far_ref, mine_ref, rows_ref, sems
         ):
-            fetch(
-                sems,
-                (leaf_hbm, leaf_ref),
-                (route_hbm, route_ref),
-                (moment_hbm, moment_ref),
-            )
-            total[...] = partial_ref[...]
+            copy = pltpu.make_async_copy(moment_hbm, moment_ref, sems.at[0])
+            later = pltpu.make_async_copy(partial_hbm, partial_ref, sems.at[1])
+            copy.start()
+            later.start()
+            owner = flags(indices(own_ref, 2), leaves)
             me = lax.axis_index("chip") * 2 + lax.axis_index("core")
+            far_ref[...] = select(flags(indices(own_ref, 1), spots), terms_ref[...].reshape(spots, width))
+            mine_ref[...] = select(owner, terms_ref[me])
+            copy.wait()
 
             def tile(e):
-                mine, other = leaf_ref[0, e], leaf_ref[1, e]
-                target = me + 1 + route_ref[0, e]
-                target = jnp.where(target >= domains, target - domains, target)
-                far_term = terms_ref[target, pl.ds(other, 1), :]
-                total[mine] = total[mine] + force(
+                at = pl.ds(e, 1)
+                part = force(
                     weight_ref[e],
-                    moment_ref[e],
-                    far_term,
-                    terms_ref[me, pl.ds(mine, 1), :],
-                    centred_ref[mine],
-                )
+                    moment_ref[e, 0:8, :],
+                    far_ref[at, :],
+                    mine_ref[at, :],
+                    moment_ref[e, 8:16, :],
+                )
+                for c in range(3):
+                    rows_ref[c, at, :] = part[c + 1 : c + 2]
 
             grouped(exports, tile)
+            later.wait()
             for c in range(3):
-                for leaf in range(leaves):
-                    accel_ref[c, leaf : leaf + 1, :] = total[leaf, c + 1 : c + 2, :]
+                accel_ref[c] = partial_ref[c] + by_leaf(owner, rows_ref[c])
             awake = own_ref[ACTIVE] == 1.0
             square = jnp.zeros((leaves, width), f32)
             for c in range(3):
@@ -419,17 +495,18 @@
             finish,
             "finish_force",
             (shape(3, leaves, width), shape(members, width)),
-            [hbm] * 3 + [vmem] * 5,
+            [hbm] * 2 + [vmem] * 3,
             [
-                pltpu.VMEM((leaves, 4, width), f32),
-                leaf_table,
-                route_table,
-                pltpu.VMEM((exports, 8, width), f32),
-                pltpu.SemaphoreType.DMA((3,)),
+                pltpu.VMEM((exports, 16, width), f32),
+                pltpu.VMEM((3, leaves, width), f32),
+                pltpu.VMEM((exports, width), f32),
+                pltpu.VMEM((exports, width), f32),
+                pltpu.VMEM((3, exports, width), f32),
+                pltpu.SemaphoreType.DMA((2,)),
             ],
             exports * tile_flops * 16,
-            6 + stash_mib + wire_mib,
-        )(export_leaves, export_route, kept(rows), own, centred, terms, partial, weights)
+            8 + stash_mib + wire_mib + exports * spots * 16 // MIB,
+        )(kept(rows), kept(partial), own, terms, weights)
 
         everywhere = lax.all_to_all(least, everyone, split_axis=0, concat_axis=0, tiled=True)
         return density, accel.transpose(1, 0, 2), jnp.min(everywhere)

time: 51 us -> 50.9 us (level)
  transfers between devices with their start and end apart: 3 -> 3, of which waited for: 3 -> 3; matrix products, arithmetic and copies ran while one was open for 0% -> 0% of each run, Pallas kernels for 23% -> 24%
where the time goes in v8:
time: 50.9 us; the launch traced here: 50.4 us
  Pallas kernels  18.3 us (36%)
  blocking collectives  12 us (24%)
  starting transfers between devices  11.1 us (22%)
  waiting for transfers between devices  7.77 us (15%)
  between operations  0.67 us (1%)
  other arithmetic  0.63 us (1%)
    all_to_all x1, blocking collectives, body(): lax.all_to_all(least, everyone, split_axis=0, concat_axis=0, tiled=True)  12 us
    all_to_all x1, starting transfers between devices, body(): lax.all_to_all(outgoing, 'chip', split_axis=0, concat_axis=0, tiled=True)  7.32 us
    pallas_call x1, Pallas kernels, body(): call(prepare, 'prepare_force', (shape(leaves, width), pltpu.HBM((3, leave...  6.99 us
    all_to_all x1, waiting for transfers between devices, body(): lax.all_to_all(outgoing, 'chip', split_axis=0, concat_axis=0, tiled=True)  5.24 us
    pallas_call x1, Pallas kernels, body(): call(local_density, 'local_density', (shape(TABLE + 3 * sheets, leaves, w...  5.05 us
    all_to_all x1, starting transfers between devices, body(): lax.all_to_all(outgoing, ('chip', 'core'), split_axis=0, concat_axis=0, t...  3.73 us
    pallas_call x1, Pallas kernels, body(): call(remote_density, 'remote_density', pltpu.HBM((domains, leaves, width)...  2.43 us
    pallas_call x1, Pallas kernels, body(): call(finish, 'finish_force', (shape(3, leaves, width), shape(members, wid...  2.28 us
  transfers between devices with their start and end apart: 3, of which 3 were waited for; matrix products, arithmetic and copies ran while one was open for 0% of the time, Pallas kernels for 24%

profile of v8, /device:TPU:0, one launch (start us, length us, event | category | flops | bytes accessed | tf_op | source)
XLA Modules:
  0.0 50.4 jit_solution(12724608056684471792)
XLA Ops:
  0.6 1.5 %copy_out.1 = f32[8,5,16,128]{3,2,1,0:T(8,128)} custom-call(f32[3,16,128]{2,1,0:T(8,128)} %bitcast.11, f32[16,128]{1,0:T(8,128)} %h_ref.1, f32[16,128]{1,0:T(8,128)} %mass_ref.1), custom_call_target="tpu_custom_call" | custom-call | tf_op jit(solution)/shard_map/copy_out/pallas_call | solution.py:193
  2.2 7.3 %all-to-all-start = ((f32[8,80,128]{2,1,0:T(8,128)}), f32[8,80,128]{2,1,0:T(8,128)S(1)}, u32[]{:S(2)}, u32[]{:S(2)}) async-start(f32[8,80,128]{2,1,0:T(8,128)} %bitcast.10), calls=%async_computation | async-start | bytes 655360 | tf_op jit(solution)/shard_map/all_to_all | solution.py:205
  9.5 5.1 %local_density.1 = (f32[20,16,128]{2,1,0:T(8,128)S(1)}, bf16[16,48,128]{2,1,0:T(8,128)(2,1)S(1)}, f32[16,8,128]{2,1,0:T(8,128)}, bf16[24,48,128]{2,1,0:T(8,128)(2,1)S(1)}, f32[4,24,128]{2,1,0:T(8,128)S(1)}) custom-call(s32[2,16]{1,0:T(2,128)} %bitcast.13, f32[3,16,128]{2,1,0:T(8,128)} %bitcast.12, f32[16,128]{1,0:T(8,128)} %h_ref.1, f32[16,128]{1,0:T(8,128)} %mass_ref.1, ...), custom_call_target="tpu_custom_call" | custom-call | flops 7864320 | bytes 65536 | tf_op jit(solution)/shard_map/local_density/pallas_call | solution.py:290
  14.6 5.2 %all-to-all-done.near_ref = f32[8,80,128]{2,1,0:T(8,128)S(1)} async-done(((f32[8,80,128]{2,1,0:T(8,128)}), f32[8,80,128]{2,1,0:T(8,128)S(1)}, u32[]{:S(2)}, u32[]{:S(2)}) %all-to-all-start) | async-done | bytes 327712 | tf_op jit(solution)/shard_map/all_to_all | solution.py:205
  19.8 0.0 collective-permute-start
  19.8 1.6 %collective-permute-done.peer_ref = f32[8,80,128]{2,1,0:T(8,128)S(1)} collective-permute-done((f32[8,80,128]{2,1,0:T(8,128)S(1)}, f32[8,80,128]{2,1,0:T(8,128)S(1)}, u32[]{:S(2)}, u32[]{:S(2)}) %collective-permute-start) | collective-permute-done | bytes 327712 | tf_op jit(solution)/shard_map/ppermute | solution.py:315
  21.4 2.4 %remote_density.1.spread_hbm = f32[16,16,128]{2,1,0:T(8,128)} custom-call(bf16[24,48,128]{2,1,0:T(8,128)(2,1)S(1)} %get-tuple-element.16.right_by_ref, f32[4,24,128]{2,1,0:T(8,128)S(1)} %get-tuple-element.17.own_by_ref, f32[20,16,128]{2,1,0:T(8,128)S(1)} %get-tuple-element.19.own_ref, f32[8,80,128]{2,1,0:T(8,128)S(1)} %all-to-all-done.near_ref, ...), custom_call_target="tpu_custom_call" | custom-call | flops 11796480 | bytes 65536 | tf_op jit(solution)/shard_map/remote_density/pallas_call | solution.py:363
  23.9 3.7 %all-to-all-start.1 = ((f32[16,16,128]{2,1,0:T(8,128)}), f32[16,16,128]{2,1,0:T(8,128)S(1)}, u32[]{:S(2)}, u32[]{:S(2)}) async-start(f32[16,16,128]{2,1,0:T(8,128)} %remote_density.1.spread_hbm), calls=%async_computation.1 | async-start | bytes 262144 | tf_op jit(solution)/shard_map/all_to_all | solution.py:372
  27.6 7.0 %prepare_force.1 = (f32[16,128]{1,0:T(8,128)}, f32[3,16,128]{2,1,0:T(8,128)}, bf16[24,384,128]{2,1,0:T(8,128)(2,1)S(1)}, f32[24,16,128]{2,1,0:T(8,128)}) custom-call(s32[2,16]{1,0:T(2,128)} %bitcast.14, s32[2,24]{1,0:T(2,128)} %bitcast.16, s32[1,24]{1,0:T(1,128)} %bitcast.18, f32[16,16,128]{2,1,0:T(8,128)} %remote_density.1.spread_hbm, ...), custom_call_target="tpu_custom_call" | custom-call | flops 39321600 | bytes 65536 | tf_op jit(solution)/shard_map/prepare_force/pallas_call | solution.py:428
  34.6 0.9 %all-to-all-done.1.terms_ref = f32[16,16,128]{2,1,0:T(8,128)S(1)} async-done(((f32[16,16,128]{2,1,0:T(8,128)}), f32[16,16,128]{2,1,0:T(8,128)S(1)}, u32[]{:S(2)}, u32[]{:S(2)}) %all-to-all-start.1) | async-done | bytes 131104 | tf_op jit(solution)/shard_map/all_to_all | solution.py:372
  35.5 2.3 %finish_force.1 = (f32[3,16,128]{2,1,0:T(8,128)}, f32[32,128]{1,0:T(8,128)S(1)}) custom-call(f32[24,16,128]{2,1,0:T(8,128)} %get-tuple-element.24.moment_hbm, f32[3,16,128]{2,1,0:T(8,128)} %get-tuple-element.25.partial_hbm, f32[20,16,128]{2,1,0:T(8,128)S(1)} %get-tuple-element.19.own_ref, f32[16,16,128]{2,1,0:T(8,128)S(1)} %all-to-all-done.1.terms_ref, ...), custom_call_target="tpu_custom_call" | custom-call | flops 6291456 | bytes 65536 | tf_op jit(solution)/shard_map/finish_force/pallas_call | solution.py:494
  37.8 12.0 %all_to_all.19 = f32[32,1,128]{2,1,0:T(1,128)S(1)} all-to-all(f32[32,1,128]{2,1,0:T(1,128)S(1)} %bitcast.9), channel_id=1, replica_groups=mesh['grp'=2,'chip'=8,'core'=2] {'grp','chip','core'}, dimensions={0} | all-to-all | bytes 32768 | tf_op jit(solution)/shard_map/all_to_all | solution.py:511
  49.8 0.6 %reduce_min.9 = f32[]{:T(128)} reduce(f32[32,1,128]{2,1,0:T(1,128)S(1)} %all_to_all.19, f32[]{:T(128)} %constant.0.clone.1), dimensions={0,1,2}, to_apply=%region_0.0 | reduce | flops 4095 | bytes 16392 | tf_op jit(solution)/shard_map/reduce_min | solution.py:512
Async XLA Ops:
  2.2 17.6 %all-to-all-start = ((f32[8,80,128]{2,1,0:T(8,128)}), f32[8,80,128]{2,1,0:T(8,128)S(1)}, u32[]{:S(2)}, u32[]{:S(2)}) async-start(f32[8,80,128]{2,1,0:T(8,128)} %bitcast.10), calls=%async_computation | async-start | bytes 655360 | tf_op jit(solution)/shard_map/all_to_all | solution.py:205
  19.8 1.6 %collective-permute-start = (f32[8,80,128]{2,1,0:T(8,128)S(1)}, f32[8,80,128]{2,1,0:T(8,128)S(1)}, u32[]{:S(2)}, u32[]{:S(2)}) collective-permute-start(f32[8,80,128]{2,1,0:T(8,128)S(1)} %all-to-all-done.near_ref), channel_id=1, source_target_pairs={{0,1},{1,0},{2,3},{3,2},{4,5},{5,4},{6,7},{7,6},{8,9},{9,8},{10,11... | collective-permute-start | bytes 983048 | tf_op jit(solution)/shard_map/ppermute | solution.py:315
  23.9 11.6 %all-to-all-start.1 = ((f32[16,16,128]{2,1,0:T(8,128)}), f32[16,16,128]{2,1,0:T(8,128)S(1)}, u32[]{:S(2)}, u32[]{:S(2)}) async-start(f32[16,16,128]{2,1,0:T(8,128)} %remote_density.1.spread_hbm), calls=%async_computation.1 | async-start | bytes 262144 | tf_op jit(solution)/shard_map/all_to_all | solution.py:372

commit v9 on v8

--- a/solution.py
+++ b/solution.py
@@ -10,6 +10,7 @@
 ADIABATIC = 5.0 / 3.0
 COURANT = 0.3
 GROUP = 24
+MOST = 2
 TINY = 1e-30
 NORM = 8.0 / math.pi
 MIB = 1 << 20
@@ -251,24 +252,34 @@
             core = lax.axis_index("core")
             me = lax.axis_index("chip") * 2 + core
 
-            def note(e):
+            own_ref[pl.ds(TABLE, 4 * sheets)] = jnp.full((4 * sheets, leaves, width), -1.0, f32)
+            right_by_ref[...] = jnp.zeros_like(right_by_ref)
+            own_by_ref[...] = jnp.zeros_like(own_by_ref)
+
+            def write(kind, at, number):
+                own_ref[TABLE + kind * sheets + at // leaves, pl.ds(at % leaves, 1), :] = jnp.full(
+                    (1, width), number.astype(f32)
+                )
+
+            def note(e, used):
                 mine, other = leaf_ref[0, e], leaf_ref[1, e]
                 target = me + 1 + route_ref[0, e]
                 target = jnp.where(target >= domains, target - domains, target)
                 chip = target // 2
-                spot = jnp.where(target - chip * 2 == core, chip, chip + chips) * leaves + other
-                at = pl.ds(e, 1)
-                sheet_of, within = e // leaves, pl.ds(e % leaves, 1)
-                for k, number in enumerate((spot, target * leaves + other, mine)):
-                    own_ref[TABLE + k * sheets + sheet_of, within, :] = jnp.full(
-                        (1, width), number.astype(f32)
-                    )
-                right_by_ref[e] = right_ref[mine]
+                same = (target - chip * 2 == core).astype(s32)
+                slot = jnp.where(same == 1, used[0], near_slots + used[1])
+                write(0, slot, chip * leaves + other)
+                write(1, e, target * leaves + other)
+                write(2, e, mine)
+                write(3, slot, mine)
+                at = pl.ds(slot, 1)
+                right_by_ref[slot] = right_ref[mine]
                 own_by_ref[0, at, :] = row(own_ref, INVERSE, mine)
                 for c in range(3):
                     own_by_ref[1 + c, at, :] = row(own_ref, ORIGIN + c, mine)
-
-            grouped(exports, note)
+                return used[0] + same, used[1] + 1 - same
+
+            lax.fori_loop(0, exports, note, (jnp.int32(0), jnp.int32(0)))
 
             def tile(e):
                 mine, other = pair_ref[0, e], pair_ref[1, e]
@@ -281,21 +292,24 @@
 
             grouped(pairs, tile)
 
-        spots, sheets = domains * leaves, -(-exports // leaves)
-
-        def indices(own_ref, kind):
+        near_slots = -(-min(exports, MOST * (chips - 1)) // 8) * 8
+        peer_slots = -(-min(exports, MOST * chips) // 8) * 8
+        slots = near_slots + peer_slots
+        spots, sheets = domains * leaves, -(-max(exports, slots) // leaves)
+
+        def indices(own_ref, kind, first, count):
             at = TABLE + kind * sheets
-            return own_ref[at : at + sheets].reshape(sheets * leaves, width)[:exports]
+            return own_ref[at : at + sheets].reshape(sheets * leaves, width)[first : first + count]
 
         own, right, centred, right_by, own_by = call(
             local_density,
             "local_density",
             (
-                shape(TABLE + 3 * sheets, leaves, width),
+                shape(TABLE + 4 * sheets, leaves, width),
                 jax.ShapeDtypeStruct((leaves, 48, width), jnp.bfloat16),
                 pltpu.HBM((leaves, 8, width), f32),
-                jax.ShapeDtypeStruct((exports, 48, width), jnp.bfloat16),
-                shape(4, exports, width),
+                jax.ShapeDtypeStruct((slots, 48, width), jnp.bfloat16),
+                shape(4, slots, width),
             ),
             [hbm] * 9,
             [
@@ -330,28 +344,48 @@
             spot = [get(c) - row(own_ref, ORIGIN + c, mine) for c in range(3)]
             return mine, spot, [get(c) for c in items]
 
-        def remote_density(
-            right_by_ref, own_by_ref, own_ref, near_ref, peer_ref, spread_ref, far_ref, rows_ref
-        ):
-            pick = flags(indices(own_ref, 0), spots)
-            owner = flags(indices(own_ref, 2), leaves)
+        def slot_density(first, count, right_by_ref, own_by_ref, own_ref, data_ref, far_ref, rows_ref):
+            pick = flags(indices(own_ref, 0, first, count), spots // 2)
+            owner = flags(indices(own_ref, 3, first, count), leaves)
             for k, c in enumerate((0, 1, 2, 4)):
-                at = slice(c * leaves, (c + 1) * leaves)
-                data = [ref[:, at, :].reshape(spots // 2, width) for ref in (near_ref, peer_ref)]
-                far_ref[k] = select(pick, jnp.concatenate(data, axis=0))
+                data = data_ref[:, c * leaves : (c + 1) * leaves, :].reshape(spots // 2, width)
+                far_ref[k] = select(pick, data)
             for c in range(3):
-                far_ref[c] = far_ref[c] - own_by_ref[1 + c]
+                far_ref[c] = far_ref[c] - own_by_ref[1 + c, first : first + count]
 
             def tile(e):
                 rows_ref[pl.ds(e, 1), :] = density_tile(
-                    right_by_ref[e],
-                    row(own_by_ref, 0, e),
+                    right_by_ref[first + e],
+                    row(own_by_ref, 0, first + e),
                     [row(far_ref, c, e) for c in range(3)],
                     row(far_ref, 3, e),
                 )
 
-            grouped(exports, tile)
-            total = own_ref[SUM] + by_leaf(owner, rows_ref[...])
+            grouped(count, tile)
+            return by_leaf(owner, rows_ref[...])
+
+        def near_density(right_by_ref, own_by_ref, own_ref, near_ref, sum_ref, far_ref, rows_ref):
+            sum_ref[...] = own_ref[SUM] + slot_density(
+                0, near_slots, right_by_ref, own_by_ref, own_ref, near_ref, far_ref, rows_ref
+            )
+
+        wire_mib = 2 * domains * leaves * width * 20 // MIB
+        near_sum = call(
+            near_density,
+            "near_density",
+            shape(leaves, width),
+            [vmem] * 4,
+            [pltpu.VMEM((4, near_slots, width), f32), pltpu.VMEM((near_slots, width), f32)],
+            near_slots * tile_flops * 30,
+            6 + wire_mib + exports * spots * 16 // MIB,
+        )(right_by, own_by, own, near)
+
+        def peer_density(
+            right_by_ref, own_by_ref, own_ref, sum_ref, peer_ref, spread_ref, far_ref, rows_ref
+        ):
+            total = sum_ref[...] + slot_density(
+                near_slots, peer_slots, right_by_ref, own_by_ref, own_ref, peer_ref, far_ref, rows_ref
+            )
             inverse = own_ref[INVERSE]
             summed = (total + own_ref[MASS]) * (NORM * (inverse * inverse * inverse))
             density = jnp.where(own_ref[ACTIVE] == 1.0, summed, own_ref[OLD])
@@ -359,16 +393,15 @@
             for d in range(domains):
                 spread_ref[d] = term
 
-        wire_mib = 2 * domains * leaves * width * 20 // MIB
         outgoing = call(
-            remote_density,
-            "remote_density",
+            peer_density,
+            "peer_density",
             pltpu.HBM((domains, leaves, width), f32),
             [vmem] * 5,
-            [pltpu.VMEM((4, exports, width), f32), pltpu.VMEM((exports, width), f32)],
-            exports * tile_flops * 30,
+            [pltpu.VMEM((4, peer_slots, width), f32), pltpu.VMEM((peer_slots, width), f32)],
+            peer_slots * tile_flops * 30,
             6 + 2 * wire_mib + exports * spots * 16 // MIB,
-        )(right_by, own_by, own, near, peer)
+        )(right_by, own_by, own, near_sum, peer)
         terms = lax.all_to_all(outgoing, ("chip", "core"), split_axis=0, concat_axis=0, tiled=True)
 
         def prepare(
@@ -449,16 +482,16 @@
         )(pair_list, export_leaves, export_route, kept(outgoing), kept(centred), own, right, near, peer)
 
         def finish(
-            moment_hbm, partial_hbm, own_ref, terms_ref, weight_ref, accel_ref, least_ref, moment_ref,
-            partial_ref, far_ref, mine_ref, rows_ref, sems
+            moment_hbm, partial_hbm, own_ref, terms_ref, weight_ref, accel_hbm, least_ref, accel_ref,
+            moment_ref, partial_ref, far_ref, mine_ref, rows_ref, sems
         ):
             copy = pltpu.make_async_copy(moment_hbm, moment_ref, sems.at[0])
             later = pltpu.make_async_copy(partial_hbm, partial_ref, sems.at[1])
             copy.start()
             later.start()
-            owner = flags(indices(own_ref, 2), leaves)
+            owner = flags(indices(own_ref, 2, 0, exports), leaves)
             me = lax.axis_index("chip") * 2 + lax.axis_index("core")
-            far_ref[...] = select(flags(indices(own_ref, 1), spots), terms_ref[...].reshape(spots, width))
+            far_ref[...] = select(flags(indices(own_ref, 1, 0, exports), spots), terms_ref[...].reshape(spots, width))
             mine_ref[...] = select(owner, terms_ref[me])
             copy.wait()
 
@@ -484,28 +517,34 @@
                 part = jnp.where(awake, accel_ref[c], 0.0)
                 accel_ref[c] = part
                 square = square + part * part
+            done = pltpu.make_async_copy(accel_ref, accel_hbm, sems.at[2])
+            done.start()
             h = own_ref[H]
             speed = jnp.sqrt(ADIABATIC * (ADIABATIC - 1.0) * own_ref[ENERGY])
             step = COURANT * h / (speed + jnp.sqrt(h * jnp.sqrt(square)))
             least_ref[...] = jnp.full(
                 (members, width), jnp.min(jnp.where(awake, step, jnp.inf)), f32
             )
-
-        accel, least = call(
+            done.wait()
+
+        accel, least = pl.pallas_call(
             finish,
-            "finish_force",
-            (shape(3, leaves, width), shape(members, width)),
-            [hbm] * 2 + [vmem] * 3,
-            [
+            out_shape=(pltpu.HBM((3, leaves, width), f32), shape(members, width)),
+            in_specs=[hbm] * 2 + [vmem] * 3,
+            out_specs=(hbm, vmem),
+            scratch_shapes=[
+                pltpu.VMEM((3, leaves, width), f32),
                 pltpu.VMEM((exports, 16, width), f32),
                 pltpu.VMEM((3, leaves, width), f32),
                 pltpu.VMEM((exports, width), f32),
                 pltpu.VMEM((exports, width), f32),
                 pltpu.VMEM((3, exports, width), f32),
-                pltpu.SemaphoreType.DMA((2,)),
+                pltpu.SemaphoreType.DMA((3,)),
             ],
-            exports * tile_flops * 16,
-            8 + stash_mib + wire_mib + exports * spots * 16 // MIB,
+            compiler_params=pltpu.CompilerParams(
+                vmem_limit_bytes=(8 + stash_mib + wire_mib + exports * spots * 16 // MIB) * MIB
+            ),
+            name="finish_force",
         )(kept(rows), kept(partial), own, terms, weights)
 
         everywhere = lax.all_to_all(least, everyone, split_axis=0, concat_axis=0, tiled=True)

time: 50.9 us -> 50.4 us (level)
  waiting for transfers between devices: 7.77 us -> 5.75 us
  Pallas kernels: 18.3 us -> 19.8 us
    pallas_call x3 -> x4, Pallas kernels: 9.76 us -> 11.3 us  [the longest x1 5.81 us: body(): call(local_density, 'local_density', (shape(TABLE + 4 * sheets, leaves, w...]
    ppermute x1, waiting for transfers between devices: 1.63 us -> 0.35 us  [body(): peer = lax.ppermute(near, 'core', [(0, 1), (1, 0)])]
    all_to_all x1, waiting for transfers between devices: 5.24 us -> 4.49 us  [body(): lax.all_to_all(outgoing, 'chip', split_axis=0, concat_axis=0, tiled=True)]
  transfers between devices with their start and end apart: 3 -> 3, of which waited for: 3 -> 3; matrix products, arithmetic and copies ran while one was open for 0% -> 0% of each run, Pallas kernels for 24% -> 28%
where the time goes in v9:
time: 50.4 us; the launch traced here: 49.9 us
  Pallas kernels  19.8 us (39%)
  blocking collectives  12 us (24%)
  starting transfers between devices  11 us (22%)
  waiting for transfers between devices  5.75 us (11%)
  between operations  0.67 us (1%)
  other arithmetic  0.63 us (1%)
    all_to_all x1, blocking collectives, body(): lax.all_to_all(least, everyone, split_axis=0, concat_axis=0, tiled=True)  12 us
    all_to_all x1, starting transfers between devices, body(): lax.all_to_all(outgoing, 'chip', split_axis=0, concat_axis=0, tiled=True)  7.32 us
    pallas_call x1, Pallas kernels, body(): call(prepare, 'prepare_force', (shape(leaves, width), pltpu.HBM((3, leave...  6.98 us
    pallas_call x1, Pallas kernels, body(): call(local_density, 'local_density', (shape(TABLE + 4 * sheets, leaves, w...  5.81 us
    all_to_all x1, waiting for transfers between devices, body(): lax.all_to_all(outgoing, 'chip', split_axis=0, concat_axis=0, tiled=True)  4.49 us
    all_to_all x1, starting transfers between devices, body(): lax.all_to_all(outgoing, ('chip', 'core'), split_axis=0, concat_axis=0, t...  3.72 us
    pallas_call x1, Pallas kernels, body(): pl.pallas_call(finish, out_shape=(pltpu.HBM((3, leaves, width), f32), sha...  2.29 us
    pallas_call x1, Pallas kernels, body(): call(peer_density, 'peer_density', pltpu.HBM((domains, leaves, width), f3...  1.95 us
  transfers between devices with their start and end apart: 3, of which 3 were waited for; matrix products, arithmetic and copies ran while one was open for 0% of the time, Pallas kernels for 28%

profile of v9, /device:TPU:0, one launch (start us, length us, event | category | flops | bytes accessed | tf_op | source)
XLA Modules:
  0.0 49.9 jit_solution(15923849120429870848)
XLA Ops:
  0.6 1.5 %copy_out.1 = f32[8,5,16,128]{3,2,1,0:T(8,128)} custom-call(f32[3,16,128]{2,1,0:T(8,128)} %bitcast.11, f32[16,128]{1,0:T(8,128)} %h_ref.1, f32[16,128]{1,0:T(8,128)} %mass_ref.1), custom_call_target="tpu_custom_call" | custom-call | tf_op jit(solution)/shard_map/copy_out/pallas_call | solution.py:194
  2.2 7.3 %all-to-all-start = ((f32[8,80,128]{2,1,0:T(8,128)}), f32[8,80,128]{2,1,0:T(8,128)S(1)}, u32[]{:S(2)}, u32[]{:S(2)}) async-start(f32[8,80,128]{2,1,0:T(8,128)} %bitcast.10), calls=%async_computation | async-start | bytes 655360 | tf_op jit(solution)/shard_map/all_to_all | solution.py:206
  9.5 5.8 %local_density.1 = (f32[22,16,128]{2,1,0:T(8,128)S(1)}, bf16[16,48,128]{2,1,0:T(8,128)(2,1)S(1)}, f32[16,8,128]{2,1,0:T(8,128)}, bf16[32,48,128]{2,1,0:T(8,128)(2,1)S(1)}, f32[4,32,128]{2,1,0:T(8,128)S(1)}) custom-call(s32[2,16]{1,0:T(2,128)} %bitcast.13, f32[3,16,128]{2,1,0:T(8,128)} %bitcast.12, f32[16,128]{1,0:T(8,128)} %h_ref.1, f32[16,128]{1,0:T(8,128)} %mass_ref.1, ...), custom_call_target="tpu_custom_call" | custom-call | flops 7864320 | bytes 65536 | tf_op jit(solution)/shard_map/local_density/pallas_call | solution.py:304
  15.3 4.5 %all-to-all-done.near_ref = f32[8,80,128]{2,1,0:T(8,128)S(1)} async-done(((f32[8,80,128]{2,1,0:T(8,128)}), f32[8,80,128]{2,1,0:T(8,128)S(1)}, u32[]{:S(2)}, u32[]{:S(2)}) %all-to-all-start) | async-done | bytes 327712 | tf_op jit(solution)/shard_map/all_to_all | solution.py:206
  19.8 0.0 collective-permute-start
  19.8 1.3 %near_density.1.sum_ref = f32[16,128]{1,0:T(8,128)S(1)} custom-call(bf16[32,48,128]{2,1,0:T(8,128)(2,1)S(1)} %get-tuple-element.16.right_by_ref, f32[4,32,128]{2,1,0:T(8,128)S(1)} %get-tuple-element.17.own_by_ref, f32[22,16,128]{2,1,0:T(8,128)S(1)} %get-tuple-element.19.own_ref, f32[8,80,128]{2,1,0:T(8,128)S(1)} %all-to-all-done.near_ref), custom_call_target="tpu_custom_call" | custom-call | flops 7864320 | bytes 65536 | tf_op jit(solution)/shard_map/near_density/pallas_call | solution.py:373
  21.1 0.4 collective-permute-done.peer_ref
  21.4 2.0 %peer_density.1.spread_hbm = f32[16,16,128]{2,1,0:T(8,128)} custom-call(bf16[32,48,128]{2,1,0:T(8,128)(2,1)S(1)} %get-tuple-element.16.right_by_ref, f32[4,32,128]{2,1,0:T(8,128)S(1)} %get-tuple-element.17.own_by_ref, f32[22,16,128]{2,1,0:T(8,128)S(1)} %get-tuple-element.19.own_ref, f32[16,128]{1,0:T(8,128)S(1)} %near_density.1.sum_ref, ...), custom_call_target="tpu_custom_call" | custom-call | flops 7864320 | bytes 65536 | tf_op jit(solution)/shard_map/peer_density/pallas_call | solution.py:396
  23.4 3.7 %all-to-all-start.1 = ((f32[16,16,128]{2,1,0:T(8,128)}), f32[16,16,128]{2,1,0:T(8,128)S(1)}, u32[]{:S(2)}, u32[]{:S(2)}) async-start(f32[16,16,128]{2,1,0:T(8,128)} %peer_density.1.spread_hbm), calls=%async_computation.1 | async-start | bytes 262144 | tf_op jit(solution)/shard_map/all_to_all | solution.py:405
  27.1 7.0 %prepare_force.1 = (f32[16,128]{1,0:T(8,128)}, f32[3,16,128]{2,1,0:T(8,128)}, bf16[24,384,128]{2,1,0:T(8,128)(2,1)S(1)}, f32[24,16,128]{2,1,0:T(8,128)}) custom-call(s32[2,16]{1,0:T(2,128)} %bitcast.14, s32[2,24]{1,0:T(2,128)} %bitcast.16, s32[1,24]{1,0:T(1,128)} %bitcast.18, f32[16,16,128]{2,1,0:T(8,128)} %peer_density.1.spread_hbm, ...), custom_call_target="tpu_custom_call" | custom-call | flops 39321600 | bytes 65536 | tf_op jit(solution)/shard_map/prepare_force/pallas_call | solution.py:461
  34.1 0.9 %all-to-all-done.1.terms_ref = f32[16,16,128]{2,1,0:T(8,128)S(1)} async-done(((f32[16,16,128]{2,1,0:T(8,128)}), f32[16,16,128]{2,1,0:T(8,128)S(1)}, u32[]{:S(2)}, u32[]{:S(2)}) %all-to-all-start.1) | async-done | bytes 131104 | tf_op jit(solution)/shard_map/all_to_all | solution.py:405
  35.0 2.3 %finish_force.1 = (f32[3,16,128]{2,1,0:T(8,128)}, f32[32,128]{1,0:T(8,128)S(1)}) custom-call(f32[24,16,128]{2,1,0:T(8,128)} %get-tuple-element.24.moment_hbm, f32[3,16,128]{2,1,0:T(8,128)} %get-tuple-element.25.partial_hbm, f32[22,16,128]{2,1,0:T(8,128)S(1)} %get-tuple-element.19.own_ref, f32[16,16,128]{2,1,0:T(8,128)S(1)} %all-to-all-done.1.terms_ref, ...), custom_call_target="tpu_custom_call" | custom-call | tf_op jit(solution)/shard_map/finish_force/pallas_call | solution.py:530
  37.3 12.0 %all_to_all.19 = f32[32,1,128]{2,1,0:T(1,128)S(1)} all-to-all(f32[32,1,128]{2,1,0:T(1,128)S(1)} %bitcast.9), channel_id=1, replica_groups=mesh['grp'=2,'chip'=8,'core'=2] {'grp','chip','core'}, dimensions={0} | all-to-all | bytes 32768 | tf_op jit(solution)/shard_map/all_to_all | solution.py:550
  49.3 0.6 %reduce_min.9 = f32[]{:T(128)} reduce(f32[32,1,128]{2,1,0:T(1,128)S(1)} %all_to_all.19, f32[]{:T(128)} %constant.0.clone.1), dimensions={0,1,2}, to_apply=%region_0.0 | reduce | flops 4095 | bytes 16392 | tf_op jit(solution)/shard_map/reduce_min | solution.py:551
Async XLA Ops:
  2.2 17.6 %all-to-all-start = ((f32[8,80,128]{2,1,0:T(8,128)}), f32[8,80,128]{2,1,0:T(8,128)S(1)}, u32[]{:S(2)}, u32[]{:S(2)}) async-start(f32[8,80,128]{2,1,0:T(8,128)} %bitcast.10), calls=%async_computation | async-start | bytes 655360 | tf_op jit(solution)/shard_map/all_to_all | solution.py:206
  19.8 1.6 %collective-permute-start = (f32[8,80,128]{2,1,0:T(8,128)S(1)}, f32[8,80,128]{2,1,0:T(8,128)S(1)}, u32[]{:S(2)}, u32[]{:S(2)}) collective-permute-start(f32[8,80,128]{2,1,0:T(8,128)S(1)} %all-to-all-done.near_ref), channel_id=1, source_target_pairs={{0,1},{1,0},{2,3},{3,2},{4,5},{5,4},{6,7},{7,6},{8,9},{9,8},{10,11... | collective-permute-start | bytes 983048 | tf_op jit(solution)/shard_map/ppermute | solution.py:329
  23.4 11.6 %all-to-all-start.1 = ((f32[16,16,128]{2,1,0:T(8,128)}), f32[16,16,128]{2,1,0:T(8,128)S(1)}, u32[]{:S(2)}, u32[]{:S(2)}) async-start(f32[16,16,128]{2,1,0:T(8,128)} %peer_density.1.spread_hbm), calls=%async_computation.1 | async-start | bytes 262144 | tf_op jit(solution)/shard_map/all_to_all | solution.py:405

commit v10 on v9

--- a/solution.py
+++ b/solution.py
@@ -306,7 +306,7 @@
             "local_density",
             (
                 shape(TABLE + 4 * sheets, leaves, width),
-                jax.ShapeDtypeStruct((leaves, 48, width), jnp.bfloat16),
+                pltpu.HBM((leaves, 48, width), jnp.bfloat16),
                 pltpu.HBM((leaves, 8, width), f32),
                 jax.ShapeDtypeStruct((slots, 48, width), jnp.bfloat16),
                 shape(4, slots, width),
@@ -405,9 +405,9 @@
         terms = lax.all_to_all(outgoing, ("chip", "core"), split_axis=0, concat_axis=0, tiled=True)
 
         def prepare(
-            pair_hbm, leaf_hbm, route_hbm, spread_hbm, centred_hbm, own_ref, right_ref, near_ref,
-            peer_ref, density_ref, partial_ref, weight_ref, moment_ref, pair_ref, leaf_ref, route_ref,
-            term_ref, centred_ref, sum_ref, sems
+            pair_hbm, leaf_hbm, route_hbm, spread_hbm, centred_hbm, right_hbm, own_ref, near_ref,
+            peer_ref, density_ref, partial_ref, weight_ref, pair_ref, leaf_ref, route_ref,
+            term_ref, centred_ref, right_ref, sum_ref, sems
         ):
             fetch(
                 sems,
@@ -416,6 +416,7 @@
                 (route_hbm, route_ref),
                 (spread_hbm.at[0], term_ref),
                 (centred_hbm, centred_ref),
+                (right_hbm, right_ref),
             )
             fresh = (ADIABATIC - 1.0) * own_ref[ENERGY] / term_ref[...]
             density_ref[...] = jnp.where(own_ref[ACTIVE] == 1.0, fresh, own_ref[OLD])
@@ -447,9 +448,9 @@
                 mine, spot, (h, far_mass) = export(
                     leaf_ref, route_ref, near_ref, peer_ref, own_ref, e, (3, 4)
                 )
-                weight_ref[e] = stack(weigh(mine, spot, 1.0 / h, slope_scale(h)))
-                moment_ref[e, 0:8, :] = moments(far_mass, spot)
-                moment_ref[e, 8:16, :] = centred_ref[mine]
+                weight_ref[e, : 3 * width, :] = stack(weigh(mine, spot, 1.0 / h, slope_scale(h)))
+                extra = [far_mass] + [far_mass * item for item in spot] + [centred_ref[mine][:4]]
+                weight_ref[e, 3 * width :, :] = stack(jnp.concatenate(extra, axis=0))
 
             grouped(pairs, local_tile)
             grouped(exports, remote_tile)
@@ -458,51 +459,50 @@
                     partial_ref[c, leaf : leaf + 1, :] = sum_ref[leaf, c + 1 : c + 2, :]
 
         stash_mib = 2 * exports * width * (6 * width + 32) // MIB
-        density, partial, weights, rows = call(
+        density, partial, weights = call(
             prepare,
             "prepare_force",
             (
                 shape(leaves, width),
                 pltpu.HBM((3, leaves, width), f32),
-                jax.ShapeDtypeStruct((exports, 3 * width, width), jnp.bfloat16),
-                pltpu.HBM((exports, 16, width), f32),
+                jax.ShapeDtypeStruct((exports, 3 * width + 24, width), jnp.bfloat16),
             ),
-            [hbm] * 5 + [vmem] * 4,
+            [hbm] * 6 + [vmem] * 3,
             [
                 pair_table,
                 leaf_table,
                 route_table,
                 sheet,
                 pltpu.VMEM((leaves, 8, width), f32),
+                pltpu.VMEM((leaves, 48, width), jnp.bfloat16),
                 pltpu.VMEM((leaves, 4, width), f32),
-                pltpu.SemaphoreType.DMA((5,)),
+                pltpu.SemaphoreType.DMA((6,)),
             ],
             (pairs + exports) * tile_flops * 60,
             6 + stash_mib + wire_mib,
-        )(pair_list, export_leaves, export_route, kept(outgoing), kept(centred), own, right, near, peer)
+        )(pair_list, export_leaves, export_route, kept(outgoing), kept(centred), kept(right), own, near, peer)
 
         def finish(
-            moment_hbm, partial_hbm, own_ref, terms_ref, weight_ref, accel_hbm, least_ref, accel_ref,
-            moment_ref, partial_ref, far_ref, mine_ref, rows_ref, sems
+            partial_hbm, own_ref, terms_ref, weight_ref, accel_hbm, least_ref, accel_ref, partial_ref,
+            far_ref, mine_ref, rows_ref, sems
         ):
-            copy = pltpu.make_async_copy(moment_hbm, moment_ref, sems.at[0])
-            later = pltpu.make_async_copy(partial_hbm, partial_ref, sems.at[1])
-            copy.start()
+            later = pltpu.make_async_copy(partial_hbm, partial_ref, sems.at[0])
             later.start()
             owner = flags(indices(own_ref, 2, 0, exports), leaves)
             me = lax.axis_index("chip") * 2 + lax.axis_index("core")
             far_ref[...] = select(flags(indices(own_ref, 1, 0, exports), spots), terms_ref[...].reshape(spots, width))
             mine_ref[...] = select(owner, terms_ref[me])
-            copy.wait()
 
             def tile(e):
                 at = pl.ds(e, 1)
+                parts = weight_ref[e, 3 * width :, :].astype(f32)
+                extra = parts[:8] + parts[8:16] + parts[16:]
                 part = force(
-                    weight_ref[e],
-                    moment_ref[e, 0:8, :],
+                    weight_ref[e, : 3 * width, :],
+                    jnp.concatenate([extra[:4], extra[:4]], axis=0),
                     far_ref[at, :],
                     mine_ref[at, :],
-                    moment_ref[e, 8:16, :],
+                    extra[4:],
                 )
                 for c in range(3):
                     rows_ref[c, at, :] = part[c + 1 : c + 2]
@@ -517,7 +517,7 @@
                 part = jnp.where(awake, accel_ref[c], 0.0)
                 accel_ref[c] = part
                 square = square + part * part
-            done = pltpu.make_async_copy(accel_ref, accel_hbm, sems.at[2])
+            done = pltpu.make_async_copy(accel_ref, accel_hbm, sems.at[1])
             done.start()
             h = own_ref[H]
             speed = jnp.sqrt(ADIABATIC * (ADIABATIC - 1.0) * own_ref[ENERGY])
@@ -530,22 +530,21 @@
         accel, least = pl.pallas_call(
             finish,
             out_shape=(pltpu.HBM((3, leaves, width), f32), shape(members, width)),
-            in_specs=[hbm] * 2 + [vmem] * 3,
+            in_specs=[hbm] + [vmem] * 3,
             out_specs=(hbm, vmem),
             scratch_shapes=[
                 pltpu.VMEM((3, leaves, width), f32),
-                pltpu.VMEM((exports, 16, width), f32),
                 pltpu.VMEM((3, leaves, width), f32),
                 pltpu.VMEM((exports, width), f32),
                 pltpu.VMEM((exports, width), f32),
                 pltpu.VMEM((3, exports, width), f32),
-                pltpu.SemaphoreType.DMA((3,)),
+                pltpu.SemaphoreType.DMA((2,)),
             ],
             compiler_params=pltpu.CompilerParams(
                 vmem_limit_bytes=(8 + stash_mib + wire_mib + exports * spots * 16 // MIB) * MIB
             ),
             name="finish_force",
-        )(kept(rows), kept(partial), own, terms, weights)
+        )(kept(partial), own, terms, weights)
 
         everywhere = lax.all_to_all(least, everyone, split_axis=0, concat_axis=0, tiled=True)
         return density, accel.transpose(1, 0, 2), jnp.min(everywhere)

time: 50.4 us -> 50.4 us (level)
  no operation moved by 1% of the time
where the time goes in v10:
time: 50.4 us; the launch traced here: 49.9 us
  Pallas kernels  19.7 us (39%)
  blocking collectives  12.1 us (24%)
  starting transfers between devices  11 us (22%)
  waiting for transfers between devices  5.73 us (11%)
  between operations  0.67 us (1%)
  other arithmetic  0.63 us (1%)
    all_to_all x1, blocking collectives, body(): lax.all_to_all(least, everyone, split_axis=0, concat_axis=0, tiled=True)  12.1 us
    all_to_all x1, starting transfers between devices, body(): lax.all_to_all(outgoing, 'chip', split_axis=0, concat_axis=0, tiled=True)  7.32 us
    pallas_call x1, Pallas kernels, body(): call(prepare, 'prepare_force', (shape(leaves, width), pltpu.HBM((3, leave...  7.13 us
    pallas_call x1, Pallas kernels, body(): call(local_density, 'local_density', (shape(TABLE + 4 * sheets, leaves, w...  5.68 us
    all_to_all x1, waiting for transfers between devices, body(): lax.all_to_all(outgoing, 'chip', split_axis=0, concat_axis=0, tiled=True)  4.61 us
    all_to_all x1, starting transfers between devices, body(): lax.all_to_all(outgoing, ('chip', 'core'), split_axis=0, concat_axis=0, t...  3.72 us
    pallas_call x1, Pallas kernels, body(): pl.pallas_call(finish, out_shape=(pltpu.HBM((3, leaves, width), f32), sha...  2.09 us
    pallas_call x1, Pallas kernels, body(): call(peer_density, 'peer_density', pltpu.HBM((domains, leaves, width), f3...  1.94 us
  transfers between devices with their start and end apart: 3, of which 3 were waited for; matrix products, arithmetic and copies ran while one was open for 0% of the time, Pallas kernels for 28%

profile of v10, /device:TPU:0, one launch (start us, length us, event | category | flops | bytes accessed | tf_op | source)
XLA Modules:
  0.0 49.9 jit_solution(773359136720786487)
XLA Ops:
  0.6 1.5 %copy_out.1 = f32[8,5,16,128]{3,2,1,0:T(8,128)} custom-call(f32[3,16,128]{2,1,0:T(8,128)} %bitcast.11, f32[16,128]{1,0:T(8,128)} %h_ref.1, f32[16,128]{1,0:T(8,128)} %mass_ref.1), custom_call_target="tpu_custom_call" | custom-call | tf_op jit(solution)/shard_map/copy_out/pallas_call | solution.py:194
  2.2 7.3 %all-to-all-start = ((f32[8,80,128]{2,1,0:T(8,128)}), f32[8,80,128]{2,1,0:T(8,128)S(1)}, u32[]{:S(2)}, u32[]{:S(2)}) async-start(f32[8,80,128]{2,1,0:T(8,128)} %bitcast.10), calls=%async_computation | async-start | bytes 655360 | tf_op jit(solution)/shard_map/all_to_all | solution.py:206
  9.5 5.7 %local_density.1 = (f32[22,16,128]{2,1,0:T(8,128)S(1)}, bf16[16,48,128]{2,1,0:T(8,128)(2,1)}, f32[16,8,128]{2,1,0:T(8,128)}, bf16[32,48,128]{2,1,0:T(8,128)(2,1)S(1)}, f32[4,32,128]{2,1,0:T(8,128)S(1)}) custom-call(s32[2,16]{1,0:T(2,128)} %bitcast.13, f32[3,16,128]{2,1,0:T(8,128)} %bitcast.12, f32[16,128]{1,0:T(8,128)} %h_ref.1, f32[16,128]{1,0:T(8,128)} %mass_ref.1, ...), custom_call_target="tpu_custom_call" | custom-call | flops 7864320 | bytes 65536 | tf_op jit(solution)/shard_map/local_density/pallas_call | solution.py:304
  15.2 4.6 %all-to-all-done.near_ref = f32[8,80,128]{2,1,0:T(8,128)S(1)} async-done(((f32[8,80,128]{2,1,0:T(8,128)}), f32[8,80,128]{2,1,0:T(8,128)S(1)}, u32[]{:S(2)}, u32[]{:S(2)}) %all-to-all-start) | async-done | bytes 327712 | tf_op jit(solution)/shard_map/all_to_all | solution.py:206
  19.8 0.0 collective-permute-start
  19.8 1.3 %near_density.1.sum_ref = f32[16,128]{1,0:T(8,128)S(1)} custom-call(bf16[32,48,128]{2,1,0:T(8,128)(2,1)S(1)} %get-tuple-element.15.right_by_ref, f32[4,32,128]{2,1,0:T(8,128)S(1)} %get-tuple-element.16.own_by_ref, f32[22,16,128]{2,1,0:T(8,128)S(1)} %get-tuple-element.18.own_ref, f32[8,80,128]{2,1,0:T(8,128)S(1)} %all-to-all-done.near_ref), custom_call_target="tpu_custom_call" | custom-call | flops 7864320 | bytes 65536 | tf_op jit(solution)/shard_map/near_density/pallas_call | solution.py:373
  21.1 0.4 collective-permute-done.peer_ref
  21.4 1.9 %peer_density.1.spread_hbm = f32[16,16,128]{2,1,0:T(8,128)} custom-call(bf16[32,48,128]{2,1,0:T(8,128)(2,1)S(1)} %get-tuple-element.15.right_by_ref, f32[4,32,128]{2,1,0:T(8,128)S(1)} %get-tuple-element.16.own_by_ref, f32[22,16,128]{2,1,0:T(8,128)S(1)} %get-tuple-element.18.own_ref, f32[16,128]{1,0:T(8,128)S(1)} %near_density.1.sum_ref, ...), custom_call_target="tpu_custom_call" | custom-call | flops 7864320 | bytes 65536 | tf_op jit(solution)/shard_map/peer_density/pallas_call | solution.py:396
  23.4 3.7 %all-to-all-start.1 = ((f32[16,16,128]{2,1,0:T(8,128)}), f32[16,16,128]{2,1,0:T(8,128)S(1)}, u32[]{:S(2)}, u32[]{:S(2)}) async-start(f32[16,16,128]{2,1,0:T(8,128)} %peer_density.1.spread_hbm), calls=%async_computation.1 | async-start | bytes 262144 | tf_op jit(solution)/shard_map/all_to_all | solution.py:405
  27.1 7.1 %prepare_force.1 = (f32[16,128]{1,0:T(8,128)}, f32[3,16,128]{2,1,0:T(8,128)}, bf16[24,408,128]{2,1,0:T(8,128)(2,1)S(1)}) custom-call(s32[2,16]{1,0:T(2,128)} %bitcast.14, s32[2,24]{1,0:T(2,128)} %bitcast.16, s32[1,24]{1,0:T(1,128)} %bitcast.18, f32[16,16,128]{2,1,0:T(8,128)} %peer_density.1.spread_hbm, f32[16,8,128]{2,1,0:T(8,128)} %get-tuple-element.20.centred_hbm, ...), custom_call_target="tpu_custom_call" | custom-call | flops 39321600 | bytes 65536 | tf_op jit(solution)/shard_map/prepare_force/pallas_call | solution.py:462
  34.2 0.8 %all-to-all-done.1.terms_ref = f32[16,16,128]{2,1,0:T(8,128)S(1)} async-done(((f32[16,16,128]{2,1,0:T(8,128)}), f32[16,16,128]{2,1,0:T(8,128)S(1)}, u32[]{:S(2)}, u32[]{:S(2)}) %all-to-all-start.1) | async-done | bytes 131104 | tf_op jit(solution)/shard_map/all_to_all | solution.py:405
  35.0 2.1 %finish_force.1 = (f32[3,16,128]{2,1,0:T(8,128)}, f32[32,128]{1,0:T(8,128)S(1)}) custom-call(f32[3,16,128]{2,1,0:T(8,128)} %get-tuple-element.23.partial_hbm, f32[22,16,128]{2,1,0:T(8,128)S(1)} %get-tuple-element.18.own_ref, f32[16,16,128]{2,1,0:T(8,128)S(1)} %all-to-all-done.1.terms_ref, bf16[24,408,128]{2,1,0:T(8,128)(2,1)S(1)} %get-tuple-element.24.weight_ref), custom_call_target="tpu_custom_call" | custom-call | tf_op jit(solution)/shard_map/finish_force/pallas_call | solution.py:530
  37.1 12.1 %all_to_all.19 = f32[32,1,128]{2,1,0:T(1,128)S(1)} all-to-all(f32[32,1,128]{2,1,0:T(1,128)S(1)} %bitcast.9), channel_id=1, replica_groups=mesh['grp'=2,'chip'=8,'core'=2] {'grp','chip','core'}, dimensions={0} | all-to-all | bytes 32768 | tf_op jit(solution)/shard_map/all_to_all | solution.py:549
  49.2 0.6 %reduce_min.9 = f32[]{:T(128)} reduce(f32[32,1,128]{2,1,0:T(1,128)S(1)} %all_to_all.19, f32[]{:T(128)} %constant.0.clone.1), dimensions={0,1,2}, to_apply=%region_0.0 | reduce | flops 4095 | bytes 16392 | tf_op jit(solution)/shard_map/reduce_min | solution.py:550
Async XLA Ops:
  2.2 17.6 %all-to-all-start = ((f32[8,80,128]{2,1,0:T(8,128)}), f32[8,80,128]{2,1,0:T(8,128)S(1)}, u32[]{:S(2)}, u32[]{:S(2)}) async-start(f32[8,80,128]{2,1,0:T(8,128)} %bitcast.10), calls=%async_computation | async-start | bytes 655360 | tf_op jit(solution)/shard_map/all_to_all | solution.py:206
  19.8 1.6 %collective-permute-start = (f32[8,80,128]{2,1,0:T(8,128)S(1)}, f32[8,80,128]{2,1,0:T(8,128)S(1)}, u32[]{:S(2)}, u32[]{:S(2)}) collective-permute-start(f32[8,80,128]{2,1,0:T(8,128)S(1)} %all-to-all-done.near_ref), channel_id=1, source_target_pairs={{0,1},{1,0},{2,3},{3,2},{4,5},{5,4},{6,7},{7,6},{8,9},{9,8},{10,11... | collective-permute-start | bytes 983048 | tf_op jit(solution)/shard_map/ppermute | solution.py:329
  23.4 11.6 %all-to-all-start.1 = ((f32[16,16,128]{2,1,0:T(8,128)}), f32[16,16,128]{2,1,0:T(8,128)S(1)}, u32[]{:S(2)}, u32[]{:S(2)}) async-start(f32[16,16,128]{2,1,0:T(8,128)} %peer_density.1.spread_hbm), calls=%async_computation.1 | async-start | bytes 262144 | tf_op jit(solution)/shard_map/all_to_all | solution.py:405

commit v11 on v10

--- a/solution.py
+++ b/solution.py
@@ -381,7 +381,7 @@
         )(right_by, own_by, own, near)
 
         def peer_density(
-            right_by_ref, own_by_ref, own_ref, sum_ref, peer_ref, spread_ref, far_ref, rows_ref
+            right_by_ref, own_by_ref, own_ref, sum_ref, peer_ref, spread_ref, far_ref, rows_ref, term_ref, sems
         ):
             total = sum_ref[...] + slot_density(
                 near_slots, peer_slots, right_by_ref, own_by_ref, own_ref, peer_ref, far_ref, rows_ref
@@ -390,17 +390,24 @@
             summed = (total + own_ref[MASS]) * (NORM * (inverse * inverse * inverse))
             density = jnp.where(own_ref[ACTIVE] == 1.0, summed, own_ref[OLD])
             term = (ADIABATIC - 1.0) * own_ref[ENERGY] / density
-            for d in range(domains):
-                spread_ref[d] = term
-
-        outgoing = call(
+            term_ref[...] = term
+            fetch(sems, *[(term_ref, spread_ref.at[d]) for d in range(domains)])
+
+        outgoing = pl.pallas_call(
             peer_density,
-            "peer_density",
-            pltpu.HBM((domains, leaves, width), f32),
-            [vmem] * 5,
-            [pltpu.VMEM((4, peer_slots, width), f32), pltpu.VMEM((peer_slots, width), f32)],
-            peer_slots * tile_flops * 30,
-            6 + 2 * wire_mib + exports * spots * 16 // MIB,
+            out_shape=pltpu.HBM((domains, leaves, width), f32),
+            in_specs=[vmem] * 5,
+            out_specs=hbm,
+            scratch_shapes=[
+                pltpu.VMEM((4, peer_slots, width), f32),
+                pltpu.VMEM((peer_slots, width), f32),
+                sheet,
+                pltpu.SemaphoreType.DMA((domains,)),
+            ],
+            compiler_params=pltpu.CompilerParams(
+                vmem_limit_bytes=(6 + 2 * wire_mib + exports * spots * 16 // MIB) * MIB
+            ),
+            name="peer_density",
         )(right_by, own_by, own, near_sum, peer)
         terms = lax.all_to_all(outgoing, ("chip", "core"), split_axis=0, concat_axis=0, tiled=True)
 

time: 50.4 us -> 50.6 us (level)
  no operation moved by 1% of the time
where the time goes in v11:
time: 50.6 us; the launch traced here: 50 us
  Pallas kernels  19.8 us (39%)
  blocking collectives  12.1 us (24%)
  starting transfers between devices  11.1 us (22%)
  waiting for transfers between devices  5.73 us (11%)
  between operations  0.68 us (1%)
  other arithmetic  0.63 us (1%)
    all_to_all x1, blocking collectives, body(): lax.all_to_all(least, everyone, split_axis=0, concat_axis=0, tiled=True)  12.1 us
    all_to_all x1, starting transfers between devices, body(): lax.all_to_all(outgoing, 'chip', split_axis=0, concat_axis=0, tiled=True)  7.32 us
    pallas_call x1, Pallas kernels, body(): call(prepare, 'prepare_force', (shape(leaves, width), pltpu.HBM((3, leave...  7.13 us
    pallas_call x1, Pallas kernels, body(): call(local_density, 'local_density', (shape(TABLE + 4 * sheets, leaves, w...  5.68 us
    all_to_all x1, waiting for transfers between devices, body(): lax.all_to_all(outgoing, 'chip', split_axis=0, concat_axis=0, tiled=True)  4.61 us
    all_to_all x1, starting transfers between devices, body(): lax.all_to_all(outgoing, ('chip', 'core'), split_axis=0, concat_axis=0, t...  3.73 us
    pallas_call x1, Pallas kernels, body(): pl.pallas_call(finish, out_shape=(pltpu.HBM((3, leaves, width), f32), sha...  2.09 us
    pallas_call x1, Pallas kernels, body(): pl.pallas_call(peer_density, out_shape=pltpu.HBM((domains, leaves, width)...  2.09 us
  transfers between devices with their start and end apart: 3, of which 3 were waited for; matrix products, arithmetic and copies ran while one was open for 0% of the time, Pallas kernels for 28%

profile of v11, /device:TPU:0, one launch (start us, length us, event | category | flops | bytes accessed | tf_op | source)
XLA Modules:
  0.0 50.0 jit_solution(3903680515947796783)
XLA Ops:
  0.6 1.5 %copy_out.1 = f32[8,5,16,128]{3,2,1,0:T(8,128)} custom-call(f32[3,16,128]{2,1,0:T(8,128)} %bitcast.11, f32[16,128]{1,0:T(8,128)} %h_ref.1, f32[16,128]{1,0:T(8,128)} %mass_ref.1), custom_call_target="tpu_custom_call" | custom-call | tf_op jit(solution)/shard_map/copy_out/pallas_call | solution.py:194
  2.2 7.3 %all-to-all-start = ((f32[8,80,128]{2,1,0:T(8,128)}), f32[8,80,128]{2,1,0:T(8,128)S(1)}, u32[]{:S(2)}, u32[]{:S(2)}) async-start(f32[8,80,128]{2,1,0:T(8,128)} %bitcast.10), calls=%async_computation | async-start | bytes 655360 | tf_op jit(solution)/shard_map/all_to_all | solution.py:206
  9.5 5.7 %local_density.1 = (f32[22,16,128]{2,1,0:T(8,128)S(1)}, bf16[16,48,128]{2,1,0:T(8,128)(2,1)}, f32[16,8,128]{2,1,0:T(8,128)}, bf16[32,48,128]{2,1,0:T(8,128)(2,1)S(1)}, f32[4,32,128]{2,1,0:T(8,128)S(1)}) custom-call(s32[2,16]{1,0:T(2,128)} %bitcast.13, f32[3,16,128]{2,1,0:T(8,128)} %bitcast.12, f32[16,128]{1,0:T(8,128)} %h_ref.1, f32[16,128]{1,0:T(8,128)} %mass_ref.1, ...), custom_call_target="tpu_custom_call" | custom-call | flops 7864320 | bytes 65536 | tf_op jit(solution)/shard_map/local_density/pallas_call | solution.py:304
  15.2 4.6 %all-to-all-done.near_ref = f32[8,80,128]{2,1,0:T(8,128)S(1)} async-done(((f32[8,80,128]{2,1,0:T(8,128)}), f32[8,80,128]{2,1,0:T(8,128)S(1)}, u32[]{:S(2)}, u32[]{:S(2)}) %all-to-all-start) | async-done | bytes 327712 | tf_op jit(solution)/shard_map/all_to_all | solution.py:206
  19.8 0.0 collective-permute-start
  19.8 1.3 %near_density.1.sum_ref = f32[16,128]{1,0:T(8,128)S(1)} custom-call(bf16[32,48,128]{2,1,0:T(8,128)(2,1)S(1)} %get-tuple-element.15.right_by_ref, f32[4,32,128]{2,1,0:T(8,128)S(1)} %get-tuple-element.16.own_by_ref, f32[22,16,128]{2,1,0:T(8,128)S(1)} %get-tuple-element.18.own_ref, f32[8,80,128]{2,1,0:T(8,128)S(1)} %all-to-all-done.near_ref), custom_call_target="tpu_custom_call" | custom-call | flops 7864320 | bytes 65536 | tf_op jit(solution)/shard_map/near_density/pallas_call | solution.py:373
  21.1 0.4 collective-permute-done.peer_ref
  21.4 2.1 %peer_density.1.spread_hbm = f32[16,16,128]{2,1,0:T(8,128)} custom-call(bf16[32,48,128]{2,1,0:T(8,128)(2,1)S(1)} %get-tuple-element.15.right_by_ref, f32[4,32,128]{2,1,0:T(8,128)S(1)} %get-tuple-element.16.own_by_ref, f32[22,16,128]{2,1,0:T(8,128)S(1)} %get-tuple-element.18.own_ref, f32[16,128]{1,0:T(8,128)S(1)} %near_density.1.sum_ref, ...), custom_call_target="tpu_custom_call" | custom-call | tf_op jit(solution)/shard_map/peer_density/pallas_call | solution.py:396
  23.5 3.7 %all-to-all-start.1 = ((f32[16,16,128]{2,1,0:T(8,128)}), f32[16,16,128]{2,1,0:T(8,128)S(1)}, u32[]{:S(2)}, u32[]{:S(2)}) async-start(f32[16,16,128]{2,1,0:T(8,128)} %peer_density.1.spread_hbm), calls=%async_computation.1 | async-start | bytes 262144 | tf_op jit(solution)/shard_map/all_to_all | solution.py:412
  27.3 7.1 %prepare_force.1 = (f32[16,128]{1,0:T(8,128)}, f32[3,16,128]{2,1,0:T(8,128)}, bf16[24,408,128]{2,1,0:T(8,128)(2,1)S(1)}) custom-call(s32[2,16]{1,0:T(2,128)} %bitcast.14, s32[2,24]{1,0:T(2,128)} %bitcast.16, s32[1,24]{1,0:T(1,128)} %bitcast.18, f32[16,16,128]{2,1,0:T(8,128)} %peer_density.1.spread_hbm, f32[16,8,128]{2,1,0:T(8,128)} %get-tuple-element.20.centred_hbm, ...), custom_call_target="tpu_custom_call" | custom-call | flops 39321600 | bytes 65536 | tf_op jit(solution)/shard_map/prepare_force/pallas_call | solution.py:469
  34.4 0.8 %all-to-all-done.1.terms_ref = f32[16,16,128]{2,1,0:T(8,128)S(1)} async-done(((f32[16,16,128]{2,1,0:T(8,128)}), f32[16,16,128]{2,1,0:T(8,128)S(1)}, u32[]{:S(2)}, u32[]{:S(2)}) %all-to-all-start.1) | async-done | bytes 131104 | tf_op jit(solution)/shard_map/all_to_all | solution.py:412
  35.2 2.1 %finish_force.1 = (f32[3,16,128]{2,1,0:T(8,128)}, f32[32,128]{1,0:T(8,128)S(1)}) custom-call(f32[3,16,128]{2,1,0:T(8,128)} %get-tuple-element.23.partial_hbm, f32[22,16,128]{2,1,0:T(8,128)S(1)} %get-tuple-element.18.own_ref, f32[16,16,128]{2,1,0:T(8,128)S(1)} %all-to-all-done.1.terms_ref, bf16[24,408,128]{2,1,0:T(8,128)(2,1)S(1)} %get-tuple-element.24.weight_ref), custom_call_target="tpu_custom_call" | custom-call | tf_op jit(solution)/shard_map/finish_force/pallas_call | solution.py:537
  37.3 12.1 %all_to_all.19 = f32[32,1,128]{2,1,0:T(1,128)S(1)} all-to-all(f32[32,1,128]{2,1,0:T(1,128)S(1)} %bitcast.9), channel_id=1, replica_groups=mesh['grp'=2,'chip'=8,'core'=2] {'grp','chip','core'}, dimensions={0} | all-to-all | bytes 32768 | tf_op jit(solution)/shard_map/all_to_all | solution.py:556
  49.4 0.6 %reduce_min.9 = f32[]{:T(128)} reduce(f32[32,1,128]{2,1,0:T(1,128)S(1)} %all_to_all.19, f32[]{:T(128)} %constant.0.clone.1), dimensions={0,1,2}, to_apply=%region_0.0 | reduce | flops 4095 | bytes 16392 | tf_op jit(solution)/shard_map/reduce_min | solution.py:557
Async XLA Ops:
  2.2 17.6 %all-to-all-start = ((f32[8,80,128]{2,1,0:T(8,128)}), f32[8,80,128]{2,1,0:T(8,128)S(1)}, u32[]{:S(2)}, u32[]{:S(2)}) async-start(f32[8,80,128]{2,1,0:T(8,128)} %bitcast.10), calls=%async_computation | async-start | bytes 655360 | tf_op jit(solution)/shard_map/all_to_all | solution.py:206
  19.8 1.6 %collective-permute-start = (f32[8,80,128]{2,1,0:T(8,128)S(1)}, f32[8,80,128]{2,1,0:T(8,128)S(1)}, u32[]{:S(2)}, u32[]{:S(2)}) collective-permute-start(f32[8,80,128]{2,1,0:T(8,128)S(1)} %all-to-all-done.near_ref), channel_id=1, source_target_pairs={{0,1},{1,0},{2,3},{3,2},{4,5},{5,4},{6,7},{7,6},{8,9},{9,8},{10,11... | collective-permute-start | bytes 983048 | tf_op jit(solution)/shard_map/ppermute | solution.py:329
  23.5 11.6 %all-to-all-start.1 = ((f32[16,16,128]{2,1,0:T(8,128)}), f32[16,16,128]{2,1,0:T(8,128)S(1)}, u32[]{:S(2)}, u32[]{:S(2)}) async-start(f32[16,16,128]{2,1,0:T(8,128)} %peer_density.1.spread_hbm), calls=%async_computation.1 | async-start | bytes 262144 | tf_op jit(solution)/shard_map/all_to_all | solution.py:412
